TPU v7x, 128 devices: a whole 4x4x4 slice. The times are simulated.
128 devices in a mesh: data: 1, dap: 128 (over z, y, x, core).
Axes of the slice: x: 4, y: 4, z: 4, core: 2. Of those that a mesh axis runs over, the one named last changes fastest.
Arguments:
- msa_act: bfloat16 [2048, 512, 256], P(('data', 'dap'))
- msa_mask: int32 [2048, 512], P(('data', 'dap'))
- pair_act: float32 [512, 512, 128], P(('data', 'dap'))
- opm_gain: bfloat16 [256], replicated
- opm_shift: bfloat16 [256], replicated
- proj_a: bfloat16 [256, 32], replicated
- bias_a: bfloat16 [32], replicated
- proj_b: bfloat16 [256, 32], replicated
- bias_b: bfloat16 [32], replicated
- proj_out: bfloat16 [1024, 128], replicated
- bias_out: bfloat16 [128], replicated
- row_gain: bfloat16 [256], replicated
- row_shift: bfloat16 [256], replicated
- pair_gain: bfloat16 [128], replicated
- pair_proj: bfloat16 [128, 8], replicated
- query_w: bfloat16 [256, 256], replicated
- key_w: bfloat16 [256, 256], replicated
- value_w: bfloat16 [256, 256], replicated
- gate_w: bfloat16 [256, 256], replicated
- gate_bias: bfloat16 [256], replicated
- attn_out_w: bfloat16 [256, 256], replicated
- attn_out_b: bfloat16 [256], replicated
Outputs:
- output 1: bfloat16 [2048, 512, 256], P(('data', 'dap'))
- output 2: float32 [512, 512, 128], P(('data', 'dap'))
All inputs are finite; a program needn't handle non-finite values.
Results may differ from a plain program's by a relative error of at most 0.00800763.
Values are sent between devices in bfloat16 or wider.
A program may use at most 1 GiB of HBM per device.

v0:
```python
import math
import jax
import jax.numpy as jnp
from jax import lax
from jax.sharding import PartitionSpec as P

LN_EPS = 1e-5
COUNT_EPS = 1e-3
MASK_FILL = -1e9
SEQS_PER_STEP = 4


def layer_norm(values, norm_gain):
    values = values.astype(jnp.float32)
    centered = values - jnp.mean(values, axis=-1, keepdims=True)
    variance = jnp.mean(jnp.square(centered), axis=-1, keepdims=True)
    return centered * lax.rsqrt(variance + LN_EPS) * norm_gain.astype(jnp.float32)


def project(values, weight):
    return jnp.einsum('...m,mk->...k', values, weight, preferred_element_type=jnp.float32)


def row_attention(array_b7, mask_blk, pair_bias, row_gain, row_shift, query_w, key_w, value_w, gate_w, gate_bias, attn_out_w, attn_out_b):
    num_heads = pair_bias.shape[0]
    head_dim = query_w.shape[1] // num_heads
    blk_shape = array_b7.shape[:-1] + (num_heads, head_dim)
    normed = (layer_norm(array_b7, row_gain) + row_shift.astype(jnp.float32)).astype(jnp.bfloat16)
    query_act = project(normed, query_w).astype(jnp.bfloat16).reshape(blk_shape)
    key_act = project(normed, key_w).astype(jnp.bfloat16).reshape(blk_shape)
    value_act = project(normed, value_w).astype(jnp.bfloat16).reshape(blk_shape)
    gate_act = jax.nn.sigmoid(project(normed, gate_w) + gate_bias.astype(jnp.float32)).astype(jnp.bfloat16).reshape(blk_shape)
    logits = jnp.einsum('sihd,sjhd->shij', query_act, key_act, preferred_element_type=jnp.float32) * (head_dim ** -0.5) + pair_bias[None].astype(jnp.float32)
    logits = jnp.where(mask_blk[:, None, None, :] > 0, logits, MASK_FILL)
    weights = jax.nn.softmax(logits, axis=-1).astype(jnp.bfloat16)
    attended = jnp.einsum('shij,sjhd->sihd', weights, value_act, preferred_element_type=jnp.float32)
    gated = (attended * gate_act.astype(jnp.float32)).astype(jnp.bfloat16).reshape(array_b7.shape[:-1] + (num_heads * head_dim,))
    update = project(gated, attn_out_w) + attn_out_b.astype(jnp.float32)
    return (array_b7.astype(jnp.float32) + update).astype(jnp.bfloat16)


def solution(mesh):
    group_size = mesh.shape['dap']
    seq_spec = P(('data', 'dap'))

    def per_device(value_a7, value_a8, pair_act, opm_gain, opm_shift, proj_a, bias_a, proj_b, bias_b, proj_out, bias_out, row_gain, row_shift, pair_gain, pair_proj, query_w, key_w, value_w, gate_w, gate_bias, attn_out_w, attn_out_b):
        seq_dev, res_count, local_c7 = value_a7.shape
        rows_dev, _, pair_dim = pair_act.shape
        hidden = proj_a.shape[1]
        mask_val = value_a8.astype(jnp.bfloat16)
        normed = (layer_norm(value_a7, opm_gain) + opm_shift.astype(jnp.float32)).astype(jnp.bfloat16)
        left_act = ((project(normed, proj_a) + bias_a.astype(jnp.float32)) * mask_val[:, :, None]).astype(jnp.bfloat16)
        right_act = ((project(normed, proj_b) + bias_b.astype(jnp.float32)) * mask_val[:, :, None]).astype(jnp.bfloat16)
        proj_cube = proj_out.reshape(hidden, hidden, pair_dim)
        left_proj = jnp.einsum('sic,cde->side', left_act, proj_cube, preferred_element_type=jnp.float32).astype(jnp.bfloat16)
        partial_sum = jnp.einsum('side,sjd->ije', left_proj, right_act, preferred_element_type=jnp.float32)
        received = lax.all_to_all(partial_sum.astype(jnp.bfloat16), 'dap', 0, 0, tiled=True)
        outer_sum = jnp.sum(received.reshape(group_size, rows_dev, res_count, pair_dim), axis=0, dtype=jnp.float32)
        count_part = jnp.einsum('si,sj->ij', mask_val, mask_val, preferred_element_type=jnp.float32)
        counts = lax.psum_scatter(count_part, 'dap', scatter_dimension=0, tiled=True)
        pair_new = pair_act + (outer_sum + bias_out.astype(jnp.float32)) / (COUNT_EPS + counts)[:, :, None]

        pair_normed = layer_norm(pair_act, pair_gain).astype(jnp.bfloat16)
        bias_rows = jnp.einsum('ije,eh->hij', pair_normed, pair_proj, preferred_element_type=jnp.float32).astype(jnp.bfloat16)
        pair_bias = lax.all_gather(bias_rows, 'dap', axis=1, tiled=True)
        per_step = math.gcd(seq_dev, SEQS_PER_STEP)
        step_count = seq_dev // per_step

        def attend(blk_in):
            return row_attention(blk_in[0], blk_in[1], pair_bias, row_gain, row_shift, query_w, key_w, value_w, gate_w, gate_bias, attn_out_w, attn_out_b)

        piece_d7 = lax.map(attend, (value_a7.reshape(step_count, per_step, res_count, local_c7), mask_val.reshape(step_count, per_step, res_count)))
        return piece_d7.reshape(seq_dev, res_count, local_c7), pair_new

    in_specs = (seq_spec, seq_spec, seq_spec) + (P(),) * 19
    return jax.shard_map(per_device, mesh=mesh, in_specs=in_specs, out_specs=(seq_spec, seq_spec), check_vma=False)
```

profile of v0, /device:TPU:1, one launch (start us, length us, event | category | flops | bytes accessed | tf_op | source)
XLA Modules:
  0.0 1577.2 jit_solution(12668652570599441918)
XLA Ops:
  7.3 3.5 convert_reduce_fusion.2
  14.0 3.1 fusion.62.clone.4
  17.1 27.9 %fusion.69 = bf16[16,512,32,128]{3,1,2,0:T(8,128)(2,1)} fusion(bf16[16,512,256]{2,1,0:T(8,128)(2,1)} %param.24, f32[256]{0:T(256)S(1)} %convert_element_type.142, f32[256]{0:T(256)S(1)} %convert_element_type.141, f32[16,512]{1,0:T(8,128)S(1)} %add_rsqrt_fusion.1, f32[16,512]{1,0:T(8,128)S(1)} %broadcast_multiply_fusion.1, f32[32]{0:T(128)S(1)} %convert_element_type.147, ...), kind=kOutput, calls=%fused_computation.63 | convolution fusion | flops 2295070720 | bytes 71682176 | tf_op jit(solution)/shard_map/sic,cde->side/dot_general | solution.py:55
  45.0 74.6 %fusion.33 = bf16[512,512,128]{2,1,0:T(8,128)(2,1)} fusion(bf16[16,512,32,128]{3,1,2,0:T(8,128)(2,1)} %fusion.69, bf16[16,512,32,1]{1,2,0,3:T(8,128)(2,1)S(1)} %fusion.62.clone.4), kind=kOutput, calls=%fused_computation.44 | convolution fusion | flops 34393292800 | bytes 134742016 | tf_op jit(solution)/shard_map/side,sjd->ije/dot_general | solution.py:56
  119.6 12.0 all-to-all-start
  133.0 774.2 %all-reduce.3.cloned.1.call-done = f32[512,512]{1,0:T(8,128)} async-done(((f32[512,512]{1,0:T(8,128)}), f32[512,512]{1,0:T(8,128)}) %all-reduce.3.cloned.1.call-update) | async-done | bytes 1048592
  907.9 300.5 %all-to-all-done = bf16[512,512,128]{2,1,0:T(8,128)(2,1)} async-done(((bf16[512,512,128]{2,1,0:T(8,128)(2,1)}), bf16[512,512,128]{2,1,0:T(8,128)(2,1)}, u32[]{:S(2)}, u32[]{:S(2)}) %all-to-all-start) | async-done | bytes 67108896 | tf_op jit(solution)/shard_map/all_to_all | solution.py:57
  1208.4 21.2 %convert_reduce_fusion.1 = f32[4,512,128]{2,1,0:T(8,128)S(1)} fusion(bf16[128,4,512,128]{3,2,1,0:T(8,128)(2,1)} %bitcast.32), kind=kLoop, calls=%fused_computation.40 | loop fusion | flops 66846720 | bytes 68157440 | tf_op jit(solution)/shard_map/reduce_sum | solution.py:58
  1233.8 115.5 %all-gather.2.cloned.1.call-done = bf16[8,512,512]{2,0,1:T(8,128)(2,1)} async-done(((bf16[8,4,512]{2,0,1:T(8,128)(2,1)}), bf16[8,512,512]{2,0,1:T(8,128)(2,1)}) %all-gather.2.cloned.1.call-update) | async-done | bytes 4194320 | tf_op jit(solution)/shard_map/all_gather | solution.py:65
  1349.3 7.5 copy.36
  1356.8 212.6 %while.10 = (s32[]{:T(128)}, bf16[4,4,512,256]{3,2,1,0:T(8,128)(2,1)}, bf16[4,4,512,256]{3,2,1,0:T(8,128)(2,1)}, bf16[256]{0:T(256)(128)(2,1)S(1)}, bf16[256]{0:...) while((s32[]{:T(128)}, ...), condition=%wide.region_7.8_spmd, body=%wide.region_2.7_spmd.sunk | while | flops 2500335104 | bytes 124668592 | solution.py:72
  1365.0 4.4 convert_element_type.347
  1369.4 21.0 %fusion.140 = (f32[4,8,512]{2,1,0:T(8,128)S(1)}, f32[4,8,512,512]{2,3,1,0:T(8,128)}) fusion(bf16[4,512,8,32]{1,3,2,0:T(8,128)(2,1)S(1)} %bitcast.164, bf16[4,512,8,32]{1,3,2,0:T(8,128)(2,1)S(1)} %bitcast.165, f32[8,512,512]{1,2,0:T(8,128)} %convert_element_type.347, pred[4,512]{1,0:T(4,128)(4,1)S(1)} %compare_bitcast_fusion.2), kind=kOutput, calls=%fused_computation.84.clone.1 | convolution fusion | flops 578814464 | bytes 44107776 | tf_op jit(solution)/shard_map/while/body/eval_jaxpr/sub | solution.py:35
  1395.0 12.4 fusion.141
  1418.1 4.4 convert_element_type.347
  1422.5 21.0 %fusion.140 = (f32[4,8,512]{2,1,0:T(8,128)S(1)}, f32[4,8,512,512]{2,3,1,0:T(8,128)}) fusion(bf16[4,512,8,32]{1,3,2,0:T(8,128)(2,1)S(1)} %bitcast.164, bf16[4,512,8,32]{1,3,2,0:T(8,128)(2,1)S(1)} %bitcast.165, f32[8,512,512]{1,2,0:T(8,128)} %convert_element_type.347, pred[4,512]{1,0:T(4,128)(4,1)S(1)} %compare_bitcast_fusion.2), kind=kOutput, calls=%fused_computation.84.clone.1 | convolution fusion | flops 578814464 | bytes 44107776 | tf_op jit(solution)/shard_map/while/body/eval_jaxpr/sub | solution.py:35
  1448.1 12.4 fusion.141
  1471.2 4.4 convert_element_type.347
  1475.6 21.0 %fusion.140 = (f32[4,8,512]{2,1,0:T(8,128)S(1)}, f32[4,8,512,512]{2,3,1,0:T(8,128)}) fusion(bf16[4,512,8,32]{1,3,2,0:T(8,128)(2,1)S(1)} %bitcast.164, bf16[4,512,8,32]{1,3,2,0:T(8,128)(2,1)S(1)} %bitcast.165, f32[8,512,512]{1,2,0:T(8,128)} %convert_element_type.347, pred[4,512]{1,0:T(4,128)(4,1)S(1)} %compare_bitcast_fusion.2), kind=kOutput, calls=%fused_computation.84.clone.1 | convolution fusion | flops 578814464 | bytes 44107776 | tf_op jit(solution)/shard_map/while/body/eval_jaxpr/sub | solution.py:35
  1501.2 12.4 fusion.141
  1513.6 2.7 fusion.142
  1524.3 4.4 convert_element_type.347
  1528.7 21.0 %fusion.140 = (f32[4,8,512]{2,1,0:T(8,128)S(1)}, f32[4,8,512,512]{2,3,1,0:T(8,128)}) fusion(bf16[4,512,8,32]{1,3,2,0:T(8,128)(2,1)S(1)} %bitcast.164, bf16[4,512,8,32]{1,3,2,0:T(8,128)(2,1)S(1)} %bitcast.165, f32[8,512,512]{1,2,0:T(8,128)} %convert_element_type.347, pred[4,512]{1,0:T(4,128)(4,1)S(1)} %compare_bitcast_fusion.2), kind=kOutput, calls=%fused_computation.84.clone.1 | convolution fusion | flops 578814464 | bytes 44107776 | tf_op jit(solution)/shard_map/while/body/eval_jaxpr/sub | solution.py:35
  1554.3 12.4 fusion.141
  (138 shorter events, 68.3 us)
Async XLA Ops:
  7.2 9.9 copy-start
  7.2 6.1 copy-start.11
  7.2 6.7 copy-start.15
  7.2 6.7 copy-start.16
  7.2 6.7 copy-start.17
  7.2 6.7 copy-start.18
  7.2 6.7 copy-start.14
  119.6 12.0 copy-start.6
  119.6 13.4 copy-start.19
  119.6 13.4 copy-start.20
  119.6 1088.8 %all-to-all-start = ((bf16[512,512,128]{2,1,0:T(8,128)(2,1)}), bf16[512,512,128]{2,1,0:T(8,128)(2,1)}, u32[]{:S(2)}, u32[]{:S(2)}) async-start(bf16[512,512,128]{2,1,0:T(8,128)(2,1)} %fusion.33), calls=%async_computation | async-start | bytes 134217728 | tf_op jit(solution)/shard_map/all_to_all | solution.py:57
  131.5 775.6 %all-reduce.3.cloned.1.call-start = ((), (), s32[]{:S(2)}) async-start(), calls=%async_computation.2 | async-start | bytes 2097152
  132.9 1216.4 %all-gather.2.cloned.1.call-start = ((), (), s32[]{:S(2)}) async-start(), calls=%async_computation.1 | async-start | bytes 4227072 | tf_op jit(solution)/shard_map/all_gather | solution.py:65
  1208.4 21.2 %copy-start.4 = (f32[4,512,128]{2,1,0:T(8,128)S(1)}, f32[4,512,128]{2,1,0:T(8,128)}, u32[]{:S(2)}) copy-start(f32[4,512,128]{2,1,0:T(8,128)} %param.26) | copy-start | bytes 3145732
  1229.7 3.9 copy-start.10
  1233.7 123.1 %copy-start.13 = (bf16[256,256]{1,0:T(8,128)(2,1)S(1)}, bf16[256,256]{1,0:T(8,128)(2,1)}, u32[]{:S(2)}) copy-start(bf16[256,256]{1,0:T(8,128)(2,1)} %param.44) | copy-start | bytes 393220
  1233.7 123.1 %copy-start.21 = (bf16[256]{0:T(256)(128)(2,1)S(1)}, bf16[256]{0:T(256)(128)(2,1)}, u32[]{:S(2)}) copy-start(bf16[256]{0:T(256)(128)(2,1)} %param.35) | copy-start | bytes 1540
  1233.7 123.1 %copy-start.22 = (bf16[256]{0:T(256)(128)(2,1)S(1)}, bf16[256]{0:T(256)(128)(2,1)}, u32[]{:S(2)}) copy-start(bf16[256]{0:T(256)(128)(2,1)} %param.36) | copy-start | bytes 1540
  1233.7 123.1 %copy-start.23 = (bf16[256]{0:T(256)(128)(2,1)S(1)}, bf16[256]{0:T(256)(128)(2,1)}, u32[]{:S(2)}) copy-start(bf16[256]{0:T(256)(128)(2,1)} %param.43) | copy-start | bytes 1540
  1233.7 123.1 %copy-start.24 = (bf16[256]{0:T(256)(128)(2,1)S(1)}, bf16[256]{0:T(256)(128)(2,1)}, u32[]{:S(2)}) copy-start(bf16[256]{0:T(256)(128)(2,1)} %param.45) | copy-start | bytes 1540
  1358.7 6.3 copy-start.2
  1411.7 6.4 copy-start.2
  1464.8 6.4 copy-start.2
  1517.9 6.4 copy-start.2
  (7 other events, 21.1 us)
Sparse Core Ops, SparseCore 0:
  137.7 769.4 all-reduce.2
  1233.3 115.9 all-gather.1
where the time goes:
time: 1580 us
  waiting for transfers between devices  1190 us (75%)
  matrix products  288 us (18%)
  other arithmetic  62.7 us (4%)
    unnamed x3, waiting for transfers between devices  774 us
    all_to_all x1, waiting for transfers between devices, per_device(): lax.all_to_all(partial_sum.astype(jnp.bfloat16), 'dap', 0, 0, tiled=True)  300 us
    all_gather x1, waiting for transfers between devices, per_device(): pair_bias = lax.all_gather(bias_rows, 'dap', axis=1, tiled=True)  116 us
    sub x4, matrix products, row_attention(): weights = jax.nn.softmax(logits, axis=-1).astype(jnp.bfloat16)  83.8 us
    dot_general x1, matrix products, per_device(): jnp.einsum('side,sjd->ije', left_proj, right_act, preferred_element_type=...  74.6 us
    dot_general x4, matrix products, row_attention(): jnp.einsum('shij,sjhd->sihd', weights, value_act, preferred_element_type=...  49.8 us
    dot_general x21, matrix products, project(): jnp.einsum('...m,mk->...k', values, weight, preferred_element_type=jnp.fl...  49.3 us
  transfers between devices with their start and end apart: 3, of which 3 were waited for; matrix products, arithmetic and copies ran while one was open for 0% of the time, Pallas kernels for 0%

commit v1 on v0

v1 whole, which is shorter than its diff:
```python
import functools
import math
import jax
import jax.numpy as jnp
from jax import lax
from jax.experimental import pallas as pl
from jax.experimental.pallas import tpu as pltpu
from jax.sharding import Mesh, PartitionSpec as P

LN_EPS = 1e-5
COUNT_EPS = 1e-3
MASK_FILL = -1e9
VMEM_LIMIT = 60 * 1024 * 1024
GROUP_AXES = ('z', 'y')
SPLIT_AXES = ('x', 'c')


def attn_kernel(chunk, msa_ref, mask_ref, bias_ref, gain_ref, shift_ref, w_ref, gb_ref, wo_ref, bo_ref, out_ref, q_scr, k_scr, vb_scr, g_scr, w_scr):
    n, cm = msa_ref.shape[1:]
    heads = bias_ref.shape[0]
    hd = cm // heads
    x = msa_ref[0].astype(jnp.float32)
    mu = jnp.mean(x, axis=-1, keepdims=True)
    xc = x - mu
    var = jnp.mean(xc * xc, axis=-1, keepdims=True)
    r = (xc * lax.rsqrt(var + LN_EPS) * gain_ref[...].astype(jnp.float32) + shift_ref[...].astype(jnp.float32)).astype(jnp.bfloat16)
    q_scr[...] = jnp.dot(r, w_ref[:, 0:cm], preferred_element_type=jnp.float32).astype(jnp.bfloat16)
    k_scr[...] = jnp.dot(r, w_ref[:, cm:2*cm], preferred_element_type=jnp.float32).astype(jnp.bfloat16)
    v = jnp.dot(r, w_ref[:, 2*cm:3*cm], preferred_element_type=jnp.float32).astype(jnp.bfloat16)
    g_scr[...] = jax.nn.sigmoid(jnp.dot(r, w_ref[:, 3*cm:4*cm], preferred_element_type=jnp.float32) + gb_ref[...].astype(jnp.float32)).astype(jnp.bfloat16)
    lane_head = lax.broadcasted_iota(jnp.int32, (1, cm), 1) // hd
    for h in range(heads):
        vb_scr[h*n:(h+1)*n, :] = v * (lane_head == h).astype(jnp.bfloat16)
    keep = mask_ref[0] > 0
    scale = hd ** -0.5

    def rows(ci, carry):
        r0 = pl.multiple_of(ci * chunk, chunk)
        qc = q_scr[pl.ds(r0, chunk), :]
        for h in range(heads):
            qh = qc * (lane_head == h).astype(jnp.bfloat16)
            s = lax.dot_general(qh, k_scr[...], (((1,), (1,)), ((), ())), preferred_element_type=jnp.float32)
            s = s * scale + bias_ref[h, pl.ds(r0, chunk), :]
            s = jnp.where(keep, s, MASK_FILL)
            m = jnp.max(s, axis=-1, keepdims=True)
            e = jnp.exp(s - m)
            l = jnp.sum(e, axis=-1, keepdims=True)
            w_scr[:, h*n:(h+1)*n] = (e * (1.0 / l)).astype(jnp.bfloat16)
        o = jnp.dot(w_scr[...], vb_scr[...], preferred_element_type=jnp.float32)
        o = (o * g_scr[pl.ds(r0, chunk), :].astype(jnp.float32)).astype(jnp.bfloat16)
        u = jnp.dot(o, wo_ref[...], preferred_element_type=jnp.float32) + bo_ref[...].astype(jnp.float32)
        out_ref[0, pl.ds(r0, chunk), :] = (msa_ref[0, pl.ds(r0, chunk), :].astype(jnp.float32) + u).astype(jnp.bfloat16)
        return carry
    lax.fori_loop(0, n // chunk, rows, 0)

def attention(msa, mask, bias, gain, shift, wqkvg, gb, wo, bo, chunk=512):
    s, n, cm = msa.shape
    heads = bias.shape[0]
    const = lambda shape: pl.BlockSpec(shape, lambda i: (0,)*len(shape), pipeline_mode=pl.Buffered(1))
    return pl.pallas_call(
        functools.partial(attn_kernel, chunk),
        out_shape=jax.ShapeDtypeStruct((s, n, cm), jnp.bfloat16),
        grid=(s,),
        in_specs=[pl.BlockSpec((1, n, cm), lambda i: (i, 0, 0)), pl.BlockSpec((1, 1, n), lambda i: (i, 0, 0)),
                  const((heads, n, n)), const((1, cm)), const((1, cm)), const((cm, 4*cm)), const((1, cm)), const((cm, cm)), const((1, cm))],
        out_specs=pl.BlockSpec((1, n, cm), lambda i: (i, 0, 0)),
        scratch_shapes=[pltpu.VMEM((n, cm), jnp.bfloat16), pltpu.VMEM((n, cm), jnp.bfloat16), pltpu.VMEM((heads*n, cm), jnp.bfloat16),
                        pltpu.VMEM((n, cm), jnp.bfloat16), pltpu.VMEM((chunk, heads*n), jnp.bfloat16)],
        compiler_params=pltpu.CompilerParams(vmem_limit_bytes=60*1024*1024, dimension_semantics=("arbitrary",)),
        cost_estimate=pl.CostEstimate(flops=16*1000000000, bytes_accessed=20_000_000, transcendentals=33_000_000),
        name="row_attention",
    )(msa, mask, bias, gain, shift, wqkvg, gb, wo, bo)


def ab_kernel(msa_ref, mask_ref, gain_ref, shift_ref, w_ref, bias_ref, a_ref, b_ref, scr):
    seqs, n, cm = msa_ref.shape
    ch = a_ref.shape[0]

    def one(s, carry):
        x = msa_ref[s].astype(jnp.float32)
        mu = jnp.mean(x, axis=-1, keepdims=True)
        xc = x - mu
        var = jnp.mean(xc * xc, axis=-1, keepdims=True)
        xn = (xc * lax.rsqrt(var + LN_EPS) * gain_ref[...].astype(jnp.float32) + shift_ref[...].astype(jnp.float32)).astype(jnp.bfloat16)
        y = lax.dot_general(w_ref[...], xn, (((1,), (1,)), ((), ())), preferred_element_type=jnp.float32)
        y = (y + bias_ref[...]) * mask_ref[s]
        scr[:, pl.ds(s, 1), :] = y.reshape(2 * ch, 1, n)
        return carry
    lax.fori_loop(0, seqs, one, 0)
    a_ref[...] = scr[0:ch].astype(jnp.bfloat16)
    b_ref[0:ch] = scr[ch:2 * ch].astype(jnp.bfloat16)
    b_ref[ch] = mask_ref[:, 0, :].astype(jnp.bfloat16)


def project_ab(msa, mask, gain, shift, w_t, bias_t):
    s, n, cm = msa.shape
    ch = w_t.shape[0] // 2
    return pl.pallas_call(
        ab_kernel,
        out_shape=(jax.ShapeDtypeStruct((ch, s, n), jnp.bfloat16), jax.ShapeDtypeStruct((ch + 1, s, n), jnp.bfloat16)),
        scratch_shapes=[pltpu.VMEM((2 * ch, s, n), jnp.float32)],
        compiler_params=pltpu.CompilerParams(vmem_limit_bytes=VMEM_LIMIT),
        cost_estimate=pl.CostEstimate(flops=300_000_000, bytes_accessed=6_000_000, transcendentals=8192),
        name="project_ab",
    )(msa, mask, gain, shift, w_t, bias_t)


def opm_kernel(db, ib, at_ref, pt_ref, b_ref, m_ref, sel_ref, out_ref, lhs):
    rows = out_ref.shape[0]
    ce = pt_ref.shape[0] // db
    k = at_ref.shape[1] // rows
    n = out_ref.shape[2]
    step = pl.program_id(0)

    @pl.when(step == 0)
    def _():
        m = m_ref[...].reshape(k, n)
        mi = lax.dot_general(sel_ref[...], m, (((1,), (1,)), ((), ())), preferred_element_type=jnp.float32).astype(jnp.bfloat16)
        cnt = jnp.dot(mi, m, preferred_element_type=jnp.float32)
        for i in range(rows):
            out_ref[i, 0:ce, :] = jnp.zeros((ce, n), jnp.float32)
            out_ref[i, ce:, :] = jnp.broadcast_to(cnt[i:i + 1, :], (out_ref.shape[1] - ce, n))

    bk = jnp.concatenate([b_ref[:, dd].reshape(k, n) for dd in range(db)], axis=0)

    def block(g, carry):
        for ii in range(ib):
            col = pl.multiple_of((g * ib + ii) * k, k)
            ai = at_ref[:, pl.ds(col, k)]
            for dd in range(db):
                u = jnp.dot(pt_ref[dd * ce:(dd + 1) * ce, :], ai, preferred_element_type=jnp.float32)
                lhs[ii * ce:(ii + 1) * ce, dd * k:(dd + 1) * k] = u.astype(jnp.bfloat16)
        part = jnp.dot(lhs[...], bk, preferred_element_type=jnp.float32)
        for ii in range(ib):
            out_ref[g * ib + ii, 0:ce, :] += part[ii * ce:(ii + 1) * ce]
        return carry
    lax.fori_loop(0, rows // ib, block, 0)


def outer_product(a_t, p_t, b_all, sel, rows, db=4, ib=8):
    ch, cols = a_t.shape
    src, _, s, n = b_all.shape
    ce = p_t.shape[0] // ch
    k = src * s
    return pl.pallas_call(
        functools.partial(opm_kernel, db, ib),
        out_shape=jax.ShapeDtypeStruct((rows, ce + 8, n), jnp.float32),
        grid=(ch // db,),
        in_specs=[pl.BlockSpec((ch, cols), lambda g: (0, 0)),
                  pl.BlockSpec((db * ce, ch), lambda g: (g, 0)),
                  pl.BlockSpec((src, db, s, n), lambda g: (0, g, 0, 0)),
                  pl.BlockSpec((src, 1, s, n), lambda g: (0, ch, 0, 0)),
                  pl.BlockSpec((rows, n), lambda g: (0, 0))],
        out_specs=pl.BlockSpec((rows, ce + 8, n), lambda g: (0, 0, 0)),
        scratch_shapes=[pltpu.VMEM((ib * ce, db * k), jnp.bfloat16)],
        compiler_params=pltpu.CompilerParams(vmem_limit_bytes=VMEM_LIMIT, dimension_semantics=("arbitrary",)),
        cost_estimate=pl.CostEstimate(flops=2 * rows * ce * n * k * ch, bytes_accessed=20_000_000, transcendentals=0),
        name="outer_product",
    )(a_t, p_t, b_all, b_all, sel)


def solution(mesh):
    devices = mesh.devices
    fine = Mesh(devices.reshape(devices.shape[0], 4, 4, 4, 2), ('data', 'z', 'y', 'x', 'c'))
    everyone = ('z', 'y', 'x', 'c')
    seq_spec = P(('data',) + everyone)

    def per_device(msa, msa_mask, pair_act, opm_gain, opm_shift, proj_a, bias_a, proj_b, bias_b, proj_out, bias_out, row_gain, row_shift, pair_gain, pair_proj, query_w, key_w, value_w, gate_w, gate_bias, attn_out_w, attn_out_b):
        seqs, n, cm = msa.shape
        rows_dev, _, ce = pair_act.shape
        ch = proj_a.shape[1]
        groups = fine.shape['z'] * fine.shape['y']
        rows = n // groups
        mask = msa_mask.astype(jnp.float32).reshape(seqs, 1, n)

        pair_c = pair_act - jnp.mean(pair_act, axis=-1, keepdims=True)
        pair_var = jnp.mean(jnp.square(pair_c), axis=-1, keepdims=True)
        pair_n = (pair_c * lax.rsqrt(pair_var + LN_EPS) * pair_gain.astype(jnp.float32)).astype(jnp.bfloat16)
        bias_rows = jnp.einsum('ije,eh->ihj', pair_n, pair_proj, preferred_element_type=jnp.float32).astype(jnp.bfloat16)

        w_t = jnp.concatenate([proj_a, proj_b], axis=1).T
        ab_bias = jnp.concatenate([bias_a, bias_b]).astype(jnp.float32)[:, None]
        a_loc, b_loc = project_ab(msa, mask, opm_gain[None], opm_shift[None], w_t, ab_bias)
        b_all = lax.all_gather(b_loc, GROUP_AXES, axis=0, tiled=False)
        bias_all = lax.all_gather(bias_rows, everyone, axis=0, tiled=True)
        pair_bias = bias_all.transpose(1, 0, 2).astype(jnp.float32)

        a_send = a_loc.reshape(ch, seqs, groups, rows).transpose(2, 0, 1, 3).reshape(groups, ch, seqs * rows)
        a_recv = lax.all_to_all(a_send, GROUP_AXES, 0, 0, tiled=True)
        a_t = a_recv.reshape(groups, ch, seqs, rows).transpose(1, 3, 0, 2).reshape(ch, rows * groups * seqs)
        p_t = proj_out.reshape(ch, ch, ce).transpose(1, 2, 0).reshape(ch * ce, ch)
        first = lax.axis_index(GROUP_AXES) * rows
        sel = (lax.broadcasted_iota(jnp.int32, (rows, n), 1) == lax.broadcasted_iota(jnp.int32, (rows, n), 0) + first).astype(jnp.bfloat16)
        part = outer_product(a_t, p_t, b_all, sel, rows)
        total = lax.psum_scatter(part, SPLIT_AXES, scatter_dimension=0, tiled=True)
        outer_sum = total[:, :ce].transpose(0, 2, 1)
        counts = total[:, ce]
        pair_new = pair_act + (outer_sum + bias_out.astype(jnp.float32)) / (COUNT_EPS + counts)[:, :, None]

        qkvg_w = jnp.concatenate([query_w, key_w, value_w, gate_w], axis=1)
        msa_new = attention(msa, mask, pair_bias, row_gain[None], row_shift[None], qkvg_w, gate_bias[None], attn_out_w, attn_out_b[None])
        return msa_new, pair_new

    in_specs = (seq_spec, seq_spec, seq_spec) + (P(),) * 19
    return jax.shard_map(per_device, mesh=fine, in_specs=in_specs, out_specs=(seq_spec, seq_spec), check_vma=False)
```

time: 1580 us -> 273 us (0.17)
  waiting for transfers between devices: 1190 us -> 50.5 us
  matrix products: 288 us -> 1.34 us
  Pallas kernels: 0 us -> 154 us
  other arithmetic: 62.7 us -> 14.6 us
  local copies, waits for them, and re-layouts: 9.05 us -> 28.5 us
    unnamed x3, waiting for transfers between devices: 774 us -> 0.05 us
    all_to_all x1, waiting for transfers between devices: 300 us -> 11.4 us  [per_device(): a_recv = lax.all_to_all(a_send, GROUP_AXES, 0, 0, tiled=True)]
    dot_general x29 -> x1, matrix products: 204 us -> 1.34 us  [per_device(): jnp.einsum('ije,eh->ihj', pair_n, pair_proj, preferred_element_type=jnp.f...]
    pallas_call x0 -> x3, Pallas kernels: none -> 154 us  [the longest x1 80.7 us: attention(): pl.pallas_call(functools.partial(attn_kernel, chunk), out_shape=jax.Shape...]
    sub x4 -> x0, matrix products: 83.8 us -> none  [row_attention(): weights = jax.nn.softmax(logits, axis=-1).astype(jnp.bfloat16)]
    all_gather x1 -> x2, waiting for transfers between devices: 116 us -> 39.1 us  [the longest x1 36 us: per_device(): b_all = lax.all_gather(b_loc, GROUP_AXES, axis=0, tiled=False)]
    reduce_sum x12 -> x2, other arithmetic: 42.2 us -> 0.99 us  [the longest x1 0.64 us: per_device(): pair_var = jnp.mean(jnp.square(pair_c), axis=-1, keepdims=True)]
    reshape x1 -> x7, local copies, waits for them, and re-layouts: 0.01 us -> 16 us  [the longest x3 8.65 us: per_device(): a_loc.reshape(ch, seqs, groups, rows).transpose(2, 0, 1, 3)]
  transfers between devices with their start and end apart: 3 -> 4, of which waited for: 3 -> 3; matrix products, arithmetic and copies ran while one was open for 0% -> 12% of each run, Pallas kernels for 0% -> 53%
where the time goes in v1:
time: 273 us; the launch traced here: 272 us
  Pallas kernels  154 us (56%)
  waiting for transfers between devices  50.5 us (18%)
  local copies, waits for them, and re-layouts  28.5 us (10%)
  other arithmetic  14.6 us (5%)
  between operations  14 us (5%)
  starting transfers between devices  8.95 us (3%)
    pallas_call x1, Pallas kernels, attention(): pl.pallas_call(functools.partial(attn_kernel, chunk), out_shape=jax.Shape...  80.7 us
    pallas_call x1, Pallas kernels, outer_product(): pl.pallas_call(functools.partial(opm_kernel, db, ib), out_shape=jax.Shape...  63.2 us
    all_gather x1, waiting for transfers between devices, per_device(): b_all = lax.all_gather(b_loc, GROUP_AXES, axis=0, tiled=False)  36 us
    all_to_all x1, waiting for transfers between devices, per_device(): a_recv = lax.all_to_all(a_send, GROUP_AXES, 0, 0, tiled=True)  11.4 us
    pallas_call x1, Pallas kernels, project_ab(): pl.pallas_call(ab_kernel, out_shape=(jax.ShapeDtypeStruct((ch, s, n), jnp...  10.3 us
    all_to_all x1, starting transfers between devices, per_device(): a_recv = lax.all_to_all(a_send, GROUP_AXES, 0, 0, tiled=True)  8.65 us
    reshape x3, local copies, waits for them, and re-layouts, per_device(): a_loc.reshape(ch, seqs, groups, rows).transpose(2, 0, 1, 3)  8.65 us
    convert_element_type x1, other arithmetic, per_device(): pair_bias = bias_all.transpose(1, 0, 2).astype(jnp.float32)  6.81 us
  transfers between devices with their start and end apart: 4, of which 3 were waited for; matrix products, arithmetic and copies ran while one was open for 12% of the time, Pallas kernels for 53%

profile of v1, /device:TPU:1, one launch (start us, length us, event | category | flops | bytes accessed | tf_op | source)
XLA Modules:
  0.0 272.1 jit_solution(7227417013836004919)
XLA Ops:
  7.2 0.8 convert_element_type.36
  10.2 1.2 broadcast_in_dim.28.gain_ref
  11.4 1.2 broadcast_in_dim.29.shift_ref
  12.6 1.4 maximum_bitcast_fusion.w_ref
  14.0 10.3 %project_ab.1 = (bf16[32,16,512]{2,1,0:T(8,128)(2,1)}, bf16[33,16,512]{2,1,0:T(8,128)(2,1)}) custom-call(bf16[16,512,256]{2,1,0:T(8,128)(2,1)} %msa_ref.3, f32[16,1,512]{2,1,0:T(1,128)} %reshape.75.mask_ref, bf16[1,256]{1,0:T(2,128)(2,1)} %broadcast_in_dim.28.gain_ref, bf16[1,256]{1,0:T(2,128)(2,1)} %broadcast_in_dim.29.shift_ref, ...), custom_call_target="tpu_custom_call" | custom-call | flops 300000000 | bytes 6000000 | tf_op jit(solution)/shard_map/project_ab/pallas_call | solution.py:98
  25.4 1.3 fusion
  26.8 2.7 reshape.76
  29.5 1.9 copy.59
  31.4 4.1 %reshape.77 = bf16[16,32,512]{2,1,0:T(8,128)(2,1)} reshape(bf16[16,32,16,32]{3,2,1,0:T(8,128)(2,1)} %bitcast.30) | data formatting | bytes 1048576 | tf_op jit(solution)/shard_map/reshape | solution.py:188
  35.5 8.7 %all-to-all-start = ((bf16[16,32,512]{2,1,0:T(8,128)(2,1)}), bf16[16,32,512]{2,1,0:T(8,128)(2,1)}, u32[]{:S(2)}, u32[]{:S(2)}) async-start(bf16[16,32,512]{2,1,0:T(8,128)(2,1)} %reshape.77), calls=%async_computation | async-start | bytes 1048576 | tf_op jit(solution)/shard_map/all_to_all | solution.py:189
  44.4 1.4 copy.51
  46.5 11.4 %all-to-all-done = bf16[16,32,512]{2,1,0:T(8,128)(2,1)} async-done(((bf16[16,32,512]{2,1,0:T(8,128)(2,1)}), bf16[16,32,512]{2,1,0:T(8,128)(2,1)}, u32[]{:S(2)}, u32[]{:S(2)}) %all-to-all-start) | async-done | bytes 524320 | tf_op jit(solution)/shard_map/all_to_all | solution.py:189
  57.8 2.7 reshape.78
  60.5 5.2 %copy.50 = bf16[32,32,16,16]{0,3,2,1:T(8,128)(2,1)} copy(bf16[32,32,16,16]{1,3,0,2:T(8,128)(2,1)S(1)} %bitcast.31) | data formatting | bytes 1048576 | tf_op jit(solution)/shard_map/transpose | solution.py:190
  65.7 2.6 copy.52.at_ref
  68.3 36.0 %all-gather.6.cloned.1.call-done = bf16[528,16,512]{2,1,0:T(8,128)(2,1)} async-done(((bf16[33,16,512]{2,1,0:T(8,128)(2,1)}), bf16[528,16,512]{2,1,0:T(8,128)(2,1)}) %all-gather.6.cloned.1.call-update) | async-done | bytes 8650768 | tf_op jit(solution)/shard_map/all_gather | solution.py:184
  104.3 63.2 %outer_product.1 = f32[32,136,512]{2,1,0:T(8,128)} custom-call(bf16[32,8192]{1,0:T(8,128)(2,1)} %copy.52.at_ref, bf16[4096,32]{1,0:T(8,128)(2,1)} %bitcast.33, bf16[16,33,16,512]{3,2,1,0:T(8,128)(2,1)} %bitcast.36, bf16[16,33,16,512]{3,2,1,0:T(8,128)(2,1)} %bitcast.37, bf16[32,512]{1,0:T(8,128)(2,1)} %fusion.7.sel_ref), custom_call_target="tpu_custom_call" | custom-call | flops 34359738368 | bytes 20000000 | tf_op jit(solution)/shard_map/outer_product/pallas_call | solution.py:145
  170.5 0.9 pad_maximum_fusion.w_ref
  171.4 3.0 %all-gather.4.cloned.1.call-done = bf16[512,8,512]{2,1,0:T(8,128)(2,1)} async-done(((bf16[4,8,512]{2,1,0:T(8,128)(2,1)}), bf16[512,8,512]{2,1,0:T(8,128)(2,1)}) %all-gather.4.cloned.1.call-update) | async-done | bytes 4194320 | tf_op jit(solution)/shard_map/all_gather | solution.py:185
  174.4 6.8 %convert_bitcast_fusion.bias_ref = f32[8,512,512]{2,1,0:T(8,128)} fusion(bf16[512,8,512]{2,1,0:T(8,128)(2,1)} %all-gather.4.cloned.1.call-done), kind=kLoop, calls=%fused_computation | loop fusion | flops 2097152 | bytes 12582912 | tf_op jit(solution)/shard_map/convert_element_type | solution.py:186
  181.2 80.7 %row_attention.1 = bf16[16,512,256]{2,1,0:T(8,128)(2,1)} custom-call(bf16[16,512,256]{2,1,0:T(8,128)(2,1)} %msa_ref.3, f32[16,1,512]{2,1,0:T(1,128)} %reshape.75.mask_ref, f32[8,512,512]{2,1,0:T(8,128)} %convert_bitcast_fusion.bias_ref, bf16[1,256]{1,0:T(2,128)(2,1)} %broadcast_in_dim.24.gain_ref, bf16[1,256]{1,0:T(2,128)(2,1)} %broadcast_in_dim.25.shift_ref, ...), custom_call_target="tpu_custom_call" | custom-call | flops 16000000000 | bytes 20000000 | tf_op jit(solution)/shard_map/row_attention/pallas_call | solution.py:60
  262.0 0.8 slice_add_fusion.1
  262.8 1.4 fusion.3
  264.3 1.3 copy.54
  (50 shorter events, 7.1 us)
Async XLA Ops:
  7.2 18.3 %copy-start = (bf16[128,8]{0,1:T(8,128)(2,1)S(1)}, bf16[128,8]{0,1:T(8,128)(2,1)}, u32[]{:S(2)}) copy-start(bf16[128,8]{0,1:T(8,128)(2,1)} %param.36) | copy-start | bytes 6148
  7.2 17.2 %copy-start.7 = (bf16[128]{0:T(256)(128)(2,1)S(1)}, bf16[128]{0:T(256)(128)(2,1)}, u32[]{:S(2)}) copy-start(bf16[128]{0:T(256)(128)(2,1)} %param.35) | copy-start | bytes 772
  7.2 17.2 %copy-start.1 = (f32[4,512,128]{2,1,0:T(8,128)S(1)}, f32[4,512,128]{2,1,0:T(8,128)}, u32[]{:S(2)}) copy-start(f32[4,512,128]{2,1,0:T(8,128)} %param.24) | copy-start | bytes 3145732
  7.2 97.1 %all-gather.6.cloned.1.call-start = ((), (), s32[]{:S(2)}) async-start(), calls=%async_computation.4 | async-start | bytes 9191424 | tf_op jit(solution)/shard_map/all_gather | solution.py:184
  24.3 150.1 %all-gather.4.cloned.1.call-start = ((), (), s32[]{:S(2)}) async-start(), calls=%async_computation.2 | async-start | bytes 4227072 | tf_op jit(solution)/shard_map/all_gather | solution.py:185
  29.5 14.8 %copy-start.2 = (bf16[1024,128]{1,0:T(8,128)(2,1)S(1)}, bf16[1024,128]{1,0:T(8,128)(2,1)}, u32[]{:S(2)}) copy-start(bf16[1024,128]{1,0:T(8,128)(2,1)} %param.31) | copy-start | bytes 786436
  35.5 22.4 %all-to-all-start = ((bf16[16,32,512]{2,1,0:T(8,128)(2,1)}), bf16[16,32,512]{2,1,0:T(8,128)(2,1)}, u32[]{:S(2)}, u32[]{:S(2)}) async-start(bf16[16,32,512]{2,1,0:T(8,128)(2,1)} %reshape.77), calls=%async_computation | async-start | bytes 1048576 | tf_op jit(solution)/shard_map/all_to_all | solution.py:189
  44.1 217.9 %reduce-scatter.2.cloned.1.call-start = ((), (), s32[]{:S(2)}) async-start(), calls=%async_computation.3 | async-start | bytes 10027008 | tf_op jit(solution)/shard_map/reduce_scatter | solution.py:195
  167.5 0.7 copy-start.8
  167.5 0.7 copy-start.9
  167.5 1.3 copy-start.10
  167.6 1.8 copy-start.11
  167.6 2.4 copy-start.12
  167.6 2.9 %copy-start.3 = (bf16[256,256]{1,0:T(8,128)(2,1)S(1)}, bf16[256,256]{1,0:T(8,128)(2,1)}, u32[]{:S(2)}) copy-start(bf16[256,256]{1,0:T(8,128)(2,1)} %param.40) | copy-start | bytes 393220
  167.6 2.9 %copy-start.4 = (bf16[256,256]{1,0:T(8,128)(2,1)S(1)}, bf16[256,256]{1,0:T(8,128)(2,1)}, u32[]{:S(2)}) copy-start(bf16[256,256]{1,0:T(8,128)(2,1)} %param.39) | copy-start | bytes 393220
  167.6 2.9 %copy-start.5 = (bf16[256,256]{1,0:T(8,128)(2,1)S(1)}, bf16[256,256]{1,0:T(8,128)(2,1)}, u32[]{:S(2)}) copy-start(bf16[256,256]{1,0:T(8,128)(2,1)} %param.38) | copy-start | bytes 393220
  167.6 2.9 %copy-start.6 = (bf16[256,256]{1,0:T(8,128)(2,1)S(1)}, bf16[256,256]{1,0:T(8,128)(2,1)}, u32[]{:S(2)}) copy-start(bf16[256,256]{1,0:T(8,128)(2,1)} %param.37) | copy-start | bytes 393220
Sparse Core Ops, SparseCore 0:
  24.4 79.8 all-gather.5
  107.5 66.9 all-gather.3
  176.8 51.4 reduce-scatter.1

commit v2 on v1

v2 whole, which is shorter than its diff:
```python
import functools
import math
import jax
import jax.numpy as jnp
from jax import lax
from jax.experimental import pallas as pl
from jax.experimental.pallas import tpu as pltpu
from jax.sharding import Mesh, PartitionSpec as P

LN_EPS = 1e-5
COUNT_EPS = 1e-3
MASK_FILL = -1e9
VMEM_LIMIT = 60 * 1024 * 1024
LANES = 128
SUBLANES = 8
ALL_AXES = ('z', 'y', 'x', 'c')
GROUP_AXES = ('z', 'y')
SPLIT_AXES = ('x', 'c')


def attn_kernel(chunk, msa_ref, mask_ref, bias_ref, gain_ref, shift_ref, w_ref, gb_ref, wo_ref, bo_ref, *rest):
    out_ref, q_scr, k_scr, vb_scr, g_scr, w_scr = rest[-6:]
    n, cm = msa_ref.shape[1:]
    heads = bias_ref.shape[0]
    hd = cm // heads
    x = msa_ref[0].astype(jnp.float32)
    mu = jnp.mean(x, axis=-1, keepdims=True)
    xc = x - mu
    var = jnp.mean(xc * xc, axis=-1, keepdims=True)
    r = (xc * lax.rsqrt(var + LN_EPS) * gain_ref[...].astype(jnp.float32) + shift_ref[...].astype(jnp.float32)).astype(jnp.bfloat16)
    q_scr[...] = jnp.dot(r, w_ref[:, 0:cm], preferred_element_type=jnp.float32).astype(jnp.bfloat16)
    k_scr[...] = jnp.dot(r, w_ref[:, cm:2*cm], preferred_element_type=jnp.float32).astype(jnp.bfloat16)
    v = jnp.dot(r, w_ref[:, 2*cm:3*cm], preferred_element_type=jnp.float32).astype(jnp.bfloat16)
    g_scr[...] = jax.nn.sigmoid(jnp.dot(r, w_ref[:, 3*cm:4*cm], preferred_element_type=jnp.float32) + gb_ref[...].astype(jnp.float32)).astype(jnp.bfloat16)
    lane_head = lax.broadcasted_iota(jnp.int32, (1, cm), 1) // hd
    for h in range(heads):
        vb_scr[h*n:(h+1)*n, :] = v * (lane_head == h).astype(jnp.bfloat16)
    keep = mask_ref[0] > 0
    scale = hd ** -0.5

    def rows(ci, carry):
        r0 = pl.multiple_of(ci * chunk, chunk)
        qc = q_scr[pl.ds(r0, chunk), :]
        for h in range(heads):
            qh = qc * (lane_head == h).astype(jnp.bfloat16)
            s = lax.dot_general(qh, k_scr[...], (((1,), (1,)), ((), ())), preferred_element_type=jnp.float32)
            s = s * scale + bias_ref[h, pl.ds(r0, chunk), :]
            s = jnp.where(keep, s, MASK_FILL)
            m = jnp.max(s, axis=-1, keepdims=True)
            e = jnp.exp(s - m)
            l = jnp.sum(e, axis=-1, keepdims=True)
            w_scr[:, h*n:(h+1)*n] = (e * (1.0 / l)).astype(jnp.bfloat16)
        o = jnp.dot(w_scr[...], vb_scr[...], preferred_element_type=jnp.float32)
        o = (o * g_scr[pl.ds(r0, chunk), :].astype(jnp.float32)).astype(jnp.bfloat16)
        u = jnp.dot(o, wo_ref[...], preferred_element_type=jnp.float32) + bo_ref[...].astype(jnp.float32)
        out_ref[0, pl.ds(r0, chunk), :] = (msa_ref[0, pl.ds(r0, chunk), :].astype(jnp.float32) + u).astype(jnp.bfloat16)
        return carry
    lax.fori_loop(0, n // chunk, rows, 0)

def attention(msa, mask, bias, gain, shift, wqkvg, gb, wo, bo, first, count, before=None, chunk=512):
    s, n, cm = msa.shape
    heads = bias.shape[0]
    const = lambda shape: pl.BlockSpec(shape, lambda i: (0,) * len(shape), pipeline_mode=pl.Buffered(1))
    extra = () if before is None else (before,)
    return pl.pallas_call(
        functools.partial(attn_kernel, chunk),
        out_shape=jax.ShapeDtypeStruct((s, n, cm), jnp.bfloat16),
        grid=(count,),
        in_specs=[pl.BlockSpec((1, n, cm), lambda i: (i + first, 0, 0)), pl.BlockSpec((1, 1, n), lambda i: (i + first, 0, 0)),
                  const((heads, n, n)), const((1, cm)), const((1, cm)), const((cm, 4 * cm)), const((1, cm)), const((cm, cm)), const((1, cm))]
                 + [pl.BlockSpec(memory_space=pl.ANY)] * len(extra),
        out_specs=pl.BlockSpec((1, n, cm), lambda i: (i + first, 0, 0)),
        scratch_shapes=[pltpu.VMEM((n, cm), jnp.bfloat16), pltpu.VMEM((n, cm), jnp.bfloat16), pltpu.VMEM((heads * n, cm), jnp.bfloat16),
                        pltpu.VMEM((n, cm), jnp.bfloat16), pltpu.VMEM((chunk, heads * n), jnp.bfloat16)],
        input_output_aliases={9: 0} if extra else {},
        compiler_params=pltpu.CompilerParams(vmem_limit_bytes=VMEM_LIMIT, dimension_semantics=("arbitrary",)),
        cost_estimate=pl.CostEstimate(flops=count * 1_500_000_000, bytes_accessed=20_000_000, transcendentals=count * 2_000_000),
        name="row_attention",
    )(msa, mask, bias, gain, shift, wqkvg, gb, wo, bo, *extra)


def ab_kernel(msa_ref, mask_ref, gain_ref, shift_ref, w_ref, bias_ref, a_ref, b_ref, scr_a, scr_b):
    seqs, n, cm = msa_ref.shape
    ch = scr_b.shape[0]
    quads = n // LANES
    subs = a_ref.shape[0] // quads
    width = LANES // subs
    lane = lax.broadcasted_iota(jnp.int32, (SUBLANES, LANES), 1) // width

    def one(s, carry):
        x = msa_ref[s].astype(jnp.float32)
        mu = jnp.mean(x, axis=-1, keepdims=True)
        xc = x - mu
        var = jnp.mean(xc * xc, axis=-1, keepdims=True)
        xn = (xc * lax.rsqrt(var + LN_EPS) * gain_ref[...].astype(jnp.float32) + shift_ref[...].astype(jnp.float32)).astype(jnp.bfloat16)
        y = lax.dot_general(w_ref[...], xn, (((1,), (1,)), ((), ())), preferred_element_type=jnp.float32)
        y = (y + bias_ref[...]) * mask_ref[s]
        scr_b[:, pl.ds(s, 1), :] = y[ch:2 * ch].reshape(ch, 1, n)
        for zz in range(quads):
            tiles = [y[c4 * SUBLANES:(c4 + 1) * SUBLANES, zz * LANES:(zz + 1) * LANES] for c4 in range(subs)]
            for yy in range(subs):
                out = tiles[yy]
                for c4 in range(subs):
                    if c4 != yy:
                        out = jnp.where(lane == c4, pltpu.roll(tiles[c4], ((c4 - yy) * width) % LANES, 1), out)
                scr_a[zz * subs + yy, pl.ds(pl.multiple_of(s * SUBLANES, SUBLANES), SUBLANES), :] = out
        return carry
    lax.fori_loop(0, seqs, one, 0)
    a_ref[...] = scr_a[...].astype(jnp.bfloat16)
    b_ref[0:ch] = scr_b[...].astype(jnp.bfloat16)
    b_ref[ch] = mask_ref[:, 0, :].astype(jnp.bfloat16)


def project_ab(msa, mask, gain, shift, w_t, bias_t):
    s, n, cm = msa.shape
    ch = w_t.shape[0] // 2
    return pl.pallas_call(
        ab_kernel,
        out_shape=(jax.ShapeDtypeStruct((16, s * SUBLANES, LANES), jnp.bfloat16), jax.ShapeDtypeStruct((ch + 1, s, n), jnp.bfloat16)),
        scratch_shapes=[pltpu.VMEM((16, s * SUBLANES, LANES), jnp.float32), pltpu.VMEM((ch, s, n), jnp.float32)],
        compiler_params=pltpu.CompilerParams(vmem_limit_bytes=VMEM_LIMIT),
        cost_estimate=pl.CostEstimate(flops=300_000_000, bytes_accessed=6_000_000, transcendentals=8192),
        name="project_ab",
    )(msa, mask, gain, shift, w_t, bias_t)


def opm_kernel(db, ib, half, ar_ref, pt_ref, b_ref, m_ref, sel_ref, out_ref, lhs, af, at2):
    rows = out_ref.shape[0]
    ce = pt_ref.shape[0] // db
    ch = pt_ref.shape[1]
    k = m_ref.shape[0] * m_ref.shape[2]
    n = out_ref.shape[2]
    full = at2.shape[1] // ch
    step = pl.program_id(0)

    @pl.when(step == 0)
    def _():
        m = m_ref[...].reshape(k, n)
        mi = lax.dot_general(sel_ref[...], m, (((1,), (1,)), ((), ())), preferred_element_type=jnp.float32).astype(jnp.bfloat16)
        cnt = jnp.dot(mi, m, preferred_element_type=jnp.float32)
        for i in range(rows):
            out_ref[i, 0:ce, :] = jnp.zeros((ce, n), jnp.float32)
            out_ref[i, ce:, :] = jnp.broadcast_to(cnt[i:i + 1, :], (out_ref.shape[1] - ce, n))
        af[...] = ar_ref[...].reshape(af.shape).astype(jnp.float32)
        eye = (lax.broadcasted_iota(jnp.int32, (LANES, LANES), 0) == lax.broadcasted_iota(jnp.int32, (LANES, LANES), 1)).astype(jnp.bfloat16)
        for c8 in range(SUBLANES):
            x = af[pl.ds(c8, k, stride=SUBLANES), :].astype(jnp.bfloat16)
            t = lax.dot_general(eye, x, (((1,), (1,)), ((), ())), preferred_element_type=jnp.float32)
            for c4 in range(ch // SUBLANES):
                for kk in range(k // LANES):
                    at2[kk, pl.ds(c4 * SUBLANES + c8, full, stride=ch), :] = t[c4 * full:(c4 + 1) * full, kk * LANES:(kk + 1) * LANES]

    bk = jnp.concatenate([b_ref[:, dd].reshape(k, n) for dd in range(db)], axis=0)

    def block(g, carry):
        for ii in range(ib):
            i = (g * (ib // 2) + ii // 2) * 4 + half * 2 + ii % 2
            ai = jnp.concatenate([at2[kk, pl.ds(pl.multiple_of(i * ch, ch), ch), :] for kk in range(k // LANES)], axis=1).astype(jnp.bfloat16)
            for dd in range(db):
                u = jnp.dot(pt_ref[dd * ce:(dd + 1) * ce, :], ai, preferred_element_type=jnp.float32)
                lhs[ii * ce:(ii + 1) * ce, dd * k:(dd + 1) * k] = u.astype(jnp.bfloat16)
        part = jnp.dot(lhs[...], bk, preferred_element_type=jnp.float32)
        for ii in range(ib):
            out_ref[g * ib + ii, 0:ce, :] += part[ii * ce:(ii + 1) * ce]
        return carry
    lax.fori_loop(0, rows // ib, block, 0)


def outer_product(a_recv, p_t, b_all, sel, half, db=4, ib=8):
    rows = sel.shape[0]
    ch = p_t.shape[1]
    src, _, s, n = b_all.shape
    ce = p_t.shape[0] // ch
    k = src * s
    return pl.pallas_call(
        functools.partial(opm_kernel, db, ib, half),
        out_shape=jax.ShapeDtypeStruct((rows, ce + 8, n), jnp.float32),
        grid=(ch // db,),
        in_specs=[pl.BlockSpec(a_recv.shape, lambda g: (0, 0, 0)),
                  pl.BlockSpec((db * ce, ch), lambda g: (g, 0)),
                  pl.BlockSpec((src, db, s, n), lambda g: (0, g, 0, 0)),
                  pl.BlockSpec((src, 1, s, n), lambda g: (0, ch, 0, 0)),
                  pl.BlockSpec((rows, n), lambda g: (0, 0))],
        out_specs=pl.BlockSpec((rows, ce + 8, n), lambda g: (0, 0, 0)),
        scratch_shapes=[pltpu.VMEM((ib * ce, db * k), jnp.bfloat16), pltpu.VMEM((k * SUBLANES, LANES), jnp.float32),
                        pltpu.VMEM((k // LANES, 2 * rows * ch, LANES), jnp.float32)],
        compiler_params=pltpu.CompilerParams(vmem_limit_bytes=VMEM_LIMIT, dimension_semantics=("arbitrary",)),
        cost_estimate=pl.CostEstimate(flops=2 * rows * ce * n * k * ch, bytes_accessed=20_000_000, transcendentals=0),
        name="outer_product",
    )(a_recv, p_t, b_all, b_all, sel)


def exchange_kernel(rows_ref, a_ref, bias_ref, ar_ref, own_sem, send_sem, recv_sem, a_send, a_recv):
    mesh_id = pl.DeviceIdType.MESH
    me = {name: lax.axis_index(name) for name in ALL_AXES}
    size = {'z': bias_ref.shape[1], 'y': bias_ref.shape[2], 'x': bias_ref.shape[3], 'c': bias_ref.shape[4]}

    def moved(name, k):
        return lax.rem(me[name] + k, size[name])

    plane = [(dz, dy) for dz in range(size['z']) for dy in range(size['y']) if dz or dy]
    barrier = pltpu.get_barrier_semaphore()
    peers = [{'z': moved('z', dz), 'y': moved('y', dy)} for dz, dy in plane]
    peers += [{'x': moved('x', k)} for k in range(1, size['x'])] + [{'c': moved('c', k)} for k in range(1, size['c'])]
    for peer in peers:
        pl.semaphore_signal(barrier, inc=1, device_id=peer, device_id_type=mesh_id)

    own = [pltpu.make_async_copy(rows_ref.at[part], bias_ref.at[part, me['z'], me['y'], me['x'], me['c']], own_sem.at[part]) for part in range(2)]
    for copy in own:
        copy.start()
    pl.semaphore_wait(barrier, len(peers))

    def spread(part, name, done, slot):
        where = tuple(pl.ds(0, size[ax]) if ax in done else me[ax] for ax in ALL_AXES)
        ref = bias_ref.at[(part,) + where]
        copies = []
        for k in range(1, size[name]):
            copies.append(pltpu.make_async_remote_copy(
                src_ref=ref, dst_ref=ref, send_sem=send_sem.at[slot, k - 1], recv_sem=recv_sem.at[slot, k - 1],
                device_id={name: moved(name, k)}, device_id_type=mesh_id))
        for copy in copies:
            copy.start()
        return copies

    for copy in own:
        copy.wait()
    orders = (('x', 'y', 'z'), ('z', 'x', 'y'))
    flying = [spread(part, orders[part][0], (), part) for part in range(2)]
    here = me['z'] * size['y'] + me['y']
    sends = []
    for j, (dz, dy) in enumerate(plane):
        dst = moved('z', dz) * size['y'] + moved('y', dy)
        sends.append(pltpu.make_async_remote_copy(
            src_ref=a_ref.at[dst], dst_ref=ar_ref.at[here], send_sem=a_send.at[j], recv_sem=a_recv.at[j],
            device_id={'z': moved('z', dz), 'y': moved('y', dy)}, device_id_type=mesh_id))
    for copy in sends:
        copy.start()
    ar_ref[here] = a_ref[here]
    for phase in range(1, 3):
        for part in range(2):
            for copy in flying[part]:
                copy.wait()
            flying[part] = spread(part, orders[part][phase], orders[part][:phase], phase * 2 + part)
    for part in range(2):
        for copy in flying[part]:
            copy.wait()
        flying[part] = spread(part, 'c', orders[part], 6 + part)
    for copy in flying[0] + flying[1] + sends:
        copy.wait()


def exchange(rows, a_msg, sizes):
    half = rows.shape[1:]
    hops = max(sizes) - 1
    groups = sizes[0] * sizes[1]
    return pl.pallas_call(
        exchange_kernel,
        out_shape=(jax.ShapeDtypeStruct((2,) + tuple(sizes) + half, jnp.bfloat16), jax.ShapeDtypeStruct(a_msg.shape, jnp.bfloat16)),
        in_specs=[pl.BlockSpec(memory_space=pl.ANY), pl.BlockSpec(memory_space=pltpu.VMEM)],
        out_specs=(pl.BlockSpec(memory_space=pltpu.VMEM), pl.BlockSpec(memory_space=pltpu.VMEM)),
        scratch_shapes=[pltpu.SemaphoreType.DMA((2,)), pltpu.SemaphoreType.DMA((8, hops)), pltpu.SemaphoreType.DMA((8, hops)),
                        pltpu.SemaphoreType.DMA((groups - 1,)), pltpu.SemaphoreType.DMA((groups - 1,))],
        compiler_params=pltpu.CompilerParams(collective_id=0, has_side_effects=True, vmem_limit_bytes=VMEM_LIMIT),
        cost_estimate=pl.CostEstimate(flops=10_000_000_000, bytes_accessed=10_000_000, transcendentals=0),
        name="exchange",
    )(rows, a_msg)


def solution(mesh):
    devices = mesh.devices
    fine = Mesh(devices.reshape(devices.shape[0], 4, 4, 4, 2), ('data', 'z', 'y', 'x', 'c'))
    seq_spec = P(('data',) + ALL_AXES)

    def per_device(msa, msa_mask, pair_act, opm_gain, opm_shift, proj_a, bias_a, proj_b, bias_b, proj_out, bias_out, row_gain, row_shift, pair_gain, pair_proj, query_w, key_w, value_w, gate_w, gate_bias, attn_out_w, attn_out_b):
        seqs, n, cm = msa.shape
        rows_dev, _, ce = pair_act.shape
        ch = proj_a.shape[1]
        groups = fine.shape['z'] * fine.shape['y']
        rows = n // groups
        mask = msa_mask.astype(jnp.float32).reshape(seqs, 1, n)

        w_t = jnp.concatenate([proj_a, proj_b], axis=1).T
        ab_bias = jnp.concatenate([bias_a, bias_b]).astype(jnp.float32)[:, None]
        a_msg, b_loc = project_ab(msa, mask, opm_gain[None], opm_shift[None], w_t, ab_bias)
        b_all = lax.all_gather(b_loc, GROUP_AXES, axis=0, tiled=False)

        pair_in, a_msg = lax.optimization_barrier((pair_act, a_msg))
        pair_c = pair_in - jnp.mean(pair_in, axis=-1, keepdims=True)
        pair_var = jnp.mean(jnp.square(pair_c), axis=-1, keepdims=True)
        pair_n = (pair_c * lax.rsqrt(pair_var + LN_EPS) * pair_gain.astype(jnp.float32)).astype(jnp.bfloat16)
        bias_rows = jnp.einsum('ije,eh->ihj', pair_n, pair_proj, preferred_element_type=jnp.float32).astype(jnp.bfloat16)
        heads = bias_rows.shape[1]
        bias_rows = bias_rows.reshape(rows_dev, heads, 2, n // 2).transpose(2, 0, 1, 3).reshape(2, rows_dev * heads, n // 2)
        sizes = tuple(fine.shape[ax] for ax in ALL_AXES)
        bias_all, a_recv = exchange(bias_rows, a_msg, sizes)
        pair_bias = bias_all.reshape(2, n, heads, n // 2).transpose(2, 1, 0, 3).reshape(heads, n, n).astype(jnp.float32)

        qkvg_w = jnp.concatenate([query_w, key_w, value_w, gate_w], axis=1)
        attend = functools.partial(attention, msa, mask, pair_bias, row_gain[None], row_shift[None], qkvg_w, gate_bias[None], attn_out_w, attn_out_b[None])
        early = seqs // 2
        msa_new = attend(0, early)
        a_recv, msa_new = lax.optimization_barrier((a_recv, msa_new))

        p_t = proj_out.reshape(ch, ch, ce).transpose(1, 2, 0).reshape(ch * ce, ch)
        first = lax.axis_index(GROUP_AXES) * rows
        order = lax.broadcasted_iota(jnp.int32, (rows // 2, n), 0)
        cols = lax.broadcasted_iota(jnp.int32, (rows // 2, n), 1)
        totals = []
        for half in range(2):
            mine = first + (order // 2) * 4 + half * 2 + order % 2
            part = outer_product(a_recv, p_t, b_all, (cols == mine).astype(jnp.bfloat16), half)
            totals.append(lax.psum_scatter(part, SPLIT_AXES, scatter_dimension=0, tiled=True))
        msa_new, _ = lax.optimization_barrier((msa_new, part))
        msa_new = attend(early, seqs - early, msa_new)
        total = jnp.concatenate(totals, axis=0)
        outer_sum = total[:, :ce].transpose(0, 2, 1)
        counts = total[:, ce]
        pair_new = pair_act + (outer_sum + bias_out.astype(jnp.float32)) / (COUNT_EPS + counts)[:, :, None]
        return msa_new, pair_new

    in_specs = (seq_spec, seq_spec, seq_spec) + (P(),) * 19
    return jax.shard_map(per_device, mesh=fine, in_specs=in_specs, out_specs=(seq_spec, seq_spec), check_vma=False)
```

time: 273 us -> 267 us (0.978)
  Pallas kernels: 154 us -> 212 us
  waiting for transfers between devices: 50.5 us -> 0.07 us
  other arithmetic: 14.6 us -> 4.86 us
  starting transfers between devices: 8.95 us -> 0.12 us
  local copies, waits for them, and re-layouts: 28.5 us -> 34.6 us
    pallas_call x2 -> x4, Pallas kernels: 73.5 us -> 127 us  [the longest x2 68.7 us: outer_product(): pl.pallas_call(functools.partial(opm_kernel, db, ib, half), out_shape=jax...]
    all_gather x1, waiting for transfers between devices: 36 us -> 0.01 us  [per_device(): b_all = lax.all_gather(b_loc, GROUP_AXES, axis=0, tiled=False)]
    convert_element_type x0 -> x2, local copies, waits for them, and re-layouts: none -> 21.5 us  [per_device(): bias_all.reshape(2, n, heads, n // 2).transpose(2, 1, 0, 3)]
    reshape x5 -> x1, local copies, waits for them, and re-layouts: 14 us -> 0.63 us  [per_device(): bias_rows.reshape(rows_dev, heads, 2, n // 2).transpose(2, 0, 1, 3)]
    all_to_all x1 -> x0, waiting for transfers between devices: 11.4 us -> none  [per_device(): a_recv = lax.all_to_all(a_send, GROUP_AXES, 0, 0, tiled=True)]
    all_to_all x1 -> x0, starting transfers between devices: 8.65 us -> none  [per_device(): a_recv = lax.all_to_all(a_send, GROUP_AXES, 0, 0, tiled=True)]
    convert_element_type x2 -> x1, other arithmetic: 7.49 us -> 0.7 us  [per_device(): (cols == mine).astype(jnp.bfloat16)]
    transpose x1 -> x0, local copies, waits for them, and re-layouts: 5.16 us -> none  [per_device(): a_recv.reshape(groups, ch, seqs, rows).transpose(1, 3, 0, 2)]
  transfers between devices with their start and end apart: 4 -> 3, of which waited for: 3 -> 0; matrix products, arithmetic and copies ran while one was open for 12% -> 11% of each run, Pallas kernels for 53% -> 62%
where the time goes in v2:
time: 267 us; the launch traced here: 266 us
  Pallas kernels  212 us (79%)
  local copies, waits for them, and re-layouts  34.6 us (13%)
  between operations  14 us (5%)
  other arithmetic  4.86 us (2%)
    pallas_call x2, Pallas kernels, attention(): pl.pallas_call(functools.partial(attn_kernel, chunk), out_shape=jax.Shape...  85.2 us
    pallas_call x2, Pallas kernels, outer_product(): pl.pallas_call(functools.partial(opm_kernel, db, ib, half), out_shape=jax...  68.7 us
    pallas_call x1, Pallas kernels, exchange(): pl.pallas_call(exchange_kernel, out_shape=(jax.ShapeDtypeStruct((2,) + tu...  46.5 us
    convert_element_type x2, local copies, waits for them, and re-layouts, per_device(): bias_all.reshape(2, n, heads, n // 2).transpose(2, 1, 0, 3)  21.5 us
    pallas_call x1, Pallas kernels, project_ab(): pl.pallas_call(ab_kernel, out_shape=(jax.ShapeDtypeStruct((16, s * SUBLAN...  11.7 us
  transfers between devices with their start and end apart: 3, of which 0 were waited for; matrix products, arithmetic and copies ran while one was open for 11% of the time, Pallas kernels for 62%

profile of v2, /device:TPU:1, one launch (start us, length us, event | category | flops | bytes accessed | tf_op | source)
XLA Modules:
  0.0 266.5 jit_solution(16354497266921131888)
XLA Ops:
  7.2 0.8 convert_element_type.43
  8.1 0.6 reshape.75.mask_ref
  8.7 1.2 broadcast_in_dim.24.gain_ref
  9.9 1.2 broadcast_in_dim.25.shift_ref
  11.2 0.7 maximum_convert_fusion
  11.9 0.7 copy.38.bias_ref
  12.6 1.4 maximum_bitcast_fusion.w_ref
  14.0 11.7 %project_ab.1 = (bf16[16,128,128]{2,1,0:T(8,128)(2,1)}, bf16[33,16,512]{2,1,0:T(8,128)(2,1)}) custom-call(bf16[16,512,256]{2,1,0:T(8,128)(2,1)} %msa_ref.5, f32[16,1,512]{2,1,0:T(1,128)} %reshape.75.mask_ref, bf16[1,256]{1,0:T(2,128)(2,1)} %broadcast_in_dim.24.gain_ref, bf16[1,256]{1,0:T(2,128)(2,1)} %broadcast_in_dim.25.shift_ref, ...), custom_call_target="tpu_custom_call" | custom-call | flops 300000000 | bytes 6000000 | tf_op jit(solution)/shard_map/project_ab/pallas_call | solution.py:117
  26.1 0.6 multiply_reduce_fusion
  26.8 0.7 convolution_convert_fusion
  27.5 0.6 copy.49
  28.1 46.5 %exchange.1 = (bf16[2,4,4,4,2,32,256]{6,5,4,3,2,1,0:T(8,128)(2,1)}, bf16[16,128,128]{2,1,0:T(8,128)(2,1)}) custom-call(bf16[2,32,256]{2,1,0:T(8,128)(2,1)} %bitcast.39, bf16[16,128,128]{2,1,0:T(8,128)(2,1)} %get-tuple-element.13.a_ref), custom_call_target="tpu_custom_call" | custom-call | flops 10000000000 | bytes 10000000 | tf_op jit(solution)/shard_map/exchange/pallas_call | solution.py:256
  74.7 9.8 %copy.48 = f32[2,512,8,256]{3,0,1,2:T(2,128)} copy(bf16[2,512,8,256]{3,2,1,0:T(8,128)(2,1)} %bitcast.33) | data formatting | bytes 12582912 | tf_op jit(solution)/shard_map/convert_element_type | solution.py:296
  84.5 11.7 %reshape.80.bias_ref = f32[8,512,512]{2,1,0:T(8,128)} reshape(f32[8,512,2,256]{3,2,1,0:T(2,128)} %bitcast.32) | data formatting | bytes 16777216 | tf_op jit(solution)/shard_map/convert_element_type | solution.py:296
  98.6 0.8 copy-done.7
  99.4 42.6 %row_attention.2.rest_0_ = bf16[16,512,256]{2,1,0:T(8,128)(2,1)} custom-call(bf16[16,512,256]{2,1,0:T(8,128)(2,1)} %msa_ref.5, f32[16,1,512]{2,1,0:T(1,128)} %reshape.75.mask_ref, f32[8,512,512]{2,1,0:T(8,128)} %reshape.80.bias_ref, bf16[1,256]{1,0:T(2,128)(2,1)} %broadcast_in_dim.26.gain_ref, bf16[1,256]{1,0:T(2,128)(2,1)} %broadcast_in_dim.27.shift_ref, ...), custom_call_target="tpu_custom_call" | custom-call | flops 12000000000 | bytes 20000000 | tf_op jit(solution)/shard_map/row_attention/pallas_call | solution.py:65
  142.0 1.4 copy.41
  143.5 0.7 fusion.9
  144.2 34.2 %outer_product.3 = f32[16,136,512]{2,1,0:T(8,128)} custom-call(bf16[16,128,128]{2,1,0:T(8,128)(2,1)} %get-tuple-element.17.ar_ref, bf16[4096,32]{1,0:T(8,128)(2,1)} %bitcast.34, bf16[16,33,16,512]{3,2,1,0:T(8,128)(2,1)} %bitcast.40, bf16[16,33,16,512]{3,2,1,0:T(8,128)(2,1)} %bitcast.41, bf16[16,512]{1,0:T(8,128)(2,1)} %get-tuple-element.26.sel_ref), custom_call_target="tpu_custom_call" | custom-call | flops 17179869184 | bytes 20000000 | tf_op jit(solution)/shard_map/outer_product/pallas_call | solution.py:175
  178.5 34.5 %outer_product.2 = f32[16,136,512]{2,1,0:T(8,128)} custom-call(bf16[16,128,128]{2,1,0:T(8,128)(2,1)} %get-tuple-element.17.ar_ref, bf16[4096,32]{1,0:T(8,128)(2,1)} %bitcast.35, bf16[16,33,16,512]{3,2,1,0:T(8,128)(2,1)} %bitcast.42, bf16[16,33,16,512]{3,2,1,0:T(8,128)(2,1)} %bitcast.43, bf16[16,512]{1,0:T(8,128)(2,1)} %get-tuple-element.27.sel_ref), custom_call_target="tpu_custom_call" | custom-call | flops 17179869184 | bytes 20000000 | tf_op jit(solution)/shard_map/outer_product/pallas_call | solution.py:175
  213.6 42.6 %row_attention.3 = bf16[16,512,256]{2,1,0:T(8,128)(2,1)} custom-call(bf16[16,512,256]{2,1,0:T(8,128)(2,1)} %msa_ref.5, f32[16,1,512]{2,1,0:T(1,128)} %reshape.75.mask_ref, f32[8,512,512]{2,1,0:T(8,128)} %reshape.80.bias_ref, bf16[1,256]{1,0:T(2,128)(2,1)} %broadcast_in_dim.26.gain_ref, ...), custom_call_target="tpu_custom_call", output_to_operand_aliasing={{}: (9, {})} | custom-call | flops 12000000000 | bytes 20000000 | tf_op jit(solution)/shard_map/row_attention/pallas_call | solution.py:65
  256.2 1.1 constant_dynamic-update-slice_fusion.5
  257.3 1.1 constant_dynamic-update-slice_fusion.4
  258.6 1.3 copy.43
  (56 shorter events, 3.8 us)
Async XLA Ops:
  7.2 19.6 %copy-start = (bf16[128,8]{0,1:T(8,128)(2,1)S(1)}, bf16[128,8]{0,1:T(8,128)(2,1)}, u32[]{:S(2)}) copy-start(bf16[128,8]{0,1:T(8,128)(2,1)} %param.36) | copy-start | bytes 6148
  7.2 18.6 %copy-start.1 = (f32[4,512,128]{2,1,0:T(8,128)S(1)}, f32[4,512,128]{2,1,0:T(8,128)}, u32[]{:S(2)}) copy-start(f32[4,512,128]{2,1,0:T(8,128)} %param.24) | copy-start | bytes 3145732
  7.2 18.5 %copy-start.8 = (bf16[128]{0:T(256)(128)(2,1)S(1)}, bf16[128]{0:T(256)(128)(2,1)}, u32[]{:S(2)}) copy-start(bf16[128]{0:T(256)(128)(2,1)} %param.35) | copy-start | bytes 772
  7.2 137.0 %all-gather.3.cloned.1.call-start = ((), (), s32[]{:S(2)}) async-start(), calls=%async_computation.4 | async-start | bytes 9191424 | tf_op jit(solution)/shard_map/all_gather | solution.py:285
  25.7 230.5 %reduce-scatter.3.cloned.1.call-start = ((), (), s32[]{:S(2)}) async-start(), calls=%async_computation.2 | async-start | bytes 5013504 | tf_op jit(solution)/shard_map/reduce_scatter | solution.py:312
  84.4 11.8 %copy-start.9 = (bf16[256]{0:T(256)(128)(2,1)S(1)}, bf16[256]{0:T(256)(128)(2,1)}, u32[]{:S(2)}) copy-start(bf16[256]{0:T(256)(128)(2,1)} %param.33) | copy-start | bytes 1540
  84.4 12.3 %copy-start.10 = (bf16[256]{0:T(256)(128)(2,1)S(1)}, bf16[256]{0:T(256)(128)(2,1)}, u32[]{:S(2)}) copy-start(bf16[256]{0:T(256)(128)(2,1)} %param.34) | copy-start | bytes 1540
  84.4 12.9 %copy-start.11 = (bf16[256]{0:T(256)(128)(2,1)S(1)}, bf16[256]{0:T(256)(128)(2,1)}, u32[]{:S(2)}) copy-start(bf16[256]{0:T(256)(128)(2,1)} %param.41) | copy-start | bytes 1540
  84.4 13.5 %copy-start.12 = (bf16[256]{0:T(256)(128)(2,1)S(1)}, bf16[256]{0:T(256)(128)(2,1)}, u32[]{:S(2)}) copy-start(bf16[256]{0:T(256)(128)(2,1)} %param.43) | copy-start | bytes 1540
  84.4 14.1 %copy-start.3 = (bf16[256,256]{1,0:T(8,128)(2,1)S(1)}, bf16[256,256]{1,0:T(8,128)(2,1)}, u32[]{:S(2)}) copy-start(bf16[256,256]{1,0:T(8,128)(2,1)} %param.37) | copy-start | bytes 393220
  84.5 14.1 %copy-start.4 = (bf16[256,256]{1,0:T(8,128)(2,1)S(1)}, bf16[256,256]{1,0:T(8,128)(2,1)}, u32[]{:S(2)}) copy-start(bf16[256,256]{1,0:T(8,128)(2,1)} %param.38) | copy-start | bytes 393220
  84.5 14.1 %copy-start.5 = (bf16[256,256]{1,0:T(8,128)(2,1)S(1)}, bf16[256,256]{1,0:T(8,128)(2,1)}, u32[]{:S(2)}) copy-start(bf16[256,256]{1,0:T(8,128)(2,1)} %param.39) | copy-start | bytes 393220
  84.5 14.1 %copy-start.6 = (bf16[256,256]{1,0:T(8,128)(2,1)S(1)}, bf16[256,256]{1,0:T(8,128)(2,1)}, u32[]{:S(2)}) copy-start(bf16[256,256]{1,0:T(8,128)(2,1)} %param.40) | copy-start | bytes 393220
  98.6 0.8 copy-start.7
  99.4 42.6 %copy-start.2 = (bf16[1024,128]{1,0:T(8,128)(2,1)S(1)}, bf16[1024,128]{1,0:T(8,128)(2,1)}, u32[]{:S(2)}) copy-start(bf16[1024,128]{1,0:T(8,128)(2,1)} %param.31) | copy-start | bytes 786436
  178.4 78.9 %reduce-scatter.5.cloned.1.call-start = ((), (), s32[]{:S(2)}) async-start(), calls=%async_computation.3 | async-start | bytes 5013504 | tf_op jit(solution)/shard_map/reduce_scatter | solution.py:312
  213.0 0.7 copy-start.13
Sparse Core Ops, SparseCore 0:
  25.8 86.2 all-gather.2
  178.5 33.5 reduce-scatter.2
  214.5 37.4 reduce-scatter.4

commit v3 on v2

--- a/solution.py
+++ b/solution.py
@@ -10,6 +10,7 @@
 LN_EPS = 1e-5
 COUNT_EPS = 1e-3
 MASK_FILL = -1e9
+LOG2E = math.log2(math.e)
 VMEM_LIMIT = 60 * 1024 * 1024
 LANES = 128
 SUBLANES = 8
@@ -18,83 +19,87 @@
 SPLIT_AXES = ('x', 'c')
 
 
-def attn_kernel(chunk, msa_ref, mask_ref, bias_ref, gain_ref, shift_ref, w_ref, gb_ref, wo_ref, bo_ref, *rest):
-    out_ref, q_scr, k_scr, vb_scr, g_scr, w_scr = rest[-6:]
+def attn_kernel(first, msa_ref, mask_ref, bias_ref, gain_ref, shift_ref, qw_ref, kw_ref, vw_ref, gw_ref, gb_ref, wo_ref, bo_ref, *rest):
+    out_ref, q_scr, k_scr, v_scr, g_scr, w_scr, vb_scr = rest[-7:]
     n, cm = msa_ref.shape[1:]
     heads = bias_ref.shape[0]
     hd = cm // heads
+    near, rest_scale = split_scale(hd)
     x = msa_ref[0].astype(jnp.float32)
     mu = jnp.mean(x, axis=-1, keepdims=True)
     xc = x - mu
     var = jnp.mean(xc * xc, axis=-1, keepdims=True)
     r = (xc * lax.rsqrt(var + LN_EPS) * gain_ref[...].astype(jnp.float32) + shift_ref[...].astype(jnp.float32)).astype(jnp.bfloat16)
-    q_scr[...] = jnp.dot(r, w_ref[:, 0:cm], preferred_element_type=jnp.float32).astype(jnp.bfloat16)
-    k_scr[...] = jnp.dot(r, w_ref[:, cm:2*cm], preferred_element_type=jnp.float32).astype(jnp.bfloat16)
-    v = jnp.dot(r, w_ref[:, 2*cm:3*cm], preferred_element_type=jnp.float32).astype(jnp.bfloat16)
-    g_scr[...] = jax.nn.sigmoid(jnp.dot(r, w_ref[:, 3*cm:4*cm], preferred_element_type=jnp.float32) + gb_ref[...].astype(jnp.float32)).astype(jnp.bfloat16)
+    q_scr[...] = jnp.dot(r, qw_ref[...], preferred_element_type=jnp.float32).astype(jnp.bfloat16) * jnp.bfloat16(near)
+    k_scr[...] = jnp.dot(r, kw_ref[...], preferred_element_type=jnp.float32).astype(jnp.bfloat16)
+    v = jnp.dot(r, vw_ref[...], preferred_element_type=jnp.float32).astype(jnp.bfloat16)
+    g_scr[...] = jax.nn.sigmoid(jnp.dot(r, gw_ref[...], preferred_element_type=jnp.float32) + gb_ref[...].astype(jnp.float32)).astype(jnp.bfloat16)
     lane_head = lax.broadcasted_iota(jnp.int32, (1, cm), 1) // hd
     for h in range(heads):
-        vb_scr[h*n:(h+1)*n, :] = v * (lane_head == h).astype(jnp.bfloat16)
-    keep = mask_ref[0] > 0
-    scale = hd ** -0.5
-
-    def rows(ci, carry):
-        r0 = pl.multiple_of(ci * chunk, chunk)
-        qc = q_scr[pl.ds(r0, chunk), :]
-        for h in range(heads):
-            qh = qc * (lane_head == h).astype(jnp.bfloat16)
-            s = lax.dot_general(qh, k_scr[...], (((1,), (1,)), ((), ())), preferred_element_type=jnp.float32)
-            s = s * scale + bias_ref[h, pl.ds(r0, chunk), :]
-            s = jnp.where(keep, s, MASK_FILL)
-            m = jnp.max(s, axis=-1, keepdims=True)
-            e = jnp.exp(s - m)
-            l = jnp.sum(e, axis=-1, keepdims=True)
-            w_scr[:, h*n:(h+1)*n] = (e * (1.0 / l)).astype(jnp.bfloat16)
-        o = jnp.dot(w_scr[...], vb_scr[...], preferred_element_type=jnp.float32)
-        o = (o * g_scr[pl.ds(r0, chunk), :].astype(jnp.float32)).astype(jnp.bfloat16)
-        u = jnp.dot(o, wo_ref[...], preferred_element_type=jnp.float32) + bo_ref[...].astype(jnp.float32)
-        out_ref[0, pl.ds(r0, chunk), :] = (msa_ref[0, pl.ds(r0, chunk), :].astype(jnp.float32) + u).astype(jnp.bfloat16)
-        return carry
-    lax.fori_loop(0, n // chunk, rows, 0)
-
-def attention(msa, mask, bias, gain, shift, wqkvg, gb, wo, bo, first, count, before=None, chunk=512):
+        vb_scr[h * n:(h + 1) * n, :] = v * (lane_head == h).astype(jnp.bfloat16)
+    keep = mask_ref[pl.ds(pl.program_id(0) + first, 1), :] > 0
+    q = q_scr[...]
+    for h in range(heads):
+        qh = q * (lane_head == h).astype(jnp.bfloat16)
+        s = lax.dot_general(qh, k_scr[...], (((1,), (1,)), ((), ())), preferred_element_type=jnp.float32)
+        s = jnp.where(keep, s + bias_ref[h], MASK_FILL / rest_scale)
+        m = jnp.max(s, axis=-1, keepdims=True)
+        e = jnp.exp2((s - m) * (rest_scale * LOG2E))
+        l = jnp.sum(e, axis=-1, keepdims=True)
+        w_scr[:, h * n:(h + 1) * n] = (e * (1.0 / l)).astype(jnp.bfloat16)
+    o = jnp.dot(w_scr[...], vb_scr[...], preferred_element_type=jnp.float32)
+    o = (o * g_scr[...].astype(jnp.float32)).astype(jnp.bfloat16)
+    u = jnp.dot(o, wo_ref[...], preferred_element_type=jnp.float32) + bo_ref[...].astype(jnp.float32)
+    out_ref[0] = (msa_ref[0].astype(jnp.float32) + u).astype(jnp.bfloat16)
+
+
+def split_scale(hd):
+    near = 2.0 ** math.floor(math.log2(hd ** -0.5))
+    return near, hd ** -0.5 / near
+
+
+def attention(msa, mask, bias, gain, shift, qw, kw, vw, gw, gb, wo, bo, first, count, before=None):
     s, n, cm = msa.shape
     heads = bias.shape[0]
     const = lambda shape: pl.BlockSpec(shape, lambda i: (0,) * len(shape), pipeline_mode=pl.Buffered(1))
     extra = () if before is None else (before,)
     return pl.pallas_call(
-        functools.partial(attn_kernel, chunk),
+        functools.partial(attn_kernel, first),
         out_shape=jax.ShapeDtypeStruct((s, n, cm), jnp.bfloat16),
         grid=(count,),
-        in_specs=[pl.BlockSpec((1, n, cm), lambda i: (i + first, 0, 0)), pl.BlockSpec((1, 1, n), lambda i: (i + first, 0, 0)),
-                  const((heads, n, n)), const((1, cm)), const((1, cm)), const((cm, 4 * cm)), const((1, cm)), const((cm, cm)), const((1, cm))]
+        in_specs=[pl.BlockSpec((1, n, cm), lambda i: (i + first, 0, 0)), const((s, n)),
+                  const((heads, n, n)), const((1, cm)), const((1, cm)), const((cm, cm)), const((cm, cm)), const((cm, cm)), const((cm, cm)), const((1, cm)), const((cm, cm)), const((1, cm))]
                  + [pl.BlockSpec(memory_space=pl.ANY)] * len(extra),
         out_specs=pl.BlockSpec((1, n, cm), lambda i: (i + first, 0, 0)),
-        scratch_shapes=[pltpu.VMEM((n, cm), jnp.bfloat16), pltpu.VMEM((n, cm), jnp.bfloat16), pltpu.VMEM((heads * n, cm), jnp.bfloat16),
-                        pltpu.VMEM((n, cm), jnp.bfloat16), pltpu.VMEM((chunk, heads * n), jnp.bfloat16)],
-        input_output_aliases={9: 0} if extra else {},
+        scratch_shapes=[pltpu.VMEM((n, cm), jnp.bfloat16)] * 4 + [pltpu.VMEM((n, heads * n), jnp.bfloat16), pltpu.VMEM((heads * n, cm), jnp.bfloat16)],
+        input_output_aliases={12: 0} if extra else {},
         compiler_params=pltpu.CompilerParams(vmem_limit_bytes=VMEM_LIMIT, dimension_semantics=("arbitrary",)),
         cost_estimate=pl.CostEstimate(flops=count * 1_500_000_000, bytes_accessed=20_000_000, transcendentals=count * 2_000_000),
         name="row_attention",
-    )(msa, mask, bias, gain, shift, wqkvg, gb, wo, bo, *extra)
-
-
-def ab_kernel(msa_ref, mask_ref, gain_ref, shift_ref, w_ref, bias_ref, a_ref, b_ref, scr_a, scr_b):
+    )(msa, mask, bias, gain[None], shift[None], qw, kw, vw, gw, gb[None], wo, bo[None], *extra)
+
+
+def ab_kernel(msa_ref, mask_ref, gain_ref, shift_ref, pa_ref, ba_ref, pb_ref, bb_ref, a_ref, b_ref, scr_a, scr_b):
     seqs, n, cm = msa_ref.shape
     ch = scr_b.shape[0]
     quads = n // LANES
     subs = a_ref.shape[0] // quads
     width = LANES // subs
     lane = lax.broadcasted_iota(jnp.int32, (SUBLANES, LANES), 1) // width
+    w = jnp.concatenate([pa_ref[...], pb_ref[...]], axis=1).astype(jnp.float32).T.astype(jnp.bfloat16)
+    bias = jnp.concatenate([ba_ref[...], bb_ref[...]], axis=1).astype(jnp.float32)
+    bias = jnp.broadcast_to(bias, (SUBLANES, 2 * ch)).T[:, 0:1]
+    gain = gain_ref[...].astype(jnp.float32)
+    shift = shift_ref[...].astype(jnp.float32)
 
     def one(s, carry):
         x = msa_ref[s].astype(jnp.float32)
         mu = jnp.mean(x, axis=-1, keepdims=True)
         xc = x - mu
         var = jnp.mean(xc * xc, axis=-1, keepdims=True)
-        xn = (xc * lax.rsqrt(var + LN_EPS) * gain_ref[...].astype(jnp.float32) + shift_ref[...].astype(jnp.float32)).astype(jnp.bfloat16)
-        y = lax.dot_general(w_ref[...], xn, (((1,), (1,)), ((), ())), preferred_element_type=jnp.float32)
-        y = (y + bias_ref[...]) * mask_ref[s]
+        xn = (xc * lax.rsqrt(var + LN_EPS) * gain + shift).astype(jnp.bfloat16)
+        y = lax.dot_general(w, xn, (((1,), (1,)), ((), ())), preferred_element_type=jnp.float32)
+        y = (y + bias) * mask_ref[pl.ds(s, 1), :].astype(jnp.float32)
         scr_b[:, pl.ds(s, 1), :] = y[ch:2 * ch].reshape(ch, 1, n)
         for zz in range(quads):
             tiles = [y[c4 * SUBLANES:(c4 + 1) * SUBLANES, zz * LANES:(zz + 1) * LANES] for c4 in range(subs)]
@@ -108,12 +113,12 @@
     lax.fori_loop(0, seqs, one, 0)
     a_ref[...] = scr_a[...].astype(jnp.bfloat16)
     b_ref[0:ch] = scr_b[...].astype(jnp.bfloat16)
-    b_ref[ch] = mask_ref[:, 0, :].astype(jnp.bfloat16)
-
-
-def project_ab(msa, mask, gain, shift, w_t, bias_t):
+    b_ref[ch] = mask_ref[...].astype(jnp.float32).astype(jnp.bfloat16)
+
+
+def project_ab(msa, mask, gain, shift, proj_a, bias_a, proj_b, bias_b):
     s, n, cm = msa.shape
-    ch = w_t.shape[0] // 2
+    ch = proj_a.shape[1]
     return pl.pallas_call(
         ab_kernel,
         out_shape=(jax.ShapeDtypeStruct((16, s * SUBLANES, LANES), jnp.bfloat16), jax.ShapeDtypeStruct((ch + 1, s, n), jnp.bfloat16)),
@@ -121,7 +126,7 @@
         compiler_params=pltpu.CompilerParams(vmem_limit_bytes=VMEM_LIMIT),
         cost_estimate=pl.CostEstimate(flops=300_000_000, bytes_accessed=6_000_000, transcendentals=8192),
         name="project_ab",
-    )(msa, mask, gain, shift, w_t, bias_t)
+    )(msa, mask, gain[None], shift[None], proj_a, bias_a[None], proj_b, bias_b[None])
 
 
 def opm_kernel(db, ib, half, ar_ref, pt_ref, b_ref, m_ref, sel_ref, out_ref, lhs, af, at2):
@@ -190,7 +195,7 @@
     )(a_recv, p_t, b_all, b_all, sel)
 
 
-def exchange_kernel(rows_ref, a_ref, bias_ref, ar_ref, own_sem, send_sem, recv_sem, a_send, a_recv):
+def exchange_kernel(scale, rows_ref, a_ref, out_ref, ar_ref, bias_ref, tmp, own_sem, send_sem, recv_sem, a_send, a_recv):
     mesh_id = pl.DeviceIdType.MESH
     me = {name: lax.axis_index(name) for name in ALL_AXES}
     size = {'z': bias_ref.shape[1], 'y': bias_ref.shape[2], 'x': bias_ref.shape[3], 'c': bias_ref.shape[4]}
@@ -245,20 +250,39 @@
         for copy in flying[part]:
             copy.wait()
         flying[part] = spread(part, 'c', orders[part], 6 + part)
-    for copy in flying[0] + flying[1] + sends:
+    for copy in sends:
         copy.wait()
-
-
-def exchange(rows, a_msg, sizes):
+    heads = out_ref.shape[0]
+    per = bias_ref.shape[3] * bias_ref.shape[4] * bias_ref.shape[5]
+    block = per // heads
+    wide = bias_ref.shape[6]
+    for part in range(2):
+        for copy in flying[part]:
+            copy.wait()
+
+        def place(t, carry):
+            x = bias_ref[part, t // size['y'], lax.rem(t, size['y'])].reshape(per, wide).astype(jnp.float32) * scale
+            for kk in range(wide // LANES):
+                tmp[kk] = x[:, kk * LANES:(kk + 1) * LANES]
+            for kk in range(wide // LANES):
+                for h in range(heads):
+                    out_ref[h, pl.ds(pl.multiple_of(t * block, block), block), part * wide + kk * LANES:part * wide + (kk + 1) * LANES] = tmp[kk, pl.ds(h, block, stride=heads), :]
+            return carry
+        lax.fori_loop(0, size['z'] * size['y'], place, 0)
+
+
+def exchange(rows, a_msg, sizes, heads, scale):
     half = rows.shape[1:]
+    n = 2 * half[1]
     hops = max(sizes) - 1
     groups = sizes[0] * sizes[1]
     return pl.pallas_call(
-        exchange_kernel,
-        out_shape=(jax.ShapeDtypeStruct((2,) + tuple(sizes) + half, jnp.bfloat16), jax.ShapeDtypeStruct(a_msg.shape, jnp.bfloat16)),
+        functools.partial(exchange_kernel, scale),
+        out_shape=(jax.ShapeDtypeStruct((heads, n, n), jnp.float32), jax.ShapeDtypeStruct(a_msg.shape, jnp.bfloat16)),
         in_specs=[pl.BlockSpec(memory_space=pl.ANY), pl.BlockSpec(memory_space=pltpu.VMEM)],
         out_specs=(pl.BlockSpec(memory_space=pltpu.VMEM), pl.BlockSpec(memory_space=pltpu.VMEM)),
-        scratch_shapes=[pltpu.SemaphoreType.DMA((2,)), pltpu.SemaphoreType.DMA((8, hops)), pltpu.SemaphoreType.DMA((8, hops)),
+        scratch_shapes=[pltpu.VMEM((2,) + tuple(sizes) + half, jnp.bfloat16), pltpu.VMEM((half[1] // LANES, n // groups * heads, LANES), jnp.float32),
+                        pltpu.SemaphoreType.DMA((2,)), pltpu.SemaphoreType.DMA((8, hops)), pltpu.SemaphoreType.DMA((8, hops)),
                         pltpu.SemaphoreType.DMA((groups - 1,)), pltpu.SemaphoreType.DMA((groups - 1,))],
         compiler_params=pltpu.CompilerParams(collective_id=0, has_side_effects=True, vmem_limit_bytes=VMEM_LIMIT),
         cost_estimate=pl.CostEstimate(flops=10_000_000_000, bytes_accessed=10_000_000, transcendentals=0),
@@ -277,11 +301,8 @@
         ch = proj_a.shape[1]
         groups = fine.shape['z'] * fine.shape['y']
         rows = n // groups
-        mask = msa_mask.astype(jnp.float32).reshape(seqs, 1, n)
-
-        w_t = jnp.concatenate([proj_a, proj_b], axis=1).T
-        ab_bias = jnp.concatenate([bias_a, bias_b]).astype(jnp.float32)[:, None]
-        a_msg, b_loc = project_ab(msa, mask, opm_gain[None], opm_shift[None], w_t, ab_bias)
+
+        a_msg, b_loc = project_ab(msa, msa_mask, opm_gain, opm_shift, proj_a, bias_a, proj_b, bias_b)
         b_all = lax.all_gather(b_loc, GROUP_AXES, axis=0, tiled=False)
 
         pair_in, a_msg = lax.optimization_barrier((pair_act, a_msg))
@@ -292,11 +313,10 @@
         heads = bias_rows.shape[1]
         bias_rows = bias_rows.reshape(rows_dev, heads, 2, n // 2).transpose(2, 0, 1, 3).reshape(2, rows_dev * heads, n // 2)
         sizes = tuple(fine.shape[ax] for ax in ALL_AXES)
-        bias_all, a_recv = exchange(bias_rows, a_msg, sizes)
-        pair_bias = bias_all.reshape(2, n, heads, n // 2).transpose(2, 1, 0, 3).reshape(heads, n, n).astype(jnp.float32)
-
-        qkvg_w = jnp.concatenate([query_w, key_w, value_w, gate_w], axis=1)
-        attend = functools.partial(attention, msa, mask, pair_bias, row_gain[None], row_shift[None], qkvg_w, gate_bias[None], attn_out_w, attn_out_b[None])
+        near, rest_scale = split_scale(cm // heads)
+        pair_bias, a_recv = exchange(bias_rows, a_msg, sizes, heads, 1.0 / rest_scale)
+
+        attend = functools.partial(attention, msa, msa_mask, pair_bias, row_gain, row_shift, query_w, key_w, value_w, gate_w, gate_bias, attn_out_w, attn_out_b)
         early = seqs // 2
         msa_new = attend(0, early)
         a_recv, msa_new = lax.optimization_barrier((a_recv, msa_new))

time: 267 us -> 242 us (0.906)
  local copies, waits for them, and re-layouts: 34.6 us -> 13.8 us
  other arithmetic: 4.86 us -> 1.93 us
    convert_element_type x3 -> x0, local copies, waits for them, and re-layouts: 22.2 us -> none  [the longest x2 21.5 us: per_device(): bias_all.reshape(2, n, heads, n // 2).transpose(2, 1, 0, 3)]
    unnamed x35 -> x24, local copies, waits for them, and re-layouts: 3.92 us -> 5.99 us
  transfers between devices with their start and end apart: 3 -> 3, of which waited for: 0 -> 0; matrix products, arithmetic and copies ran while one was open for 11% -> 3% of each run, Pallas kernels for 62% -> 68%
where the time goes in v3:
time: 242 us; the launch traced here: 241 us
  Pallas kernels  211 us (87%)
  between operations  13.9 us (6%)
  local copies, waits for them, and re-layouts  13.8 us (6%)
    pallas_call x2, Pallas kernels, attention(): pl.pallas_call(functools.partial(attn_kernel, first), out_shape=jax.Shape...  81.3 us
    pallas_call x2, Pallas kernels, outer_product(): pl.pallas_call(functools.partial(opm_kernel, db, ib, half), out_shape=jax...  68.5 us
    pallas_call x1, Pallas kernels, exchange(): pl.pallas_call(functools.partial(exchange_kernel, scale), out_shape=(jax....  49 us
    pallas_call x1, Pallas kernels, project_ab(): pl.pallas_call(ab_kernel, out_shape=(jax.ShapeDtypeStruct((16, s * SUBLAN...  11.9 us
    unnamed x24, local copies, waits for them, and re-layouts  5.99 us
  transfers between devices with their start and end apart: 3, of which 0 were waited for; matrix products, arithmetic and copies ran while one was open for 3% of the time, Pallas kernels for 68%

profile of v3, /device:TPU:1, one launch (start us, length us, event | category | flops | bytes accessed | tf_op | source)
XLA Modules:
  0.0 241.5 jit_solution(16925604662530196098)
XLA Ops:
  7.2 1.2 broadcast_in_dim.16.gain_ref
  8.5 1.2 broadcast_in_dim.34.shift_ref
  9.7 1.4 copy.31.pa_ref
  11.1 1.5 copy.32.pb_ref
  12.6 11.9 %project_ab.1 = (bf16[16,128,128]{2,1,0:T(8,128)(2,1)}, bf16[33,16,512]{2,1,0:T(8,128)(2,1)}) custom-call(bf16[16,512,256]{2,1,0:T(8,128)(2,1)} %msa_ref.5, s32[16,512]{1,0:T(8,128)} %mask_ref.5, bf16[1,256]{1,0:T(2,128)(2,1)} %broadcast_in_dim.16.gain_ref, bf16[1,256]{1,0:T(2,128)(2,1)} %broadcast_in_dim.34.shift_ref, bf16[256,32]{1,0:T(8,128)(2,1)} %copy.31.pa_ref, ...), custom_call_target="tpu_custom_call" | custom-call | flops 300000000 | bytes 6000000 | tf_op jit(solution)/shard_map/project_ab/pallas_call | solution.py:122
  24.6 0.3 reduce_sum.18
  25.0 0.6 multiply_reduce_fusion
  25.7 0.7 convolution_convert_fusion
  26.4 0.6 copy.40
  27.0 0.5 broadcast_in_dim.37.gain_ref
  27.6 0.6 broadcast_in_dim.38.shift_ref
  28.1 0.6 broadcast_in_dim.39.gb_ref
  28.7 0.6 broadcast_in_dim.40.bo_ref
  29.3 49.0 %exchange.1 = (f32[8,512,512]{2,1,0:T(8,128)}, bf16[16,128,128]{2,1,0:T(8,128)(2,1)}) custom-call(bf16[2,32,256]{2,1,0:T(8,128)(2,1)} %bitcast.30, bf16[16,128,128]{2,1,0:T(8,128)(2,1)} %get-tuple-element.13.a_ref), custom_call_target="tpu_custom_call" | custom-call | flops 10000000000 | bytes 10000000 | tf_op jit(solution)/shard_map/exchange/pallas_call | solution.py:279
  78.4 40.7 %row_attention.2.rest_0_ = bf16[16,512,256]{2,1,0:T(8,128)(2,1)} custom-call(bf16[16,512,256]{2,1,0:T(8,128)(2,1)} %msa_ref.5, s32[16,512]{1,0:T(8,128)} %mask_ref.5, f32[8,512,512]{2,1,0:T(8,128)} %get-tuple-element.14.bias_ref, bf16[1,256]{1,0:T(2,128)(2,1)} %broadcast_in_dim.37.gain_ref, bf16[1,256]{1,0:T(2,128)(2,1)} %broadcast_in_dim.38.shift_ref, ...), custom_call_target="tpu_custom_call" | custom-call | flops 12000000000 | bytes 20000000 | tf_op jit(solution)/shard_map/row_attention/pallas_call | solution.py:66
  119.0 1.4 copy.34
  120.4 0.7 fusion.9
  121.1 34.2 %outer_product.3 = f32[16,136,512]{2,1,0:T(8,128)} custom-call(bf16[16,128,128]{2,1,0:T(8,128)(2,1)} %get-tuple-element.17.ar_ref, bf16[4096,32]{1,0:T(8,128)(2,1)} %bitcast.25, bf16[16,33,16,512]{3,2,1,0:T(8,128)(2,1)} %bitcast.33, bf16[16,33,16,512]{3,2,1,0:T(8,128)(2,1)} %bitcast.34, bf16[16,512]{1,0:T(8,128)(2,1)} %get-tuple-element.24.sel_ref), custom_call_target="tpu_custom_call" | custom-call | flops 17179869184 | bytes 20000000 | tf_op jit(solution)/shard_map/outer_product/pallas_call | solution.py:180
  155.6 34.3 %outer_product.2 = f32[16,136,512]{2,1,0:T(8,128)} custom-call(bf16[16,128,128]{2,1,0:T(8,128)(2,1)} %get-tuple-element.17.ar_ref, bf16[4096,32]{1,0:T(8,128)(2,1)} %bitcast.26, bf16[16,33,16,512]{3,2,1,0:T(8,128)(2,1)} %bitcast.35, bf16[16,33,16,512]{3,2,1,0:T(8,128)(2,1)} %bitcast.36, bf16[16,512]{1,0:T(8,128)(2,1)} %get-tuple-element.25.sel_ref), custom_call_target="tpu_custom_call" | custom-call | flops 17179869184 | bytes 20000000 | tf_op jit(solution)/shard_map/outer_product/pallas_call | solution.py:180
  189.9 0.3 copy.35
  190.6 40.6 %row_attention.3 = bf16[16,512,256]{2,1,0:T(8,128)(2,1)} custom-call(bf16[16,512,256]{2,1,0:T(8,128)(2,1)} %msa_ref.5, s32[16,512]{1,0:T(8,128)} %mask_ref.5, f32[8,512,512]{2,1,0:T(8,128)} %get-tuple-element.14.bias_ref, bf16[1,256]{1,0:T(2,128)(2,1)} %broadcast_in_dim.37.gain_ref, ...), custom_call_target="tpu_custom_call", output_to_operand_aliasing={{}: (12, {})} | custom-call | flops 12000000000 | bytes 20000000 | tf_op jit(solution)/shard_map/row_attention/pallas_call | solution.py:66
  231.2 1.1 constant_dynamic-update-slice_fusion.1
  232.3 1.1 constant_dynamic-update-slice_fusion
  233.6 1.3 copy.36
  (37 shorter events, 1.0 us)
Async XLA Ops:
  7.2 18.5 %copy-start = (bf16[128,8]{0,1:T(8,128)(2,1)S(1)}, bf16[128,8]{0,1:T(8,128)(2,1)}, u32[]{:S(2)}) copy-start(bf16[128,8]{0,1:T(8,128)(2,1)} %param.36) | copy-start | bytes 6148
  7.2 114.0 %all-gather.3.cloned.1.call-start = ((), (), s32[]{:S(2)}) async-start(), calls=%async_computation.4 | async-start | bytes 9191424 | tf_op jit(solution)/shard_map/all_gather | solution.py:306
  12.6 12.0 %copy-start.3 = (bf16[128]{0:T(256)(128)(2,1)S(1)}, bf16[128]{0:T(256)(128)(2,1)}, u32[]{:S(2)}) copy-start(bf16[128]{0:T(256)(128)(2,1)} %param.35) | copy-start | bytes 772
  12.6 12.0 %copy-start.1 = (f32[4,512,128]{2,1,0:T(8,128)S(1)}, f32[4,512,128]{2,1,0:T(8,128)}, u32[]{:S(2)}) copy-start(f32[4,512,128]{2,1,0:T(8,128)} %param.24) | copy-start | bytes 3145732
  24.5 206.7 %reduce-scatter.3.cloned.1.call-start = ((), (), s32[]{:S(2)}) async-start(), calls=%async_computation.2 | async-start | bytes 5013504 | tf_op jit(solution)/shard_map/reduce_scatter | solution.py:332
  25.0 2.1 copy-start.4
  25.0 2.6 %copy-start.5 = (bf16[256]{0:T(256)(128)(2,1)S(1)}, bf16[256]{0:T(256)(128)(2,1)}, u32[]{:S(2)}) copy-start(bf16[256]{0:T(256)(128)(2,1)} %param.34) | copy-start | bytes 1540
  25.0 3.1 %copy-start.6 = (bf16[256]{0:T(256)(128)(2,1)S(1)}, bf16[256]{0:T(256)(128)(2,1)}, u32[]{:S(2)}) copy-start(bf16[256]{0:T(256)(128)(2,1)} %param.41) | copy-start | bytes 1540
  25.0 3.7 %copy-start.7 = (bf16[256]{0:T(256)(128)(2,1)S(1)}, bf16[256]{0:T(256)(128)(2,1)}, u32[]{:S(2)}) copy-start(bf16[256]{0:T(256)(128)(2,1)} %param.43) | copy-start | bytes 1540
  78.3 40.7 %copy-start.2 = (bf16[1024,128]{1,0:T(8,128)(2,1)S(1)}, bf16[1024,128]{1,0:T(8,128)(2,1)}, u32[]{:S(2)}) copy-start(bf16[1024,128]{1,0:T(8,128)(2,1)} %param.31) | copy-start | bytes 786436
  155.4 76.9 %reduce-scatter.5.cloned.1.call-start = ((), (), s32[]{:S(2)}) async-start(), calls=%async_computation.3 | async-start | bytes 5013504 | tf_op jit(solution)/shard_map/reduce_scatter | solution.py:332
  189.9 0.7 copy-start.8
Sparse Core Ops, SparseCore 0:
  24.6 86.2 all-gather.2
  155.5 32.8 reduce-scatter.2
  190.8 37.4 reduce-scatter.4

commit v4 on v3

--- a/solution.py
+++ b/solution.py
@@ -129,73 +129,91 @@
     )(msa, mask, gain[None], shift[None], proj_a, bias_a[None], proj_b, bias_b[None])
 
 
-def opm_kernel(db, ib, half, ar_ref, pt_ref, b_ref, m_ref, sel_ref, out_ref, lhs, af, at2):
-    rows = out_ref.shape[0]
-    ce = pt_ref.shape[0] // db
-    ch = pt_ref.shape[1]
+def opm_kernel(db, ib, u_ref, b_ref, m_ref, sel_ref, out_ref):
+    rows, wide, n = out_ref.shape
+    ce = u_ref.shape[0] // rows
     k = m_ref.shape[0] * m_ref.shape[2]
-    n = out_ref.shape[2]
-    full = at2.shape[1] // ch
-    step = pl.program_id(0)
-
-    @pl.when(step == 0)
+
+    @pl.when(pl.program_id(0) == 0)
     def _():
         m = m_ref[...].reshape(k, n)
         mi = lax.dot_general(sel_ref[...], m, (((1,), (1,)), ((), ())), preferred_element_type=jnp.float32).astype(jnp.bfloat16)
         cnt = jnp.dot(mi, m, preferred_element_type=jnp.float32)
         for i in range(rows):
             out_ref[i, 0:ce, :] = jnp.zeros((ce, n), jnp.float32)
-            out_ref[i, ce:, :] = jnp.broadcast_to(cnt[i:i + 1, :], (out_ref.shape[1] - ce, n))
-        af[...] = ar_ref[...].reshape(af.shape).astype(jnp.float32)
-        eye = (lax.broadcasted_iota(jnp.int32, (LANES, LANES), 0) == lax.broadcasted_iota(jnp.int32, (LANES, LANES), 1)).astype(jnp.bfloat16)
-        for c8 in range(SUBLANES):
-            x = af[pl.ds(c8, k, stride=SUBLANES), :].astype(jnp.bfloat16)
-            t = lax.dot_general(eye, x, (((1,), (1,)), ((), ())), preferred_element_type=jnp.float32)
-            for c4 in range(ch // SUBLANES):
-                for kk in range(k // LANES):
-                    at2[kk, pl.ds(c4 * SUBLANES + c8, full, stride=ch), :] = t[c4 * full:(c4 + 1) * full, kk * LANES:(kk + 1) * LANES]
+            out_ref[i, ce:, :] = jnp.broadcast_to(cnt[i:i + 1, :], (wide - ce, n))
 
     bk = jnp.concatenate([b_ref[:, dd].reshape(k, n) for dd in range(db)], axis=0)
 
     def block(g, carry):
-        for ii in range(ib):
-            i = (g * (ib // 2) + ii // 2) * 4 + half * 2 + ii % 2
-            ai = jnp.concatenate([at2[kk, pl.ds(pl.multiple_of(i * ch, ch), ch), :] for kk in range(k // LANES)], axis=1).astype(jnp.bfloat16)
-            for dd in range(db):
-                u = jnp.dot(pt_ref[dd * ce:(dd + 1) * ce, :], ai, preferred_element_type=jnp.float32)
-                lhs[ii * ce:(ii + 1) * ce, dd * k:(dd + 1) * k] = u.astype(jnp.bfloat16)
-        part = jnp.dot(lhs[...], bk, preferred_element_type=jnp.float32)
+        size = ib * ce
+        part = jnp.dot(u_ref[pl.ds(pl.multiple_of(g * size, size), size), :], bk, preferred_element_type=jnp.float32)
         for ii in range(ib):
             out_ref[g * ib + ii, 0:ce, :] += part[ii * ce:(ii + 1) * ce]
         return carry
     lax.fori_loop(0, rows // ib, block, 0)
 
 
-def outer_product(a_recv, p_t, b_all, sel, half, db=4, ib=8):
-    rows = sel.shape[0]
-    ch = p_t.shape[1]
-    src, _, s, n = b_all.shape
-    ce = p_t.shape[0] // ch
+def outer_product(u, b_all, sel, half, db=4, ib=8):
+    rows, n = sel.shape
+    src, ch, s, _ = b_all.shape
+    ch -= 1
+    ce = u.shape[0] // (2 * rows)
     k = src * s
     return pl.pallas_call(
-        functools.partial(opm_kernel, db, ib, half),
-        out_shape=jax.ShapeDtypeStruct((rows, ce + 8, n), jnp.float32),
+        functools.partial(opm_kernel, db, ib),
+        out_shape=jax.ShapeDtypeStruct((rows, ce + SUBLANES, n), jnp.float32),
         grid=(ch // db,),
-        in_specs=[pl.BlockSpec(a_recv.shape, lambda g: (0, 0, 0)),
-                  pl.BlockSpec((db * ce, ch), lambda g: (g, 0)),
+        in_specs=[pl.BlockSpec((rows * ce, db * k), lambda g: (half, g)),
                   pl.BlockSpec((src, db, s, n), lambda g: (0, g, 0, 0)),
                   pl.BlockSpec((src, 1, s, n), lambda g: (0, ch, 0, 0)),
                   pl.BlockSpec((rows, n), lambda g: (0, 0))],
-        out_specs=pl.BlockSpec((rows, ce + 8, n), lambda g: (0, 0, 0)),
-        scratch_shapes=[pltpu.VMEM((ib * ce, db * k), jnp.bfloat16), pltpu.VMEM((k * SUBLANES, LANES), jnp.float32),
-                        pltpu.VMEM((k // LANES, 2 * rows * ch, LANES), jnp.float32)],
+        out_specs=pl.BlockSpec((rows, ce + SUBLANES, n), lambda g: (0, 0, 0)),
         compiler_params=pltpu.CompilerParams(vmem_limit_bytes=VMEM_LIMIT, dimension_semantics=("arbitrary",)),
-        cost_estimate=pl.CostEstimate(flops=2 * rows * ce * n * k * ch, bytes_accessed=20_000_000, transcendentals=0),
+        cost_estimate=pl.CostEstimate(flops=2 * rows * ce * n * k * ch, bytes_accessed=50_000_000, transcendentals=0),
         name="outer_product",
-    )(a_recv, p_t, b_all, b_all, sel)
-
-
-def exchange_kernel(scale, rows_ref, a_ref, out_ref, ar_ref, bias_ref, tmp, own_sem, send_sem, recv_sem, a_send, a_recv):
+    )(u, b_all, b_all, sel)
+
+
+def turn_a(ar_ref, at_ref, af, at2):
+    k = af.shape[0] // SUBLANES
+    rows, ch = 2 * at_ref.shape[0], at_ref.shape[1]
+    af[...] = ar_ref[...].reshape(af.shape).astype(jnp.float32)
+    eye = (lax.broadcasted_iota(jnp.int32, (LANES, LANES), 0) == lax.broadcasted_iota(jnp.int32, (LANES, LANES), 1)).astype(jnp.bfloat16)
+    for c8 in range(SUBLANES):
+        x = af[pl.ds(c8, k, stride=SUBLANES), :].astype(jnp.bfloat16)
+        t = lax.dot_general(eye, x, (((1,), (1,)), ((), ())), preferred_element_type=jnp.float32)
+        for c4 in range(ch // SUBLANES):
+            for kk in range(k // LANES):
+                at2[kk, pl.ds(c4 * SUBLANES + c8, rows, stride=ch), :] = t[c4 * rows:(c4 + 1) * rows, kk * LANES:(kk + 1) * LANES]
+    for par in range(2):
+        for kk in range(k // LANES):
+            both = at2[kk].reshape(rows // 2, 2 * ch, LANES)[:, par * ch:(par + 1) * ch]
+            at_ref[:, :, par * k + kk * LANES:par * k + (kk + 1) * LANES] = both.astype(jnp.bfloat16)
+
+
+def u_rows(t, at_ref, pt_ref, slab, u_ref, sem, ce, per):
+    pairs, ch, k = at_ref.shape
+    k //= 2
+    slot = lax.rem(t, 2)
+    row = slot * pairs + (t // 2) * 2
+    copy = pltpu.make_async_copy(slab.at[slot], u_ref.at[pl.ds(pl.multiple_of(row * ce, 2 * ce), 2 * ce), :], sem.at[slot])
+
+    @pl.when(t >= 2)
+    def _():
+        copy.wait()
+
+    def some(p, carry):
+        u = jnp.dot(pt_ref[pl.ds(pl.multiple_of(p * per * ce, per * ce), per * ce), :], at_ref[t], preferred_element_type=jnp.float32).astype(jnp.bfloat16)
+        for dd in range(per):
+            for par in range(2):
+                slab[slot, par * ce:(par + 1) * ce, pl.ds(pl.multiple_of((p * per + dd) * k, k), k)] = u[dd * ce:(dd + 1) * ce, par * k:(par + 1) * k]
+        return carry
+    lax.fori_loop(0, ch // per, some, 0)
+    copy.start()
+
+
+def exchange_kernel(scale, rows_ref, a_ref, pt_ref, out_ref, u_ref, ar_ref, bias_ref, tmp, at_ref, af, at2, slab, slab_sem, own_sem, send_sem, recv_sem, a_send, a_recv):
     mesh_id = pl.DeviceIdType.MESH
     me = {name: lax.axis_index(name) for name in ALL_AXES}
     size = {'z': bias_ref.shape[1], 'y': bias_ref.shape[2], 'x': bias_ref.shape[3], 'c': bias_ref.shape[4]}
@@ -241,17 +259,34 @@
     for copy in sends:
         copy.start()
     ar_ref[here] = a_ref[here]
-    for phase in range(1, 3):
+
+    def advance(phase):
         for part in range(2):
             for copy in flying[part]:
                 copy.wait()
-            flying[part] = spread(part, orders[part][phase], orders[part][:phase], phase * 2 + part)
-    for part in range(2):
-        for copy in flying[part]:
-            copy.wait()
-        flying[part] = spread(part, 'c', orders[part], 6 + part)
+            if phase < 3:
+                flying[part] = spread(part, orders[part][phase], orders[part][:phase], phase * 2 + part)
+            else:
+                flying[part] = spread(part, 'c', orders[part], 6 + part)
+
+    pairs = at_ref.shape[0]
+    ce = slab.shape[1] // 2
+
+    def run(lo, hi):
+        def body(t, carry):
+            u_rows(t, at_ref, pt_ref, slab, u_ref, slab_sem, ce, 16)
+            return carry
+        lax.fori_loop(lo, hi, body, 0)
+
+    advance(1)
     for copy in sends:
         copy.wait()
+    turn_a(ar_ref, at_ref, af, at2)
+    run(0, pairs // 4)
+    advance(2)
+    run(pairs // 4, 3 * pairs // 4)
+    advance(3)
+    run(3 * pairs // 4, pairs)
     heads = out_ref.shape[0]
     per = bias_ref.shape[3] * bias_ref.shape[4] * bias_ref.shape[5]
     block = per // heads
@@ -269,25 +304,33 @@
                     out_ref[h, pl.ds(pl.multiple_of(t * block, block), block), part * wide + kk * LANES:part * wide + (kk + 1) * LANES] = tmp[kk, pl.ds(h, block, stride=heads), :]
             return carry
         lax.fori_loop(0, size['z'] * size['y'], place, 0)
-
-
-def exchange(rows, a_msg, sizes, heads, scale):
+    for s in range(2):
+        pltpu.make_async_copy(slab.at[s], u_ref.at[pl.ds(0, 2 * ce), :], slab_sem.at[s]).wait()
+
+
+def exchange(rows, a_msg, p_t, sizes, heads, scale):
     half = rows.shape[1:]
     n = 2 * half[1]
     hops = max(sizes) - 1
     groups = sizes[0] * sizes[1]
+    ch = p_t.shape[1]
+    ce = p_t.shape[0] // ch
+    mine = n // groups
+    k = a_msg.shape[0] * a_msg.shape[1] // SUBLANES
     return pl.pallas_call(
         functools.partial(exchange_kernel, scale),
-        out_shape=(jax.ShapeDtypeStruct((heads, n, n), jnp.float32), jax.ShapeDtypeStruct(a_msg.shape, jnp.bfloat16)),
-        in_specs=[pl.BlockSpec(memory_space=pl.ANY), pl.BlockSpec(memory_space=pltpu.VMEM)],
-        out_specs=(pl.BlockSpec(memory_space=pltpu.VMEM), pl.BlockSpec(memory_space=pltpu.VMEM)),
-        scratch_shapes=[pltpu.VMEM((2,) + tuple(sizes) + half, jnp.bfloat16), pltpu.VMEM((half[1] // LANES, n // groups * heads, LANES), jnp.float32),
+        out_shape=(jax.ShapeDtypeStruct((heads, n, n), jnp.float32), jax.ShapeDtypeStruct((mine * ce, ch * k), jnp.bfloat16)),
+        in_specs=[pl.BlockSpec(memory_space=pl.ANY), pl.BlockSpec(memory_space=pltpu.VMEM), pl.BlockSpec(memory_space=pltpu.VMEM)],
+        out_specs=(pl.BlockSpec(memory_space=pltpu.VMEM), pl.BlockSpec(memory_space=pl.ANY)),
+        scratch_shapes=[pltpu.VMEM(a_msg.shape, jnp.bfloat16), pltpu.VMEM((2,) + tuple(sizes) + half, jnp.bfloat16), pltpu.VMEM((half[1] // LANES, n // groups * heads, LANES), jnp.float32),
+                        pltpu.VMEM((mine // 2, ch, 2 * k), jnp.bfloat16), pltpu.VMEM((k * SUBLANES, LANES), jnp.float32), pltpu.VMEM((k // LANES, mine * ch, LANES), jnp.float32),
+                        pltpu.VMEM((2, 2 * ce, ch * k), jnp.bfloat16), pltpu.SemaphoreType.DMA((2,)),
                         pltpu.SemaphoreType.DMA((2,)), pltpu.SemaphoreType.DMA((8, hops)), pltpu.SemaphoreType.DMA((8, hops)),
                         pltpu.SemaphoreType.DMA((groups - 1,)), pltpu.SemaphoreType.DMA((groups - 1,))],
         compiler_params=pltpu.CompilerParams(collective_id=0, has_side_effects=True, vmem_limit_bytes=VMEM_LIMIT),
         cost_estimate=pl.CostEstimate(flops=10_000_000_000, bytes_accessed=10_000_000, transcendentals=0),
         name="exchange",
-    )(rows, a_msg)
+    )(rows, a_msg, p_t)
 
 
 def solution(mesh):
@@ -314,21 +357,21 @@
         bias_rows = bias_rows.reshape(rows_dev, heads, 2, n // 2).transpose(2, 0, 1, 3).reshape(2, rows_dev * heads, n // 2)
         sizes = tuple(fine.shape[ax] for ax in ALL_AXES)
         near, rest_scale = split_scale(cm // heads)
-        pair_bias, a_recv = exchange(bias_rows, a_msg, sizes, heads, 1.0 / rest_scale)
+        p_t = proj_out.reshape(ch, ch, ce).transpose(1, 2, 0).reshape(ch * ce, ch)
+        pair_bias, u = exchange(bias_rows, a_msg, p_t, sizes, heads, 1.0 / rest_scale)
 
         attend = functools.partial(attention, msa, msa_mask, pair_bias, row_gain, row_shift, query_w, key_w, value_w, gate_w, gate_bias, attn_out_w, attn_out_b)
-        early = seqs // 2
+        early = seqs * 7 // 16
         msa_new = attend(0, early)
-        a_recv, msa_new = lax.optimization_barrier((a_recv, msa_new))
-
-        p_t = proj_out.reshape(ch, ch, ce).transpose(1, 2, 0).reshape(ch * ce, ch)
+
         first = lax.axis_index(GROUP_AXES) * rows
         order = lax.broadcasted_iota(jnp.int32, (rows // 2, n), 0)
         cols = lax.broadcasted_iota(jnp.int32, (rows // 2, n), 1)
+        picks = [(cols == first + (order // 2) * 4 + half * 2 + order % 2).astype(jnp.bfloat16) for half in range(2)]
+        picks, msa_new = lax.optimization_barrier((picks, msa_new))
         totals = []
         for half in range(2):
-            mine = first + (order // 2) * 4 + half * 2 + order % 2
-            part = outer_product(a_recv, p_t, b_all, (cols == mine).astype(jnp.bfloat16), half)
+            part = outer_product(u, b_all, picks[half], half, ib=16)
             totals.append(lax.psum_scatter(part, SPLIT_AXES, scatter_dimension=0, tiled=True))
         msa_new, _ = lax.optimization_barrier((msa_new, part))
         msa_new = attend(early, seqs - early, msa_new)

time: 242 us -> 240 us (level)
  Pallas kernels: 211 us -> 197 us
  waiting for transfers between devices: 0.07 us -> 9.07 us
    pallas_call x2, Pallas kernels: 68.5 us -> 48.8 us  [outer_product(): pl.pallas_call(functools.partial(opm_kernel, db, ib), out_shape=jax.Shape...]
    reduce_scatter x2, waiting for transfers between devices: 0.02 us -> 9.02 us  [per_device(): lax.psum_scatter(part, SPLIT_AXES, scatter_dimension=0, tiled=True)]
    pallas_call x1, Pallas kernels: 49 us -> 55.6 us  [exchange(): pl.pallas_call(functools.partial(exchange_kernel, scale), out_shape=(jax....]
  transfers between devices with their start and end apart: 3 -> 3, of which waited for: 0 -> 1; matrix products, arithmetic and copies ran while one was open for 3% -> 3% of each run, Pallas kernels for 68% -> 68%
where the time goes in v4:
time: 240 us; the launch traced here: 237 us
  Pallas kernels  197 us (82%)
  local copies, waits for them, and re-layouts  13.9 us (6%)
  between operations  13.9 us (6%)
  waiting for transfers between devices  9.07 us (4%)
    pallas_call x2, Pallas kernels, attention(): pl.pallas_call(functools.partial(attn_kernel, first), out_shape=jax.Shape...  81.2 us
    pallas_call x1, Pallas kernels, exchange(): pl.pallas_call(functools.partial(exchange_kernel, scale), out_shape=(jax....  55.6 us
    pallas_call x2, Pallas kernels, outer_product(): pl.pallas_call(functools.partial(opm_kernel, db, ib), out_shape=jax.Shape...  48.8 us
    pallas_call x1, Pallas kernels, project_ab(): pl.pallas_call(ab_kernel, out_shape=(jax.ShapeDtypeStruct((16, s * SUBLAN...  11.9 us
    reduce_scatter x2, waiting for transfers between devices, per_device(): lax.psum_scatter(part, SPLIT_AXES, scatter_dimension=0, tiled=True)  9.02 us
    unnamed x24, local copies, waits for them, and re-layouts  6 us
  transfers between devices with their start and end apart: 3, of which 1 were waited for; matrix products, arithmetic and copies ran while one was open for 3% of the time, Pallas kernels for 68%

profile of v4, /device:TPU:1, one launch (start us, length us, event | category | flops | bytes accessed | tf_op | source)
XLA Modules:
  0.0 237.3 jit_solution(14388746062932952120)
XLA Ops:
  7.2 1.3 broadcast_in_dim.16.gain_ref
  8.6 1.2 broadcast_in_dim.34.shift_ref
  9.8 1.5 copy.31.pa_ref
  11.3 1.5 copy.32.pb_ref
  12.8 11.9 %project_ab.1 = (bf16[16,128,128]{2,1,0:T(8,128)(2,1)}, bf16[33,16,512]{2,1,0:T(8,128)(2,1)}) custom-call(bf16[16,512,256]{2,1,0:T(8,128)(2,1)} %msa_ref.5, s32[16,512]{1,0:T(8,128)} %mask_ref.5, bf16[1,256]{1,0:T(2,128)(2,1)} %broadcast_in_dim.16.gain_ref, bf16[1,256]{1,0:T(2,128)(2,1)} %broadcast_in_dim.34.shift_ref, bf16[256,32]{1,0:T(8,128)(2,1)} %copy.31.pa_ref, ...), custom_call_target="tpu_custom_call" | custom-call | flops 300000000 | bytes 6000000 | tf_op jit(solution)/shard_map/project_ab/pallas_call | solution.py:122
  24.7 0.3 reduce_sum.18
  25.1 0.6 multiply_reduce_fusion
  25.8 0.7 convolution_convert_fusion
  26.5 0.6 copy.40
  27.1 1.4 copy.34
  28.5 0.5 broadcast_in_dim.37.gain_ref
  29.0 0.5 broadcast_in_dim.38.shift_ref
  29.6 0.6 broadcast_in_dim.39.gb_ref
  30.2 0.6 broadcast_in_dim.40.bo_ref
  30.8 0.7 fusion.8
  31.5 55.6 %exchange.1 = (f32[8,512,512]{2,1,0:T(8,128)}, bf16[4096,8192]{1,0:T(8,128)(2,1)}) custom-call(bf16[2,32,256]{2,1,0:T(8,128)(2,1)} %bitcast.33, bf16[16,128,128]{2,1,0:T(8,128)(2,1)} %get-tuple-element.14.a_ref, bf16[4096,32]{1,0:T(8,128)(2,1)} %bitcast.29), custom_call_target="tpu_custom_call" | custom-call | flops 10000000000 | bytes 10000000 | tf_op jit(solution)/shard_map/exchange/pallas_call | solution.py:320
  87.1 36.1 %row_attention.2.rest_0_ = bf16[16,512,256]{2,1,0:T(8,128)(2,1)} custom-call(bf16[16,512,256]{2,1,0:T(8,128)(2,1)} %msa_ref.5, s32[16,512]{1,0:T(8,128)} %mask_ref.5, f32[8,512,512]{2,1,0:T(8,128)} %get-tuple-element.15.bias_ref, bf16[1,256]{1,0:T(2,128)(2,1)} %broadcast_in_dim.37.gain_ref, bf16[1,256]{1,0:T(2,128)(2,1)} %broadcast_in_dim.38.shift_ref, ...), custom_call_target="tpu_custom_call" | custom-call | flops 10499999744 | bytes 20000000 | tf_op jit(solution)/shard_map/row_attention/pallas_call | solution.py:66
  123.2 24.4 %outer_product.3 = f32[16,136,512]{2,1,0:T(8,128)} custom-call(bf16[4096,8192]{1,0:T(8,128)(2,1)} %get-tuple-element.17.u_ref, bf16[16,33,16,512]{3,2,1,0:T(8,128)(2,1)} %bitcast.25, bf16[16,33,16,512]{3,2,1,0:T(8,128)(2,1)} %bitcast.26, bf16[16,512]{1,0:T(8,128)(2,1)} %get-tuple-element.21.sel_ref), custom_call_target="tpu_custom_call" | custom-call | flops 17179869184 | bytes 50000000 | tf_op jit(solution)/shard_map/outer_product/pallas_call | solution.py:163
  147.8 24.4 %outer_product.2 = f32[16,136,512]{2,1,0:T(8,128)} custom-call(bf16[4096,8192]{1,0:T(8,128)(2,1)} %get-tuple-element.17.u_ref, bf16[16,33,16,512]{3,2,1,0:T(8,128)(2,1)} %bitcast.27, bf16[16,33,16,512]{3,2,1,0:T(8,128)(2,1)} %bitcast.28, bf16[16,512]{1,0:T(8,128)(2,1)} %get-tuple-element.19.sel_ref), custom_call_target="tpu_custom_call" | custom-call | flops 17179869184 | bytes 50000000 | tf_op jit(solution)/shard_map/outer_product/pallas_call | solution.py:163
  172.9 45.1 %row_attention.3 = bf16[16,512,256]{2,1,0:T(8,128)(2,1)} custom-call(bf16[16,512,256]{2,1,0:T(8,128)(2,1)} %msa_ref.5, s32[16,512]{1,0:T(8,128)} %mask_ref.5, f32[8,512,512]{2,1,0:T(8,128)} %get-tuple-element.15.bias_ref, bf16[1,256]{1,0:T(2,128)(2,1)} %broadcast_in_dim.37.gain_ref, ...), custom_call_target="tpu_custom_call", output_to_operand_aliasing={{}: (12, {})} | custom-call | flops 13500000256 | bytes 20000000 | tf_op jit(solution)/shard_map/row_attention/pallas_call | solution.py:66
  218.0 1.1 constant_dynamic-update-slice_fusion.1
  219.1 9.0 %reduce-scatter.5.cloned.1.call-done = f32[2,136,512]{2,1,0:T(8,128)} async-done(((f32[16,136,512]{2,1,0:T(8,128)}), f32[2,136,512]{2,1,0:T(8,128)}) %reduce-scatter.5.cloned.1.call-update) | async-done | bytes 557072 | tf_op jit(solution)/shard_map/reduce_scatter | solution.py:375
  228.1 1.1 constant_dynamic-update-slice_fusion
  229.4 1.3 copy.36
  (37 shorter events, 1.3 us)
Async XLA Ops:
  7.2 18.6 %copy-start = (bf16[128,8]{0,1:T(8,128)(2,1)S(1)}, bf16[128,8]{0,1:T(8,128)(2,1)}, u32[]{:S(2)}) copy-start(bf16[128,8]{0,1:T(8,128)(2,1)} %param.36) | copy-start | bytes 6148
  7.2 17.5 %copy-start.1 = (f32[4,512,128]{2,1,0:T(8,128)S(1)}, f32[4,512,128]{2,1,0:T(8,128)}, u32[]{:S(2)}) copy-start(f32[4,512,128]{2,1,0:T(8,128)} %param.24) | copy-start | bytes 3145732
  7.2 17.5 %copy-start.3 = (bf16[128]{0:T(256)(128)(2,1)S(1)}, bf16[128]{0:T(256)(128)(2,1)}, u32[]{:S(2)}) copy-start(bf16[128]{0:T(256)(128)(2,1)} %param.35) | copy-start | bytes 772
  7.2 116.0 %all-gather.3.cloned.1.call-start = ((), (), s32[]{:S(2)}) async-start(), calls=%async_computation.4 | async-start | bytes 9191424 | tf_op jit(solution)/shard_map/all_gather | solution.py:349
  9.8 17.3 %copy-start.2 = (bf16[1024,128]{1,0:T(8,128)(2,1)S(1)}, bf16[1024,128]{1,0:T(8,128)(2,1)}, u32[]{:S(2)}) copy-start(bf16[1024,128]{1,0:T(8,128)(2,1)} %param.31) | copy-start | bytes 786436
  12.7 15.8 %copy-start.4 = (bf16[256]{0:T(256)(128)(2,1)S(1)}, bf16[256]{0:T(256)(128)(2,1)}, u32[]{:S(2)}) copy-start(bf16[256]{0:T(256)(128)(2,1)} %param.33) | copy-start | bytes 1540
  12.7 16.3 %copy-start.5 = (bf16[256]{0:T(256)(128)(2,1)S(1)}, bf16[256]{0:T(256)(128)(2,1)}, u32[]{:S(2)}) copy-start(bf16[256]{0:T(256)(128)(2,1)} %param.34) | copy-start | bytes 1540
  12.7 16.8 %copy-start.6 = (bf16[256]{0:T(256)(128)(2,1)S(1)}, bf16[256]{0:T(256)(128)(2,1)}, u32[]{:S(2)}) copy-start(bf16[256]{0:T(256)(128)(2,1)} %param.41) | copy-start | bytes 1540
  12.8 17.4 %copy-start.7 = (bf16[256]{0:T(256)(128)(2,1)S(1)}, bf16[256]{0:T(256)(128)(2,1)}, u32[]{:S(2)}) copy-start(bf16[256]{0:T(256)(128)(2,1)} %param.43) | copy-start | bytes 1540
  24.6 193.4 %reduce-scatter.3.cloned.1.call-start = ((), (), s32[]{:S(2)}) async-start(), calls=%async_computation.2 | async-start | bytes 5013504 | tf_op jit(solution)/shard_map/reduce_scatter | solution.py:375
  147.6 80.5 %reduce-scatter.5.cloned.1.call-start = ((), (), s32[]{:S(2)}) async-start(), calls=%async_computation.3 | async-start | bytes 5013504 | tf_op jit(solution)/shard_map/reduce_scatter | solution.py:375
  172.2 0.7 copy-start.8
Sparse Core Ops, SparseCore 0:
  24.8 83.7 all-gather.2
  147.7 40.4 reduce-scatter.2
  190.6 37.4 reduce-scatter.4

commit v5 on v4

--- a/solution.py
+++ b/solution.py
@@ -29,11 +29,11 @@
     mu = jnp.mean(x, axis=-1, keepdims=True)
     xc = x - mu
     var = jnp.mean(xc * xc, axis=-1, keepdims=True)
-    r = (xc * lax.rsqrt(var + LN_EPS) * gain_ref[...].astype(jnp.float32) + shift_ref[...].astype(jnp.float32)).astype(jnp.bfloat16)
+    r = (xc * lax.rsqrt(var + LN_EPS) * gain_ref[...].astype(jnp.float32).reshape(1, cm) + shift_ref[...].astype(jnp.float32).reshape(1, cm)).astype(jnp.bfloat16)
     q_scr[...] = jnp.dot(r, qw_ref[...], preferred_element_type=jnp.float32).astype(jnp.bfloat16) * jnp.bfloat16(near)
     k_scr[...] = jnp.dot(r, kw_ref[...], preferred_element_type=jnp.float32).astype(jnp.bfloat16)
     v = jnp.dot(r, vw_ref[...], preferred_element_type=jnp.float32).astype(jnp.bfloat16)
-    g_scr[...] = jax.nn.sigmoid(jnp.dot(r, gw_ref[...], preferred_element_type=jnp.float32) + gb_ref[...].astype(jnp.float32)).astype(jnp.bfloat16)
+    g_scr[...] = jax.nn.sigmoid(jnp.dot(r, gw_ref[...], preferred_element_type=jnp.float32) + gb_ref[...].astype(jnp.float32).reshape(1, cm)).astype(jnp.bfloat16)
     lane_head = lax.broadcasted_iota(jnp.int32, (1, cm), 1) // hd
     for h in range(heads):
         vb_scr[h * n:(h + 1) * n, :] = v * (lane_head == h).astype(jnp.bfloat16)
@@ -49,7 +49,7 @@
         w_scr[:, h * n:(h + 1) * n] = (e * (1.0 / l)).astype(jnp.bfloat16)
     o = jnp.dot(w_scr[...], vb_scr[...], preferred_element_type=jnp.float32)
     o = (o * g_scr[...].astype(jnp.float32)).astype(jnp.bfloat16)
-    u = jnp.dot(o, wo_ref[...], preferred_element_type=jnp.float32) + bo_ref[...].astype(jnp.float32)
+    u = jnp.dot(o, wo_ref[...], preferred_element_type=jnp.float32) + bo_ref[...].astype(jnp.float32).reshape(1, cm)
     out_ref[0] = (msa_ref[0].astype(jnp.float32) + u).astype(jnp.bfloat16)
 
 
@@ -68,7 +68,7 @@
         out_shape=jax.ShapeDtypeStruct((s, n, cm), jnp.bfloat16),
         grid=(count,),
         in_specs=[pl.BlockSpec((1, n, cm), lambda i: (i + first, 0, 0)), const((s, n)),
-                  const((heads, n, n)), const((1, cm)), const((1, cm)), const((cm, cm)), const((cm, cm)), const((cm, cm)), const((cm, cm)), const((1, cm)), const((cm, cm)), const((1, cm))]
+                  const((heads, n, n)), const((cm,)), const((cm,)), const((cm, cm)), const((cm, cm)), const((cm, cm)), const((cm, cm)), const((cm,)), const((cm, cm)), const((cm,))]
                  + [pl.BlockSpec(memory_space=pl.ANY)] * len(extra),
         out_specs=pl.BlockSpec((1, n, cm), lambda i: (i + first, 0, 0)),
         scratch_shapes=[pltpu.VMEM((n, cm), jnp.bfloat16)] * 4 + [pltpu.VMEM((n, heads * n), jnp.bfloat16), pltpu.VMEM((heads * n, cm), jnp.bfloat16)],
@@ -76,7 +76,7 @@
         compiler_params=pltpu.CompilerParams(vmem_limit_bytes=VMEM_LIMIT, dimension_semantics=("arbitrary",)),
         cost_estimate=pl.CostEstimate(flops=count * 1_500_000_000, bytes_accessed=20_000_000, transcendentals=count * 2_000_000),
         name="row_attention",
-    )(msa, mask, bias, gain[None], shift[None], qw, kw, vw, gw, gb[None], wo, bo[None], *extra)
+    )(msa, mask, bias, gain, shift, qw, kw, vw, gw, gb, wo, bo, *extra)
 
 
 def ab_kernel(msa_ref, mask_ref, gain_ref, shift_ref, pa_ref, ba_ref, pb_ref, bb_ref, a_ref, b_ref, scr_a, scr_b):
@@ -86,11 +86,11 @@
     subs = a_ref.shape[0] // quads
     width = LANES // subs
     lane = lax.broadcasted_iota(jnp.int32, (SUBLANES, LANES), 1) // width
-    w = jnp.concatenate([pa_ref[...], pb_ref[...]], axis=1).astype(jnp.float32).T.astype(jnp.bfloat16)
-    bias = jnp.concatenate([ba_ref[...], bb_ref[...]], axis=1).astype(jnp.float32)
+    w = jnp.concatenate([pa_ref[...], pb_ref[...]], axis=0)
+    bias = jnp.concatenate([ba_ref[...].astype(jnp.float32).reshape(1, ch), bb_ref[...].astype(jnp.float32).reshape(1, ch)], axis=1)
     bias = jnp.broadcast_to(bias, (SUBLANES, 2 * ch)).T[:, 0:1]
-    gain = gain_ref[...].astype(jnp.float32)
-    shift = shift_ref[...].astype(jnp.float32)
+    gain = gain_ref[...].astype(jnp.float32).reshape(1, cm)
+    shift = shift_ref[...].astype(jnp.float32).reshape(1, cm)
 
     def one(s, carry):
         x = msa_ref[s].astype(jnp.float32)
@@ -110,7 +110,7 @@
                         out = jnp.where(lane == c4, pltpu.roll(tiles[c4], ((c4 - yy) * width) % LANES, 1), out)
                 scr_a[zz * subs + yy, pl.ds(pl.multiple_of(s * SUBLANES, SUBLANES), SUBLANES), :] = out
         return carry
-    lax.fori_loop(0, seqs, one, 0)
+    lax.fori_loop(0, seqs, one, 0, unroll=2)
     a_ref[...] = scr_a[...].astype(jnp.bfloat16)
     b_ref[0:ch] = scr_b[...].astype(jnp.bfloat16)
     b_ref[ch] = mask_ref[...].astype(jnp.float32).astype(jnp.bfloat16)
@@ -126,7 +126,7 @@
         compiler_params=pltpu.CompilerParams(vmem_limit_bytes=VMEM_LIMIT),
         cost_estimate=pl.CostEstimate(flops=300_000_000, bytes_accessed=6_000_000, transcendentals=8192),
         name="project_ab",
-    )(msa, mask, gain[None], shift[None], proj_a, bias_a[None], proj_b, bias_b[None])
+    )(msa, mask, gain, shift, proj_a.T, bias_a, proj_b.T, bias_b)
 
 
 def opm_kernel(db, ib, u_ref, b_ref, m_ref, sel_ref, out_ref):
@@ -245,10 +245,7 @@
             copy.start()
         return copies
 
-    for copy in own:
-        copy.wait()
     orders = (('x', 'y', 'z'), ('z', 'x', 'y'))
-    flying = [spread(part, orders[part][0], (), part) for part in range(2)]
     here = me['z'] * size['y'] + me['y']
     sends = []
     for j, (dz, dy) in enumerate(plane):
@@ -259,6 +256,9 @@
     for copy in sends:
         copy.start()
     ar_ref[here] = a_ref[here]
+    for copy in own:
+        copy.wait()
+    flying = [spread(part, orders[part][0], (), part) for part in range(2)]
 
     def advance(phase):
         for part in range(2):
@@ -278,9 +278,9 @@
             return carry
         lax.fori_loop(lo, hi, body, 0)
 
-    advance(1)
     for copy in sends:
         copy.wait()
+    advance(1)
     turn_a(ar_ref, at_ref, af, at2)
     run(0, pairs // 4)
     advance(2)
@@ -361,7 +361,7 @@
         pair_bias, u = exchange(bias_rows, a_msg, p_t, sizes, heads, 1.0 / rest_scale)
 
         attend = functools.partial(attention, msa, msa_mask, pair_bias, row_gain, row_shift, query_w, key_w, value_w, gate_w, gate_bias, attn_out_w, attn_out_b)
-        early = seqs * 7 // 16
+        early = seqs // 4
         msa_new = attend(0, early)
 
         first = lax.axis_index(GROUP_AXES) * rows

time: 240 us -> 219 us (0.912)
  local copies, waits for them, and re-layouts: 13.9 us -> 6.16 us
  Pallas kernels: 197 us -> 191 us
  waiting for transfers between devices: 9.07 us -> 4.47 us
    reduce_scatter x2, waiting for transfers between devices: 9.02 us -> 0.02 us  [per_device(): lax.psum_scatter(part, SPLIT_AXES, scatter_dimension=0, tiled=True)]
    broadcast_in_dim x6 -> x0, local copies, waits for them, and re-layouts: 4.8 us -> none  [the longest x1 1.32 us: project_ab(): gain[None]]
    all_gather x1, waiting for transfers between devices: 0.01 us -> 4.4 us  [per_device(): b_all = lax.all_gather(b_loc, GROUP_AXES, axis=0, tiled=False)]
    pallas_call x1, Pallas kernels: 55.6 us -> 51.4 us  [exchange(): pl.pallas_call(functools.partial(exchange_kernel, scale), out_shape=(jax....]
    unnamed x24 -> x14, local copies, waits for them, and re-layouts: 6 us -> 3.05 us
  transfers between devices with their start and end apart: 3 -> 3, of which waited for: 1 -> 1; matrix products, arithmetic and copies ran while one was open for 3% -> 3% of each run, Pallas kernels for 68% -> 72%
where the time goes in v5:
time: 219 us
  Pallas kernels  191 us (87%)
  between operations  13.9 us (6%)
  local copies, waits for them, and re-layouts  6.16 us (3%)
  waiting for transfers between devices  4.47 us (2%)
    pallas_call x2, Pallas kernels, attention(): pl.pallas_call(functools.partial(attn_kernel, first), out_shape=jax.Shape...  81.5 us
    pallas_call x1, Pallas kernels, exchange(): pl.pallas_call(functools.partial(exchange_kernel, scale), out_shape=(jax....  51.4 us
    pallas_call x2, Pallas kernels, outer_product(): pl.pallas_call(functools.partial(opm_kernel, db, ib), out_shape=jax.Shape...  48.7 us
    pallas_call x1, Pallas kernels, project_ab(): pl.pallas_call(ab_kernel, out_shape=(jax.ShapeDtypeStruct((16, s * SUBLAN...  9.48 us
    all_gather x1, waiting for transfers between devices, per_device(): b_all = lax.all_gather(b_loc, GROUP_AXES, axis=0, tiled=False)  4.4 us
  transfers between devices with their start and end apart: 3, of which 1 were waited for; matrix products, arithmetic and copies ran while one was open for 3% of the time, Pallas kernels for 72%

profile of v5, /device:TPU:1, one launch (start us, length us, event | category | flops | bytes accessed | tf_op | source)
XLA Modules:
  0.0 218.6 jit_solution(15814663563986758927)
XLA Ops:
  7.2 0.0 all-gather.3.cloned.1.call-start
  7.3 9.5 %project_ab.1 = (bf16[16,128,128]{2,1,0:T(8,128)(2,1)}, bf16[33,16,512]{2,1,0:T(8,128)(2,1)}) custom-call(bf16[16,512,256]{2,1,0:T(8,128)(2,1)} %msa_ref.5, s32[16,512]{1,0:T(8,128)} %mask_ref.5, bf16[256]{0:T(256)(128)(2,1)} %gain_ref.3, bf16[256]{0:T(256)(128)(2,1)} %shift_ref.3, bf16[32,256]{1,0:T(8,128)(2,1)} %bitcast.34, bf16[32]{0:T(256)(128)(2,1)} %ba_ref.1, ...), custom_call_target="tpu_custom_call" | custom-call | flops 300000000 | bytes 6000000 | tf_op jit(solution)/shard_map/project_ab/pallas_call | solution.py:122
  16.7 0.0 all-gather.3.cloned.1.call-update
  16.8 0.0 reduce-scatter.3.cloned.1.call-start
  16.8 0.3 reduce_sum.18
  17.2 0.6 multiply_reduce_fusion
  17.9 0.7 convolution_convert_fusion
  18.6 0.6 copy.36
  19.2 1.4 copy.30
  20.6 0.7 fusion.8
  21.4 51.4 %exchange.1 = (f32[8,512,512]{2,1,0:T(8,128)}, bf16[4096,8192]{1,0:T(8,128)(2,1)}) custom-call(bf16[2,32,256]{2,1,0:T(8,128)(2,1)} %bitcast.33, bf16[16,128,128]{2,1,0:T(8,128)(2,1)} %get-tuple-element.14.a_ref, bf16[4096,32]{1,0:T(8,128)(2,1)} %bitcast.29), custom_call_target="tpu_custom_call" | custom-call | flops 10000000000 | bytes 10000000 | tf_op jit(solution)/shard_map/exchange/pallas_call | solution.py:320
  72.8 22.5 %row_attention.2.rest_0_ = bf16[16,512,256]{2,1,0:T(8,128)(2,1)} custom-call(bf16[16,512,256]{2,1,0:T(8,128)(2,1)} %msa_ref.5, s32[16,512]{1,0:T(8,128)} %mask_ref.5, f32[8,512,512]{2,1,0:T(8,128)} %get-tuple-element.15.bias_ref, bf16[256]{0:T(256)(128)(2,1)} %gain_ref.5, bf16[256]{0:T(256)(128)(2,1)} %shift_ref.5, bf16[256,256]{1,0:T(8,128)(2,1)} %qw_ref.3, ...), custom_call_target="tpu_custom_call" | custom-call | flops 6000000000 | bytes 20000000 | tf_op jit(solution)/shard_map/row_attention/pallas_call | solution.py:66
  95.3 4.4 %all-gather.3.cloned.1.call-done = bf16[528,16,512]{2,1,0:T(8,128)(2,1)} async-done(((bf16[33,16,512]{2,1,0:T(8,128)(2,1)}), bf16[528,16,512]{2,1,0:T(8,128)(2,1)}) %all-gather.3.cloned.1.call-update) | async-done | bytes 8650768 | tf_op jit(solution)/shard_map/all_gather | solution.py:349
  99.7 24.4 %outer_product.3 = f32[16,136,512]{2,1,0:T(8,128)} custom-call(bf16[4096,8192]{1,0:T(8,128)(2,1)} %get-tuple-element.17.u_ref, bf16[16,33,16,512]{3,2,1,0:T(8,128)(2,1)} %bitcast.25, bf16[16,33,16,512]{3,2,1,0:T(8,128)(2,1)} %bitcast.26, bf16[16,512]{1,0:T(8,128)(2,1)} %get-tuple-element.21.sel_ref), custom_call_target="tpu_custom_call" | custom-call | flops 17179869184 | bytes 50000000 | tf_op jit(solution)/shard_map/outer_product/pallas_call | solution.py:163
  124.1 0.2 reduce-scatter.5.cloned.1.call-start
  124.3 24.4 %outer_product.2 = f32[16,136,512]{2,1,0:T(8,128)} custom-call(bf16[4096,8192]{1,0:T(8,128)(2,1)} %get-tuple-element.17.u_ref, bf16[16,33,16,512]{3,2,1,0:T(8,128)(2,1)} %bitcast.27, bf16[16,33,16,512]{3,2,1,0:T(8,128)(2,1)} %bitcast.28, bf16[16,512]{1,0:T(8,128)(2,1)} %get-tuple-element.19.sel_ref), custom_call_target="tpu_custom_call" | custom-call | flops 17179869184 | bytes 50000000 | tf_op jit(solution)/shard_map/outer_product/pallas_call | solution.py:163
  148.7 0.3 copy.31
  149.1 0.3 copy-done.4
  149.3 58.9 %row_attention.3 = bf16[16,512,256]{2,1,0:T(8,128)(2,1)} custom-call(bf16[16,512,256]{2,1,0:T(8,128)(2,1)} %msa_ref.5, s32[16,512]{1,0:T(8,128)} %mask_ref.5, f32[8,512,512]{2,1,0:T(8,128)} %get-tuple-element.15.bias_ref, bf16[256]{0:T(256)(128)(2,1)} %gain_ref.5, bf16[256]{0:T(256)(128)(2,1)} %shift_ref.5, ...), custom_call_target="tpu_custom_call", output_to_operand_aliasing={{}: (12, {})} | custom-call | flops 17999998976 | bytes 20000000 | tf_op jit(solution)/shard_map/row_attention/pallas_call | solution.py:66
  208.3 1.1 constant_dynamic-update-slice_fusion.1
  209.4 0.0 reduce-scatter.5.cloned.1.call-done
  209.4 1.1 constant_dynamic-update-slice_fusion
  210.5 0.2 fusion.2
  210.7 1.3 copy.32
  (21 shorter events, 0.1 us)
Async XLA Ops:
  7.2 10.7 %copy-start = (bf16[128,8]{0,1:T(8,128)(2,1)S(1)}, bf16[128,8]{0,1:T(8,128)(2,1)}, u32[]{:S(2)}) copy-start(bf16[128,8]{0,1:T(8,128)(2,1)} %param.36) | copy-start | bytes 6148
  7.2 9.7 %copy-start.1 = (f32[4,512,128]{2,1,0:T(8,128)S(1)}, f32[4,512,128]{2,1,0:T(8,128)}, u32[]{:S(2)}) copy-start(f32[4,512,128]{2,1,0:T(8,128)} %param.24) | copy-start | bytes 3145732
  7.2 9.6 %copy-start.3 = (bf16[128]{0:T(256)(128)(2,1)S(1)}, bf16[128]{0:T(256)(128)(2,1)}, u32[]{:S(2)}) copy-start(bf16[128]{0:T(256)(128)(2,1)} %param.35) | copy-start | bytes 772
  7.2 12.0 %copy-start.2 = (bf16[1024,128]{1,0:T(8,128)(2,1)S(1)}, bf16[1024,128]{1,0:T(8,128)(2,1)}, u32[]{:S(2)}) copy-start(bf16[1024,128]{1,0:T(8,128)(2,1)} %param.31) | copy-start | bytes 786436
  7.2 92.5 %all-gather.3.cloned.1.call-start = ((), (), s32[]{:S(2)}) async-start(), calls=%async_computation.4 | async-start | bytes 9191424 | tf_op jit(solution)/shard_map/all_gather | solution.py:349
  16.8 191.5 %reduce-scatter.3.cloned.1.call-start = ((), (), s32[]{:S(2)}) async-start(), calls=%async_computation.2 | async-start | bytes 5013504 | tf_op jit(solution)/shard_map/reduce_scatter | solution.py:375
  124.1 85.3 %reduce-scatter.5.cloned.1.call-start = ((), (), s32[]{:S(2)}) async-start(), calls=%async_computation.3 | async-start | bytes 5013504 | tf_op jit(solution)/shard_map/reduce_scatter | solution.py:375
  148.7 0.7 copy-start.4
Sparse Core Ops, SparseCore 0:
  16.9 82.7 all-gather.2
  124.2 35.7 reduce-scatter.2
  162.4 37.4 reduce-scatter.4

commit v6 on v5

--- a/solution.py
+++ b/solution.py
@@ -19,36 +19,28 @@
 SPLIT_AXES = ('x', 'c')
 
 
-def attn_kernel(first, msa_ref, mask_ref, bias_ref, gain_ref, shift_ref, qw_ref, kw_ref, vw_ref, gw_ref, gb_ref, wo_ref, bo_ref, *rest):
-    out_ref, q_scr, k_scr, v_scr, g_scr, w_scr, vb_scr = rest[-7:]
+def attn_kernel(first, msa_ref, qkvg_ref, mask_ref, bias_ref, wo_ref, bo_ref, *rest):
+    out_ref, w_scr, vb_scr = rest[-3:]
     n, cm = msa_ref.shape[1:]
     heads = bias_ref.shape[0]
     hd = cm // heads
-    near, rest_scale = split_scale(hd)
-    x = msa_ref[0].astype(jnp.float32)
-    mu = jnp.mean(x, axis=-1, keepdims=True)
-    xc = x - mu
-    var = jnp.mean(xc * xc, axis=-1, keepdims=True)
-    r = (xc * lax.rsqrt(var + LN_EPS) * gain_ref[...].astype(jnp.float32).reshape(1, cm) + shift_ref[...].astype(jnp.float32).reshape(1, cm)).astype(jnp.bfloat16)
-    q_scr[...] = jnp.dot(r, qw_ref[...], preferred_element_type=jnp.float32).astype(jnp.bfloat16) * jnp.bfloat16(near)
-    k_scr[...] = jnp.dot(r, kw_ref[...], preferred_element_type=jnp.float32).astype(jnp.bfloat16)
-    v = jnp.dot(r, vw_ref[...], preferred_element_type=jnp.float32).astype(jnp.bfloat16)
-    g_scr[...] = jax.nn.sigmoid(jnp.dot(r, gw_ref[...], preferred_element_type=jnp.float32) + gb_ref[...].astype(jnp.float32).reshape(1, cm)).astype(jnp.bfloat16)
+    rest_scale = split_scale(hd)[1]
     lane_head = lax.broadcasted_iota(jnp.int32, (1, cm), 1) // hd
+    v = qkvg_ref[0, 2]
     for h in range(heads):
         vb_scr[h * n:(h + 1) * n, :] = v * (lane_head == h).astype(jnp.bfloat16)
     keep = mask_ref[pl.ds(pl.program_id(0) + first, 1), :] > 0
-    q = q_scr[...]
+    q = qkvg_ref[0, 0]
     for h in range(heads):
         qh = q * (lane_head == h).astype(jnp.bfloat16)
-        s = lax.dot_general(qh, k_scr[...], (((1,), (1,)), ((), ())), preferred_element_type=jnp.float32)
+        s = lax.dot_general(qh, qkvg_ref[0, 1], (((1,), (1,)), ((), ())), preferred_element_type=jnp.float32)
         s = jnp.where(keep, s + bias_ref[h], MASK_FILL / rest_scale)
         m = jnp.max(s, axis=-1, keepdims=True)
         e = jnp.exp2((s - m) * (rest_scale * LOG2E))
         l = jnp.sum(e, axis=-1, keepdims=True)
         w_scr[:, h * n:(h + 1) * n] = (e * (1.0 / l)).astype(jnp.bfloat16)
     o = jnp.dot(w_scr[...], vb_scr[...], preferred_element_type=jnp.float32)
-    o = (o * g_scr[...].astype(jnp.float32)).astype(jnp.bfloat16)
+    o = (o * qkvg_ref[0, 3].astype(jnp.float32)).astype(jnp.bfloat16)
     u = jnp.dot(o, wo_ref[...], preferred_element_type=jnp.float32) + bo_ref[...].astype(jnp.float32).reshape(1, cm)
     out_ref[0] = (msa_ref[0].astype(jnp.float32) + u).astype(jnp.bfloat16)
 
@@ -58,7 +50,7 @@
     return near, hd ** -0.5 / near
 
 
-def attention(msa, mask, bias, gain, shift, qw, kw, vw, gw, gb, wo, bo, first, count, before=None):
+def attention(msa, qkvg, mask, bias, wo, bo, first, count, before=None):
     s, n, cm = msa.shape
     heads = bias.shape[0]
     const = lambda shape: pl.BlockSpec(shape, lambda i: (0,) * len(shape), pipeline_mode=pl.Buffered(1))
@@ -67,16 +59,16 @@
         functools.partial(attn_kernel, first),
         out_shape=jax.ShapeDtypeStruct((s, n, cm), jnp.bfloat16),
         grid=(count,),
-        in_specs=[pl.BlockSpec((1, n, cm), lambda i: (i + first, 0, 0)), const((s, n)),
-                  const((heads, n, n)), const((cm,)), const((cm,)), const((cm, cm)), const((cm, cm)), const((cm, cm)), const((cm, cm)), const((cm,)), const((cm, cm)), const((cm,))]
+        in_specs=[pl.BlockSpec((1, n, cm), lambda i: (i + first, 0, 0)), pl.BlockSpec((1, 4, n, cm), lambda i: (i + first, 0, 0, 0)), const((s, n)),
+                  const((heads, n, n)), const((cm, cm)), const((cm,))]
                  + [pl.BlockSpec(memory_space=pl.ANY)] * len(extra),
         out_specs=pl.BlockSpec((1, n, cm), lambda i: (i + first, 0, 0)),
-        scratch_shapes=[pltpu.VMEM((n, cm), jnp.bfloat16)] * 4 + [pltpu.VMEM((n, heads * n), jnp.bfloat16), pltpu.VMEM((heads * n, cm), jnp.bfloat16)],
-        input_output_aliases={12: 0} if extra else {},
+        scratch_shapes=[pltpu.VMEM((n, heads * n), jnp.bfloat16), pltpu.VMEM((heads * n, cm), jnp.bfloat16)],
+        input_output_aliases={6: 0} if extra else {},
         compiler_params=pltpu.CompilerParams(vmem_limit_bytes=VMEM_LIMIT, dimension_semantics=("arbitrary",)),
         cost_estimate=pl.CostEstimate(flops=count * 1_500_000_000, bytes_accessed=20_000_000, transcendentals=count * 2_000_000),
         name="row_attention",
-    )(msa, mask, bias, gain, shift, qw, kw, vw, gw, gb, wo, bo, *extra)
+    )(msa, qkvg, mask, bias, wo, bo, *extra)
 
 
 def ab_kernel(msa_ref, mask_ref, gain_ref, shift_ref, pa_ref, ba_ref, pb_ref, bb_ref, a_ref, b_ref, scr_a, scr_b):
@@ -213,7 +205,33 @@
     copy.start()
 
 
-def exchange_kernel(scale, rows_ref, a_ref, pt_ref, out_ref, u_ref, ar_ref, bias_ref, tmp, at_ref, af, at2, slab, slab_sem, own_sem, send_sem, recv_sem, a_send, a_recv):
+def project_rows(lo, hi, near, msa_ref, gain_ref, shift_ref, weights, gb_ref, stage, sem, out_ref):
+    cm = msa_ref.shape[2]
+
+    def one(s, carry):
+        slot = lax.rem(s, 2)
+        copy = pltpu.make_async_copy(stage.at[slot], out_ref.at[s], sem.at[slot])
+
+        @pl.when(s >= 2)
+        def _():
+            copy.wait()
+        x = msa_ref[s].astype(jnp.float32)
+        mu = jnp.mean(x, axis=-1, keepdims=True)
+        xc = x - mu
+        var = jnp.mean(xc * xc, axis=-1, keepdims=True)
+        r = (xc * lax.rsqrt(var + LN_EPS) * gain_ref[...].astype(jnp.float32).reshape(1, cm) + shift_ref[...].astype(jnp.float32).reshape(1, cm)).astype(jnp.bfloat16)
+        for j, w_ref in enumerate(weights):
+            y = jnp.dot(r, w_ref[...], preferred_element_type=jnp.float32)
+            if j == 3:
+                y = jax.nn.sigmoid(y + gb_ref[...].astype(jnp.float32).reshape(1, cm))
+            y = y.astype(jnp.bfloat16)
+            stage[slot, j] = y * jnp.bfloat16(near) if j == 0 else y
+        copy.start()
+        return carry
+    lax.fori_loop(lo, hi, one, 0)
+
+
+def exchange_kernel(scale, near, rows_ref, a_ref, pt_ref, msa_ref, gain_ref, shift_ref, qw_ref, kw_ref, vw_ref, gw_ref, gb_ref, out_ref, u_ref, qkvg_ref, ar_ref, bias_ref, tmp, at_ref, af, at2, slab, slab_sem, stage, stage_sem, own_sem, send_sem, recv_sem, a_send, a_recv):
     mesh_id = pl.DeviceIdType.MESH
     me = {name: lax.axis_index(name) for name in ALL_AXES}
     size = {'z': bias_ref.shape[1], 'y': bias_ref.shape[2], 'x': bias_ref.shape[3], 'c': bias_ref.shape[4]}
@@ -278,9 +296,12 @@
             return carry
         lax.fori_loop(lo, hi, body, 0)
 
+    attn_half = msa_ref.shape[0] // 2
+    project_rows(0, attn_half, near, msa_ref, gain_ref, shift_ref, (qw_ref, kw_ref, vw_ref, gw_ref), gb_ref, stage, stage_sem, qkvg_ref)
+    advance(1)
+    project_rows(attn_half, 2 * attn_half, near, msa_ref, gain_ref, shift_ref, (qw_ref, kw_ref, vw_ref, gw_ref), gb_ref, stage, stage_sem, qkvg_ref)
     for copy in sends:
         copy.wait()
-    advance(1)
     turn_a(ar_ref, at_ref, af, at2)
     run(0, pairs // 4)
     advance(2)
@@ -305,32 +326,37 @@
             return carry
         lax.fori_loop(0, size['z'] * size['y'], place, 0)
     for s in range(2):
+        pltpu.make_async_copy(stage.at[s], qkvg_ref.at[s], stage_sem.at[s]).wait()
+    for s in range(2):
         pltpu.make_async_copy(slab.at[s], u_ref.at[pl.ds(0, 2 * ce), :], slab_sem.at[s]).wait()
 
 
-def exchange(rows, a_msg, p_t, sizes, heads, scale):
+def exchange(rows, a_msg, p_t, msa, params, sizes, heads, scale, near):
     half = rows.shape[1:]
     n = 2 * half[1]
     hops = max(sizes) - 1
     groups = sizes[0] * sizes[1]
+    seqs, _, cm = msa.shape
     ch = p_t.shape[1]
     ce = p_t.shape[0] // ch
     mine = n // groups
     k = a_msg.shape[0] * a_msg.shape[1] // SUBLANES
     return pl.pallas_call(
-        functools.partial(exchange_kernel, scale),
-        out_shape=(jax.ShapeDtypeStruct((heads, n, n), jnp.float32), jax.ShapeDtypeStruct((mine * ce, ch * k), jnp.bfloat16)),
-        in_specs=[pl.BlockSpec(memory_space=pl.ANY), pl.BlockSpec(memory_space=pltpu.VMEM), pl.BlockSpec(memory_space=pltpu.VMEM)],
-        out_specs=(pl.BlockSpec(memory_space=pltpu.VMEM), pl.BlockSpec(memory_space=pl.ANY)),
+        functools.partial(exchange_kernel, scale, near),
+        out_shape=(jax.ShapeDtypeStruct((heads, n, n), jnp.float32), jax.ShapeDtypeStruct((mine * ce, ch * k), jnp.bfloat16),
+                   jax.ShapeDtypeStruct((seqs, 4, n, cm), jnp.bfloat16)),
+        in_specs=[pl.BlockSpec(memory_space=pl.ANY)] + [pl.BlockSpec(memory_space=pltpu.VMEM)] * (3 + len(params)),
+        out_specs=(pl.BlockSpec(memory_space=pltpu.VMEM), pl.BlockSpec(memory_space=pl.ANY), pl.BlockSpec(memory_space=pl.ANY)),
         scratch_shapes=[pltpu.VMEM(a_msg.shape, jnp.bfloat16), pltpu.VMEM((2,) + tuple(sizes) + half, jnp.bfloat16), pltpu.VMEM((half[1] // LANES, n // groups * heads, LANES), jnp.float32),
                         pltpu.VMEM((mine // 2, ch, 2 * k), jnp.bfloat16), pltpu.VMEM((k * SUBLANES, LANES), jnp.float32), pltpu.VMEM((k // LANES, mine * ch, LANES), jnp.float32),
                         pltpu.VMEM((2, 2 * ce, ch * k), jnp.bfloat16), pltpu.SemaphoreType.DMA((2,)),
+                        pltpu.VMEM((2, 4, n, cm), jnp.bfloat16), pltpu.SemaphoreType.DMA((2,)),
                         pltpu.SemaphoreType.DMA((2,)), pltpu.SemaphoreType.DMA((8, hops)), pltpu.SemaphoreType.DMA((8, hops)),
                         pltpu.SemaphoreType.DMA((groups - 1,)), pltpu.SemaphoreType.DMA((groups - 1,))],
         compiler_params=pltpu.CompilerParams(collective_id=0, has_side_effects=True, vmem_limit_bytes=VMEM_LIMIT),
         cost_estimate=pl.CostEstimate(flops=10_000_000_000, bytes_accessed=10_000_000, transcendentals=0),
         name="exchange",
-    )(rows, a_msg, p_t)
+    )(rows, a_msg, p_t, msa, *params)
 
 
 def solution(mesh):
@@ -358,9 +384,9 @@
         sizes = tuple(fine.shape[ax] for ax in ALL_AXES)
         near, rest_scale = split_scale(cm // heads)
         p_t = proj_out.reshape(ch, ch, ce).transpose(1, 2, 0).reshape(ch * ce, ch)
-        pair_bias, u = exchange(bias_rows, a_msg, p_t, sizes, heads, 1.0 / rest_scale)
-
-        attend = functools.partial(attention, msa, msa_mask, pair_bias, row_gain, row_shift, query_w, key_w, value_w, gate_w, gate_bias, attn_out_w, attn_out_b)
+        pair_bias, u, qkvg = exchange(bias_rows, a_msg, p_t, msa, (row_gain, row_shift, query_w, key_w, value_w, gate_w, gate_bias), sizes, heads, 1.0 / rest_scale, near)
+
+        attend = functools.partial(attention, msa, qkvg, msa_mask, pair_bias, attn_out_w, attn_out_b)
         early = seqs // 4
         msa_new = attend(0, early)
 

time: 219 us -> 221 us (level); the launches traced: 219 us -> 218 us
  waiting for transfers between devices: 4.47 us -> 0.07 us
  Pallas kernels: 191 us -> 195 us
    pallas_call x1, Pallas kernels: 51.4 us -> 65.5 us  [exchange(): pl.pallas_call(functools.partial(exchange_kernel, scale, near), out_shape...]
    pallas_call x2, Pallas kernels: 81.5 us -> 71.5 us  [attention(): pl.pallas_call(functools.partial(attn_kernel, first), out_shape=jax.Shape...]
    all_gather x1, waiting for transfers between devices: 4.4 us -> 0.01 us  [per_device(): b_all = lax.all_gather(b_loc, GROUP_AXES, axis=0, tiled=False)]
  transfers between devices with their start and end apart: 3 -> 3, of which waited for: 1 -> 0; matrix products, arithmetic and copies ran while one was open for 3% -> 3% of each run, Pallas kernels for 72% -> 74%
where the time goes in v6:
time: 221 us; the launch traced here: 218 us
  Pallas kernels  195 us (88%)
  between operations  13.9 us (6%)
  local copies, waits for them, and re-layouts  6.16 us (3%)
    pallas_call x2, Pallas kernels, attention(): pl.pallas_call(functools.partial(attn_kernel, first), out_shape=jax.Shape...  71.5 us
    pallas_call x1, Pallas kernels, exchange(): pl.pallas_call(functools.partial(exchange_kernel, scale, near), out_shape...  65.5 us
    pallas_call x2, Pallas kernels, outer_product(): pl.pallas_call(functools.partial(opm_kernel, db, ib), out_shape=jax.Shape...  49 us
    pallas_call x1, Pallas kernels, project_ab(): pl.pallas_call(ab_kernel, out_shape=(jax.ShapeDtypeStruct((16, s * SUBLAN...  9.46 us
  transfers between devices with their start and end apart: 3, of which 0 were waited for; matrix products, arithmetic and copies ran while one was open for 3% of the time, Pallas kernels for 74%

profile of v6, /device:TPU:1, one launch (start us, length us, event | category | flops | bytes accessed | tf_op | source)
XLA Modules:
  0.0 218.3 jit_solution(8018475800367854754)
XLA Ops:
  7.2 0.0 all-gather.3.cloned.1.call-start
  7.3 9.5 %project_ab.1 = (bf16[16,128,128]{2,1,0:T(8,128)(2,1)}, bf16[33,16,512]{2,1,0:T(8,128)(2,1)}) custom-call(bf16[16,512,256]{2,1,0:T(8,128)(2,1)} %msa_ref.7, s32[16,512]{1,0:T(8,128)} %mask_ref.5, bf16[256]{0:T(256)(128)(2,1)} %gain_ref.2, bf16[256]{0:T(256)(128)(2,1)} %shift_ref.2, bf16[32,256]{1,0:T(8,128)(2,1)} %bitcast.34, bf16[32]{0:T(256)(128)(2,1)} %ba_ref.1, ...), custom_call_target="tpu_custom_call" | custom-call | flops 300000000 | bytes 6000000 | tf_op jit(solution)/shard_map/project_ab/pallas_call | solution.py:114
  16.7 0.0 all-gather.3.cloned.1.call-update
  16.7 0.0 reduce-scatter.3.cloned.1.call-start
  16.8 0.3 reduce_sum.18
  17.2 0.6 multiply_reduce_fusion
  17.9 0.7 convolution_convert_fusion
  18.6 0.6 copy.36
  19.2 1.4 copy.30
  20.6 0.7 fusion.8
  21.3 65.5 %exchange.1 = (f32[8,512,512]{2,1,0:T(8,128)}, bf16[4096,8192]{1,0:T(8,128)(2,1)}, bf16[16,4,512,256]{3,2,1,0:T(8,128)(2,1)}) custom-call(bf16[2,32,256]{2,1,0:T(8,128)(2,1)} %bitcast.33, bf16[16,128,128]{2,1,0:T(8,128)(2,1)} %get-tuple-element.15.a_ref, bf16[4096,32]{1,0:T(8,128)(2,1)} %bitcast.29, bf16[16,512,256]{2,1,0:T(8,128)(2,1)} %msa_ref.7, ...), custom_call_target="tpu_custom_call" | custom-call | flops 10000000000 | bytes 10000000 | tf_op jit(solution)/shard_map/exchange/pallas_call | solution.py:344
  86.8 20.1 %row_attention.2.rest_0_ = bf16[16,512,256]{2,1,0:T(8,128)(2,1)} custom-call(bf16[16,512,256]{2,1,0:T(8,128)(2,1)} %msa_ref.7, bf16[16,4,512,256]{3,2,1,0:T(8,128)(2,1)} %get-tuple-element.16.qkvg_ref, s32[16,512]{1,0:T(8,128)} %mask_ref.5, f32[8,512,512]{2,1,0:T(8,128)} %get-tuple-element.17.bias_ref, bf16[256,256]{1,0:T(8,128)(2,1)} %wo_ref.3, ...), custom_call_target="tpu_custom_call" | custom-call | flops 6000000000 | bytes 20000000 | tf_op jit(solution)/shard_map/row_attention/pallas_call | solution.py:58
  106.9 24.4 %outer_product.3 = f32[16,136,512]{2,1,0:T(8,128)} custom-call(bf16[4096,8192]{1,0:T(8,128)(2,1)} %get-tuple-element.19.u_ref, bf16[16,33,16,512]{3,2,1,0:T(8,128)(2,1)} %bitcast.25, bf16[16,33,16,512]{3,2,1,0:T(8,128)(2,1)} %bitcast.26, bf16[16,512]{1,0:T(8,128)(2,1)} %get-tuple-element.23.sel_ref), custom_call_target="tpu_custom_call" | custom-call | flops 17179869184 | bytes 50000000 | tf_op jit(solution)/shard_map/outer_product/pallas_call | solution.py:155
  131.3 0.0 reduce-scatter.3.cloned.1.call-update
  131.3 0.0 reduce-scatter.5.cloned.1.call-start
  131.4 24.6 %outer_product.2 = f32[16,136,512]{2,1,0:T(8,128)} custom-call(bf16[4096,8192]{1,0:T(8,128)(2,1)} %get-tuple-element.19.u_ref, bf16[16,33,16,512]{3,2,1,0:T(8,128)(2,1)} %bitcast.27, bf16[16,33,16,512]{3,2,1,0:T(8,128)(2,1)} %bitcast.28, bf16[16,512]{1,0:T(8,128)(2,1)} %get-tuple-element.21.sel_ref), custom_call_target="tpu_custom_call" | custom-call | flops 17179869184 | bytes 50000000 | tf_op jit(solution)/shard_map/outer_product/pallas_call | solution.py:155
  156.0 0.3 copy.31
  156.4 0.3 copy-done.4
  156.6 51.4 %row_attention.3 = bf16[16,512,256]{2,1,0:T(8,128)(2,1)} custom-call(bf16[16,512,256]{2,1,0:T(8,128)(2,1)} %msa_ref.7, bf16[16,4,512,256]{3,2,1,0:T(8,128)(2,1)} %get-tuple-element.16.qkvg_ref, s32[16,512]{1,0:T(8,128)} %mask_ref.5, f32[8,512,512]{2,1,0:T(8,128)} %get-tuple-element.17.bias_ref, ...), custom_call_target="tpu_custom_call", output_to_operand_aliasing={{}: (6, {})} | custom-call | flops 17999998976 | bytes 20000000 | tf_op jit(solution)/shard_map/row_attention/pallas_call | solution.py:58
  208.0 1.1 constant_dynamic-update-slice_fusion.1
  209.1 0.0 reduce-scatter.5.cloned.1.call-done
  209.1 1.1 constant_dynamic-update-slice_fusion
  210.3 0.2 fusion.2
  210.5 1.3 copy.32
  (21 shorter events, 0.1 us)
Async XLA Ops:
  7.2 10.7 %copy-start = (bf16[128,8]{0,1:T(8,128)(2,1)S(1)}, bf16[128,8]{0,1:T(8,128)(2,1)}, u32[]{:S(2)}) copy-start(bf16[128,8]{0,1:T(8,128)(2,1)} %param.36) | copy-start | bytes 6148
  7.2 9.6 %copy-start.1 = (f32[4,512,128]{2,1,0:T(8,128)S(1)}, f32[4,512,128]{2,1,0:T(8,128)}, u32[]{:S(2)}) copy-start(f32[4,512,128]{2,1,0:T(8,128)} %param.24) | copy-start | bytes 3145732
  7.2 9.6 %copy-start.3 = (bf16[128]{0:T(256)(128)(2,1)S(1)}, bf16[128]{0:T(256)(128)(2,1)}, u32[]{:S(2)}) copy-start(bf16[128]{0:T(256)(128)(2,1)} %param.35) | copy-start | bytes 772
  7.2 12.0 %copy-start.2 = (bf16[1024,128]{1,0:T(8,128)(2,1)S(1)}, bf16[1024,128]{1,0:T(8,128)(2,1)}, u32[]{:S(2)}) copy-start(bf16[1024,128]{1,0:T(8,128)(2,1)} %param.31) | copy-start | bytes 786436
  7.2 99.7 %all-gather.3.cloned.1.call-start = ((), (), s32[]{:S(2)}) async-start(), calls=%async_computation.4 | async-start | bytes 9191424 | tf_op jit(solution)/shard_map/all_gather | solution.py:375
  16.7 191.3 %reduce-scatter.3.cloned.1.call-start = ((), (), s32[]{:S(2)}) async-start(), calls=%async_computation.2 | async-start | bytes 5013504 | tf_op jit(solution)/shard_map/reduce_scatter | solution.py:401
  131.3 77.8 %reduce-scatter.5.cloned.1.call-start = ((), (), s32[]{:S(2)}) async-start(), calls=%async_computation.3 | async-start | bytes 5013504 | tf_op jit(solution)/shard_map/reduce_scatter | solution.py:401
  156.0 0.7 copy-start.4
Sparse Core Ops, SparseCore 0:
  16.9 85.0 all-gather.2
  131.4 37.6 reduce-scatter.2
  171.6 37.4 reduce-scatter.4

commit v7 on v5

--- a/solution.py
+++ b/solution.py
@@ -20,11 +20,17 @@
 
 
 def attn_kernel(first, msa_ref, mask_ref, bias_ref, gain_ref, shift_ref, qw_ref, kw_ref, vw_ref, gw_ref, gb_ref, wo_ref, bo_ref, *rest):
-    out_ref, q_scr, k_scr, v_scr, g_scr, w_scr, vb_scr = rest[-7:]
+    out_ref, q_scr, k_scr, v_scr, g_scr, w_scr, vb_scr, b_scr = rest[-8:]
     n, cm = msa_ref.shape[1:]
     heads = bias_ref.shape[0]
     hd = cm // heads
     near, rest_scale = split_scale(hd)
+
+    @pl.when(pl.program_id(0) == 0)
+    def _():
+        for h in range(heads):
+            b_scr[h] = bias_ref[h].astype(jnp.float32) * (1.0 / rest_scale)
+
     x = msa_ref[0].astype(jnp.float32)
     mu = jnp.mean(x, axis=-1, keepdims=True)
     xc = x - mu
@@ -42,7 +48,7 @@
     for h in range(heads):
         qh = q * (lane_head == h).astype(jnp.bfloat16)
         s = lax.dot_general(qh, k_scr[...], (((1,), (1,)), ((), ())), preferred_element_type=jnp.float32)
-        s = jnp.where(keep, s + bias_ref[h], MASK_FILL / rest_scale)
+        s = jnp.where(keep, s + b_scr[h], MASK_FILL / rest_scale)
         m = jnp.max(s, axis=-1, keepdims=True)
         e = jnp.exp2((s - m) * (rest_scale * LOG2E))
         l = jnp.sum(e, axis=-1, keepdims=True)
@@ -71,7 +77,7 @@
                   const((heads, n, n)), const((cm,)), const((cm,)), const((cm, cm)), const((cm, cm)), const((cm, cm)), const((cm, cm)), const((cm,)), const((cm, cm)), const((cm,))]
                  + [pl.BlockSpec(memory_space=pl.ANY)] * len(extra),
         out_specs=pl.BlockSpec((1, n, cm), lambda i: (i + first, 0, 0)),
-        scratch_shapes=[pltpu.VMEM((n, cm), jnp.bfloat16)] * 4 + [pltpu.VMEM((n, heads * n), jnp.bfloat16), pltpu.VMEM((heads * n, cm), jnp.bfloat16)],
+        scratch_shapes=[pltpu.VMEM((n, cm), jnp.bfloat16)] * 4 + [pltpu.VMEM((n, heads * n), jnp.bfloat16), pltpu.VMEM((heads * n, cm), jnp.bfloat16), pltpu.VMEM((heads, n, n), jnp.float32)],
         input_output_aliases={12: 0} if extra else {},
         compiler_params=pltpu.CompilerParams(vmem_limit_bytes=VMEM_LIMIT, dimension_semantics=("arbitrary",)),
         cost_estimate=pl.CostEstimate(flops=count * 1_500_000_000, bytes_accessed=20_000_000, transcendentals=count * 2_000_000),
@@ -213,7 +219,7 @@
     copy.start()
 
 
-def exchange_kernel(scale, rows_ref, a_ref, pt_ref, out_ref, u_ref, ar_ref, bias_ref, tmp, at_ref, af, at2, slab, slab_sem, own_sem, send_sem, recv_sem, a_send, a_recv):
+def exchange_kernel(rows_ref, a_ref, pt_ref, out_ref, u_ref, ar_ref, bias_ref, tmp, at_ref, af, at2, slab, slab_sem, own_sem, send_sem, recv_sem, a_send, a_recv):
     mesh_id = pl.DeviceIdType.MESH
     me = {name: lax.axis_index(name) for name in ALL_AXES}
     size = {'z': bias_ref.shape[1], 'y': bias_ref.shape[2], 'x': bias_ref.shape[3], 'c': bias_ref.shape[4]}
@@ -296,19 +302,19 @@
             copy.wait()
 
         def place(t, carry):
-            x = bias_ref[part, t // size['y'], lax.rem(t, size['y'])].reshape(per, wide).astype(jnp.float32) * scale
+            x = bias_ref[part, t // size['y'], lax.rem(t, size['y'])].reshape(per, wide).astype(jnp.float32)
             for kk in range(wide // LANES):
                 tmp[kk] = x[:, kk * LANES:(kk + 1) * LANES]
             for kk in range(wide // LANES):
                 for h in range(heads):
-                    out_ref[h, pl.ds(pl.multiple_of(t * block, block), block), part * wide + kk * LANES:part * wide + (kk + 1) * LANES] = tmp[kk, pl.ds(h, block, stride=heads), :]
+                    out_ref[h, pl.ds(pl.multiple_of(t * block, block), block), part * wide + kk * LANES:part * wide + (kk + 1) * LANES] = tmp[kk, pl.ds(h, block, stride=heads), :].astype(jnp.bfloat16)
             return carry
         lax.fori_loop(0, size['z'] * size['y'], place, 0)
     for s in range(2):
         pltpu.make_async_copy(slab.at[s], u_ref.at[pl.ds(0, 2 * ce), :], slab_sem.at[s]).wait()
 
 
-def exchange(rows, a_msg, p_t, sizes, heads, scale):
+def exchange(rows, a_msg, p_t, sizes, heads):
     half = rows.shape[1:]
     n = 2 * half[1]
     hops = max(sizes) - 1
@@ -318,8 +324,8 @@
     mine = n // groups
     k = a_msg.shape[0] * a_msg.shape[1] // SUBLANES
     return pl.pallas_call(
-        functools.partial(exchange_kernel, scale),
-        out_shape=(jax.ShapeDtypeStruct((heads, n, n), jnp.float32), jax.ShapeDtypeStruct((mine * ce, ch * k), jnp.bfloat16)),
+        exchange_kernel,
+        out_shape=(jax.ShapeDtypeStruct((heads, n, n), jnp.bfloat16), jax.ShapeDtypeStruct((mine * ce, ch * k), jnp.bfloat16)),
         in_specs=[pl.BlockSpec(memory_space=pl.ANY), pl.BlockSpec(memory_space=pltpu.VMEM), pl.BlockSpec(memory_space=pltpu.VMEM)],
         out_specs=(pl.BlockSpec(memory_space=pltpu.VMEM), pl.BlockSpec(memory_space=pl.ANY)),
         scratch_shapes=[pltpu.VMEM(a_msg.shape, jnp.bfloat16), pltpu.VMEM((2,) + tuple(sizes) + half, jnp.bfloat16), pltpu.VMEM((half[1] // LANES, n // groups * heads, LANES), jnp.float32),
@@ -333,6 +339,25 @@
     )(rows, a_msg, p_t)
 
 
+def pair_kernel(low_ref, high_ref, pair_ref, bias_ref, out_ref):
+    rows, n, ce = pair_ref.shape
+    bias = jnp.broadcast_to(bias_ref[...].astype(jnp.float32).reshape(1, ce), (SUBLANES, ce)).T[:, 0:1]
+    for r in range(rows):
+        t_ref = low_ref if r < rows // 2 else high_ref
+        t = t_ref[r % (rows // 2)]
+        val = (t[0:ce] + bias) / (COUNT_EPS + t[ce:ce + 1])
+        out_ref[r] = pair_ref[r] + val.T
+
+
+def finish_pair(low, high, pair_act, bias_out):
+    return pl.pallas_call(
+        pair_kernel,
+        out_shape=jax.ShapeDtypeStruct(pair_act.shape, jnp.float32),
+        cost_estimate=pl.CostEstimate(flops=2_000_000, bytes_accessed=4_000_000, transcendentals=0),
+        name="finish_pair",
+    )(low, high, pair_act, bias_out)
+
+
 def solution(mesh):
     devices = mesh.devices
     fine = Mesh(devices.reshape(devices.shape[0], 4, 4, 4, 2), ('data', 'z', 'y', 'x', 'c'))
@@ -356,9 +381,8 @@
         heads = bias_rows.shape[1]
         bias_rows = bias_rows.reshape(rows_dev, heads, 2, n // 2).transpose(2, 0, 1, 3).reshape(2, rows_dev * heads, n // 2)
         sizes = tuple(fine.shape[ax] for ax in ALL_AXES)
-        near, rest_scale = split_scale(cm // heads)
         p_t = proj_out.reshape(ch, ch, ce).transpose(1, 2, 0).reshape(ch * ce, ch)
-        pair_bias, u = exchange(bias_rows, a_msg, p_t, sizes, heads, 1.0 / rest_scale)
+        pair_bias, u = exchange(bias_rows, a_msg, p_t, sizes, heads)
 
         attend = functools.partial(attention, msa, msa_mask, pair_bias, row_gain, row_shift, query_w, key_w, value_w, gate_w, gate_bias, attn_out_w, attn_out_b)
         early = seqs // 4
@@ -375,10 +399,7 @@
             totals.append(lax.psum_scatter(part, SPLIT_AXES, scatter_dimension=0, tiled=True))
         msa_new, _ = lax.optimization_barrier((msa_new, part))
         msa_new = attend(early, seqs - early, msa_new)
-        total = jnp.concatenate(totals, axis=0)
-        outer_sum = total[:, :ce].transpose(0, 2, 1)
-        counts = total[:, ce]
-        pair_new = pair_act + (outer_sum + bias_out.astype(jnp.float32)) / (COUNT_EPS + counts)[:, :, None]
+        pair_new = finish_pair(totals[0], totals[1], pair_act, bias_out)
         return msa_new, pair_new
 
     in_specs = (seq_spec, seq_spec, seq_spec) + (P(),) * 19

time: 219 us -> 217 us (level)
  local copies, waits for them, and re-layouts: 6.16 us -> 2.06 us
    unnamed x14 -> x8, local copies, waits for them, and re-layouts: 3.05 us -> 0.02 us
    pallas_call x1 -> x2, Pallas kernels: 51.4 us -> 53 us  [the longest x1 50 us: exchange(): pl.pallas_call(exchange_kernel, out_shape=(jax.ShapeDtypeStruct((heads, n...]
  transfers between devices with their start and end apart: 3 -> 3, of which waited for: 1 -> 1; matrix products, arithmetic and copies ran while one was open for 3% -> 2% of each run, Pallas kernels for 72% -> 72%
where the time goes in v7:
time: 217 us; the launch traced here: 216 us
  Pallas kernels  192 us (88%)
  between operations  13.9 us (6%)
  waiting for transfers between devices  5.93 us (3%)
    pallas_call x2, Pallas kernels, attention(): pl.pallas_call(functools.partial(attn_kernel, first), out_shape=jax.Shape...  80.5 us
    pallas_call x1, Pallas kernels, exchange(): pl.pallas_call(exchange_kernel, out_shape=(jax.ShapeDtypeStruct((heads, n...  50 us
    pallas_call x2, Pallas kernels, outer_product(): pl.pallas_call(functools.partial(opm_kernel, db, ib), out_shape=jax.Shape...  49 us
    pallas_call x1, Pallas kernels, project_ab(): pl.pallas_call(ab_kernel, out_shape=(jax.ShapeDtypeStruct((16, s * SUBLAN...  9.51 us
    all_gather x1, waiting for transfers between devices, per_device(): b_all = lax.all_gather(b_loc, GROUP_AXES, axis=0, tiled=False)  5.87 us
  transfers between devices with their start and end apart: 3, of which 1 were waited for; matrix products, arithmetic and copies ran while one was open for 2% of the time, Pallas kernels for 72%

profile of v7, /device:TPU:1, one launch (start us, length us, event | category | flops | bytes accessed | tf_op | source)
XLA Modules:
  0.0 216.5 jit_solution(1855669994111114649)
XLA Ops:
  7.2 0.0 copy-start
  7.2 0.0 copy-start.1
  7.2 0.0 copy-start.3
  7.2 0.0 all-gather.3.cloned.1.call-start
  7.3 9.5 %project_ab.1 = (bf16[16,128,128]{2,1,0:T(8,128)(2,1)}, bf16[33,16,512]{2,1,0:T(8,128)(2,1)}) custom-call(bf16[16,512,256]{2,1,0:T(8,128)(2,1)} %msa_ref.5, s32[16,512]{1,0:T(8,128)} %mask_ref.5, bf16[256]{0:T(256)(128)(2,1)} %gain_ref.3, bf16[256]{0:T(256)(128)(2,1)} %shift_ref.3, bf16[32,256]{1,0:T(8,128)(2,1)} %bitcast.26, bf16[32]{0:T(256)(128)(2,1)} %ba_ref.1, ...), custom_call_target="tpu_custom_call" | custom-call | flops 300000000 | bytes 6000000 | tf_op jit(solution)/shard_map/project_ab/pallas_call | solution.py:128
  16.8 0.0 all-gather.3.cloned.1.call-update
  16.8 0.0 reduce-scatter.3.cloned.1.call-start
  16.9 0.3 reduce_sum.18
  17.2 0.6 multiply_reduce_fusion
  17.9 0.7 convolution_convert_fusion
  18.6 0.6 copy.30
  19.3 1.4 copy.28
  20.7 0.7 fusion.5
  21.4 50.0 %exchange.1 = (bf16[8,512,512]{2,1,0:T(8,128)(2,1)}, bf16[4096,8192]{1,0:T(8,128)(2,1)}) custom-call(bf16[2,32,256]{2,1,0:T(8,128)(2,1)} %bitcast.25, bf16[16,128,128]{2,1,0:T(8,128)(2,1)} %get-tuple-element.14.a_ref, bf16[4096,32]{1,0:T(8,128)(2,1)} %bitcast.22), custom_call_target="tpu_custom_call" | custom-call | flops 10000000000 | bytes 10000000 | tf_op jit(solution)/shard_map/exchange/pallas_call | solution.py:326
  71.4 22.0 %row_attention.2.rest_0_ = bf16[16,512,256]{2,1,0:T(8,128)(2,1)} custom-call(bf16[16,512,256]{2,1,0:T(8,128)(2,1)} %msa_ref.5, s32[16,512]{1,0:T(8,128)} %mask_ref.5, bf16[8,512,512]{2,1,0:T(8,128)(2,1)} %get-tuple-element.15.bias_ref, bf16[256]{0:T(256)(128)(2,1)} %gain_ref.5, bf16[256]{0:T(256)(128)(2,1)} %shift_ref.5, bf16[256,256]{1,0:T(8,128)(2,1)} %qw_ref.3, ...), custom_call_target="tpu_custom_call" | custom-call | flops 6000000000 | bytes 20000000 | tf_op jit(solution)/shard_map/row_attention/pallas_call | solution.py:72
  93.4 5.9 %all-gather.3.cloned.1.call-done = bf16[528,16,512]{2,1,0:T(8,128)(2,1)} async-done(((bf16[33,16,512]{2,1,0:T(8,128)(2,1)}), bf16[528,16,512]{2,1,0:T(8,128)(2,1)}) %all-gather.3.cloned.1.call-update) | async-done | bytes 8650768 | tf_op jit(solution)/shard_map/all_gather | solution.py:374
  99.3 24.4 %outer_product.3 = f32[16,136,512]{2,1,0:T(8,128)} custom-call(bf16[4096,8192]{1,0:T(8,128)(2,1)} %get-tuple-element.17.u_ref, bf16[16,33,16,512]{3,2,1,0:T(8,128)(2,1)} %bitcast.18, bf16[16,33,16,512]{3,2,1,0:T(8,128)(2,1)} %bitcast.19, bf16[16,512]{1,0:T(8,128)(2,1)} %get-tuple-element.21.sel_ref), custom_call_target="tpu_custom_call" | custom-call | flops 17179869184 | bytes 50000000 | tf_op jit(solution)/shard_map/outer_product/pallas_call | solution.py:169
  123.7 0.0 reduce-scatter.3.cloned.1.call-update
  123.8 0.0 reduce-scatter.5.cloned.1.call-start
  123.8 24.6 %outer_product.2 = f32[16,136,512]{2,1,0:T(8,128)} custom-call(bf16[4096,8192]{1,0:T(8,128)(2,1)} %get-tuple-element.17.u_ref, bf16[16,33,16,512]{3,2,1,0:T(8,128)(2,1)} %bitcast.20, bf16[16,33,16,512]{3,2,1,0:T(8,128)(2,1)} %bitcast.21, bf16[16,512]{1,0:T(8,128)(2,1)} %get-tuple-element.19.sel_ref), custom_call_target="tpu_custom_call" | custom-call | flops 17179869184 | bytes 50000000 | tf_op jit(solution)/shard_map/outer_product/pallas_call | solution.py:169
  148.4 0.0 reduce-scatter.5.cloned.1.call-update
  148.4 58.5 %row_attention.3 = bf16[16,512,256]{2,1,0:T(8,128)(2,1)} custom-call(bf16[16,512,256]{2,1,0:T(8,128)(2,1)} %msa_ref.5, s32[16,512]{1,0:T(8,128)} %mask_ref.5, bf16[8,512,512]{2,1,0:T(8,128)(2,1)} %get-tuple-element.15.bias_ref, bf16[256]{0:T(256)(128)(2,1)} %gain_ref.5, bf16[256]{0:T(256)(128)(2,1)} %shift_ref.5, ...), custom_call_target="tpu_custom_call", output_to_operand_aliasing={{}: (12, {})} | custom-call | flops 17999998976 | bytes 20000000 | tf_op jit(solution)/shard_map/row_attention/pallas_call | solution.py:72
  206.9 0.0 reduce-scatter.5.cloned.1.call-done.high_ref
  206.9 3.0 %finish_pair.1 = f32[4,512,128]{2,1,0:T(8,128)} custom-call(f32[2,136,512]{2,1,0:T(8,128)} %reduce-scatter.3.cloned.1.call-done.low_ref, f32[2,136,512]{2,1,0:T(8,128)} %reduce-scatter.5.cloned.1.call-done.high_ref, f32[4,512,128]{2,1,0:T(8,128)} %pair_ref.1, bf16[128]{0:T(256)(128)(2,1)} %bias_ref.1), custom_call_target="tpu_custom_call" | custom-call | flops 2000000 | bytes 4000000 | tf_op jit(solution)/shard_map/finish_pair/pallas_call | solution.py:353
  (12 shorter events, 0.0 us)
Async XLA Ops:
  7.2 10.7 %copy-start = (bf16[128,8]{0,1:T(8,128)(2,1)S(1)}, bf16[128,8]{0,1:T(8,128)(2,1)}, u32[]{:S(2)}) copy-start(bf16[128,8]{0,1:T(8,128)(2,1)} %param.36) | copy-start | bytes 6148
  7.2 9.7 %copy-start.1 = (f32[4,512,128]{2,1,0:T(8,128)S(1)}, f32[4,512,128]{2,1,0:T(8,128)}, u32[]{:S(2)}) copy-start(f32[4,512,128]{2,1,0:T(8,128)} %pair_ref.1) | copy-start | bytes 3145732
  7.2 9.7 %copy-start.3 = (bf16[128]{0:T(256)(128)(2,1)S(1)}, bf16[128]{0:T(256)(128)(2,1)}, u32[]{:S(2)}) copy-start(bf16[128]{0:T(256)(128)(2,1)} %param.35) | copy-start | bytes 772
  7.2 12.1 %copy-start.2 = (bf16[1024,128]{1,0:T(8,128)(2,1)S(1)}, bf16[1024,128]{1,0:T(8,128)(2,1)}, u32[]{:S(2)}) copy-start(bf16[1024,128]{1,0:T(8,128)(2,1)} %param.31) | copy-start | bytes 786436
  7.2 92.1 %all-gather.3.cloned.1.call-start = ((), (), s32[]{:S(2)}) async-start(), calls=%async_computation.4 | async-start | bytes 9191424 | tf_op jit(solution)/shard_map/all_gather | solution.py:374
  16.8 190.1 %reduce-scatter.3.cloned.1.call-start = ((), (), s32[]{:S(2)}) async-start(), calls=%async_computation.2 | async-start | bytes 5013504 | tf_op jit(solution)/shard_map/reduce_scatter | solution.py:399
  123.8 83.2 %reduce-scatter.5.cloned.1.call-start = ((), (), s32[]{:S(2)}) async-start(), calls=%async_computation.3 | async-start | bytes 5013504 | tf_op jit(solution)/shard_map/reduce_scatter | solution.py:399
Sparse Core Ops, SparseCore 0:
  16.9 82.3 all-gather.2
  123.9 35.4 reduce-scatter.2
  161.8 37.4 reduce-scatter.4
